TPU v7x, 8 devices: a whole 2x2x1 slice. The times are simulated.
8 devices in a mesh: cp: 8 (over z, y, x, core).
Axes of the slice: x: 2, y: 2, z: 1, core: 2. Of those that a mesh axis runs over, the one named last changes fastest.
Arguments:
- query: bfloat16 [4, 2048, 12, 128], P(None, 'cp')
- key_in: bfloat16 [4, 2048, 12, 128], P(None, 'cp')
- value: bfloat16 [4, 2048, 12, 128], P(None, 'cp')
- bias_u: bfloat16 [12, 128], replicated
- bias_w: bfloat16 [12, 128], replicated
- rel_k: bfloat16 [2048, 12, 128], replicated
- d_out: bfloat16 [4, 2048, 12, 128], P(None, 'cp')
Outputs:
- output 1: bfloat16 [4, 2048, 12, 128], P(None, 'cp')
- output 2: bfloat16 [4, 2048, 12, 128], P(None, 'cp')
- output 3: bfloat16 [4, 2048, 12, 128], P(None, 'cp')
- output 4: bfloat16 [4, 2048, 12, 128], P(None, 'cp')
- output 5: float32 [12, 128], replicated
- output 6: float32 [12, 128], replicated
- output 7: float32 [2048, 12, 128], replicated
All inputs are finite; a program needn't handle non-finite values.
Results may differ from a plain program's by a relative error of at most 0.00869742.
Values are sent between devices in bfloat16 or wider.
A program may use at most 1 GiB of HBM per device.

v0:
```python
import jax
import jax.numpy as jnp
from jax import lax
from jax.sharding import PartitionSpec as P


def skew_rel(by_win, rows):
    lead_dims = by_win.shape[:-2]
    flattened = by_win.reshape(lead_dims + (2 * rows * rows,))
    flattened = flattened[..., rows - 1:rows - 1 + rows * (2 * rows - 1)]
    return flattened.reshape(lead_dims + (rows, 2 * rows - 1))[..., :rows]


def unskew_rel(d_rel, rows):
    lead_dims = d_rel.shape[:-2]
    pad_cfg = [(0, 0)] * len(lead_dims)
    widened = jnp.pad(d_rel, pad_cfg + [(0, 0), (0, rows - 1)])
    flattened = widened.reshape(lead_dims + (rows * (2 * rows - 1),))
    flattened = jnp.pad(flattened, pad_cfg + [(rows - 1, 1)])
    return flattened.reshape(lead_dims + (rows, 2 * rows))


def block_logits(q_u, q_w, key_blk, window, delta):
    rows = q_u.shape[1]
    inv_sqrt = q_u.shape[-1] ** -0.5
    content = jnp.einsum('bihd,bjhd->bhij', q_u, key_blk, preferred_element_type=jnp.float32)
    by_win = jnp.einsum('bihd,chd->bhic', q_w, window, preferred_element_type=jnp.float32)
    logits = (content + skew_rel(by_win, rows)) * inv_sqrt
    row_id = jnp.arange(rows)[:, None]
    col_id = jnp.arange(rows)[None, :]
    keep = (col_id <= row_id) | (delta > 0)
    return jnp.where(keep, logits, -jnp.inf)


def fwd_update(state, q_u, q_w, key_blk, val_blk, window, delta):
    row_max, row_sum, out_acc = state
    logits = block_logits(q_u, q_w, key_blk, window, delta)
    new_max = jnp.maximum(row_max, jnp.max(logits, axis=-1))
    rescale = jnp.exp(row_max - new_max)
    weights = jnp.exp(logits - new_max[..., None])
    row_sum = row_sum * rescale + jnp.sum(weights, axis=-1)
    out_acc = out_acc * jnp.swapaxes(rescale, 1, 2)[..., None] + jnp.einsum('bhij,bjhd->bihd', weights.astype(jnp.bfloat16), val_blk, preferred_element_type=jnp.float32)
    return new_max, row_sum, out_acc


def bwd_update(q_u, q_w, d_out, log_norm, row_dot, key_blk, val_blk, window, delta):
    rows = q_u.shape[1]
    inv_sqrt = q_u.shape[-1] ** -0.5
    logits = block_logits(q_u, q_w, key_blk, window, delta)
    weights = jnp.exp(logits - log_norm[..., None])
    weights_b = weights.astype(jnp.bfloat16)
    dv_new = jnp.einsum('bhij,bihd->bjhd', weights_b, d_out, preferred_element_type=jnp.float32)
    d_weights = jnp.einsum('bihd,bjhd->bhij', d_out, val_blk, preferred_element_type=jnp.float32)
    d_logit = (weights * (d_weights - row_dot[..., None]) * inv_sqrt).astype(jnp.bfloat16)
    dk_new = jnp.einsum('bhij,bihd->bjhd', d_logit, q_u, preferred_element_type=jnp.float32)
    dqc_new = jnp.einsum('bhij,bjhd->bihd', d_logit, key_blk, preferred_element_type=jnp.float32)
    d_wide = unskew_rel(d_logit, rows)
    dqr_new = jnp.einsum('bhic,chd->bihd', d_wide, window, preferred_element_type=jnp.float32)
    d_win = jnp.einsum('bhic,bihd->chd', d_wide, q_w, preferred_element_type=jnp.float32)
    return dk_new, dv_new, dqc_new, dqr_new, d_win


def solution(mesh):
    n_dev = mesh.shape['cp']
    shift_pairs = [(sender, (sender + 1) % n_dev) for sender in range(n_dev)]
    seq_spec = P(None, 'cp', None, None)

    def local(query, key_in, value, bias_u, bias_w, rel_k, d_out):
        n_batch, rows, n_heads, head_dim = query.shape
        my_idx = lax.axis_index('cp')
        q_u = (query.astype(jnp.float32) + bias_u.astype(jnp.float32)).astype(jnp.bfloat16)
        q_w = (query.astype(jnp.float32) + bias_w.astype(jnp.float32)).astype(jnp.bfloat16)
        rk_rev = jnp.concatenate([jnp.flip(rel_k, axis=0), jnp.zeros((rows, n_heads, head_dim), jnp.bfloat16)], axis=0)

        def window_at(delta):
            return lax.dynamic_slice_in_dim(rk_rev, (n_dev - 1 - delta) * rows, 2 * rows, 0)

        def fwd_visit(step, key_blk, val_blk, state):
            src_blk = (my_idx - step) % n_dev
            delta = my_idx - src_blk
            return lax.cond(src_blk <= my_idx,
                            lambda prev_state: fwd_update(prev_state, q_u, q_w, key_blk, val_blk, window_at(delta), delta),
                            lambda prev_state: prev_state, state)

        stat_shape = (n_batch, n_heads, rows)
        start_state = (jnp.full(stat_shape, -jnp.inf, jnp.float32), jnp.zeros(stat_shape, jnp.float32), jnp.zeros(query.shape, jnp.float32))
        first_state = fwd_visit(0, key_in, value, start_state)

        def fwd_body(step, carry):
            key_blk, val_blk, state = carry
            key_blk = lax.ppermute(key_blk, 'cp', shift_pairs)
            val_blk = lax.ppermute(val_blk, 'cp', shift_pairs)
            return key_blk, val_blk, fwd_visit(step, key_blk, val_blk, state)

        row_max, row_sum, out_acc = lax.fori_loop(1, n_dev, fwd_body, (key_in, value, first_state))[2]
        out_f32 = out_acc / jnp.swapaxes(row_sum, 1, 2)[..., None]
        log_norm = row_max + jnp.log(row_sum)
        row_dot = jnp.swapaxes(jnp.sum(d_out.astype(jnp.float32) * out_f32, axis=-1), 1, 2)

        def bwd_visit(step, grads):
            key_blk, val_blk, dk_blk, dv_blk, dq_cont, dq_rel, drk_rev = grads
            src_blk = (my_idx - step) % n_dev
            delta = my_idx - src_blk

            def visit(prev):
                dk_prev, dv_prev, dqc_prev, dqr_prev, drk_prev = prev
                dk_new, dv_new, dqc_new, dqr_new, d_win = bwd_update(q_u, q_w, d_out, log_norm, row_dot, key_blk, val_blk, window_at(delta), delta)
                start = (n_dev - 1 - delta) * rows
                win_old = lax.dynamic_slice_in_dim(drk_prev, start, 2 * rows, 0)
                drk_prev = lax.dynamic_update_slice_in_dim(drk_prev, win_old + d_win, start, 0)
                return (dk_prev + dk_new, dv_prev + dv_new, dqc_prev + dqc_new, dqr_prev + dqr_new, drk_prev)

            updated = lax.cond(src_blk <= my_idx, visit, lambda prev: prev, (dk_blk, dv_blk, dq_cont, dq_rel, drk_rev))
            return (key_blk, val_blk) + updated

        zeros_blk = jnp.zeros(query.shape, jnp.float32)
        grads = bwd_visit(0, (key_in, value, zeros_blk, zeros_blk, zeros_blk, zeros_blk, jnp.zeros(rk_rev.shape, jnp.float32)))

        def bwd_body(step, grads):
            moved = tuple(lax.ppermute(travel, 'cp', shift_pairs) for travel in grads[:4])
            return bwd_visit(step, moved + grads[4:])

        grads = lax.fori_loop(1, n_dev, bwd_body, grads)
        dk_home = lax.ppermute(grads[2], 'cp', shift_pairs)
        dv_home = lax.ppermute(grads[3], 'cp', shift_pairs)
        dq_cont, dq_rel, drk_rev = grads[4:]
        d_query = (dq_cont + dq_rel).astype(jnp.bfloat16)
        d_bias_u = lax.psum(jnp.sum(dq_cont, axis=(0, 1)), 'cp')
        d_bias_w = lax.psum(jnp.sum(dq_rel, axis=(0, 1)), 'cp')
        d_rel_k = lax.psum(jnp.flip(drk_rev[:rel_k.shape[0]], axis=0), 'cp')
        return (out_f32.astype(jnp.bfloat16), d_query, dk_home.astype(jnp.bfloat16), dv_home.astype(jnp.bfloat16), d_bias_u, d_bias_w, d_rel_k)

    return jax.shard_map(local, mesh=mesh,
                         in_specs=(seq_spec, seq_spec, seq_spec, P(), P(), P(), seq_spec),
                         out_specs=(seq_spec, seq_spec, seq_spec, seq_spec, P(), P(), P()),
                         check_vma=False)
```

profile of v0, /device:TPU:0, one launch (start us, length us, event | category | flops | bytes accessed | tf_op | source)
XLA Modules:
  0.0 5977.9 jit_solution(13155695783571569256)
XLA Ops:
  11.8 89.9 %rev.8 = bf16[2048,12,128]{2,0,1:T(8,128)(2,1)} reverse(bf16[2048,12,128]{2,0,1:T(8,128)(2,1)} %param.24), dimensions={0} | reverse | bytes 12582912 | tf_op jit(solution)/shard_map/jit(_flip)/rev | solution.py:73
  118.3 177.6 %conditional.4 = (f32[4,12,256]{2,1,0:T(8,128)}, f32[4,12,256]{2,1,0:T(8,128)S(1)}, f32[4,256,12,128]{3,1,2,0:T(8,128)}) conditional(s32[]{:T(128)} %convert_element_type.79, () %tuple.82, (s32[]{:T(128)}, bf16[4,256,12,128]{3,1,0,2:T(8,128)(2,1)}, bf16[4,256,12,128]{3,1,2,0:T(8,128)(2,1)S(1)}, bf16[2304,12,128]{2,0,1:T(8,128)(2,1)}, ...), branch_computations={%region_0.1_spmd, %region_1.4_spmd} | conditional | flops 3248107520 | bytes 373145760 | solution.py:81
  118.3 15.3 convolution_bitcast_fusion
  133.6 25.0 copy.33
  158.6 25.5 reshape.49
  184.1 25.4 slice.28
  209.5 30.0 reshape.50
  239.5 10.8 slice.29
  250.3 12.6 copy.80
  295.9 1526.8 %while.50 = (s32[]{:T(128)}, bf16[4,256,12,128]{3,1,2,0:T(8,128)(2,1)}, bf16[4,256,12,128]{3,1,2,0:T(8,128)(2,1)}, f32[4,12,256]{2,1,0:T(8,128)}, f32[4,12,256]{...) while((s32[]{:T(128)}, ...), condition=%wide.region_9.10_spmd, body=%wide.region_4.9_spmd.sunk | while | flops 3249704960 | bytes 392364544 | solution.py:95
  299.4 35.2 collective-permute-done
  334.7 33.7 collective-permute-done.1
  376.2 164.3 %collective-permute-start = (bf16[4,256,12,128]{3,1,2,0:T(8,128)(2,1)}, bf16[4,256,12,128]{3,1,2,0:T(8,128)(2,1)}, u32[]{:S(2)}, u32[]{:S(2)}) collective-permute-start(bf16[4,256,12,128]{3,1,2,0:T(8,128)(2,1)} %get-tuple-element.1180), channel_id=1, source_target_pairs={{0,1},{1,2},{2,3},{3,4},{4,5},{5,6},{6,7},{7,0}} | collective-permute-start | bytes 9437192 | tf_op jit(solution)/shard_map/while/body/eval_jaxpr/ppermute | solution.py:91
  542.9 32.7 collective-permute-done
  575.7 33.7 collective-permute-done.1
  618.7 167.8 %collective-permute-start.1 = (bf16[4,256,12,128]{3,1,2,0:T(8,128)(2,1)}, bf16[4,256,12,128]{3,1,2,0:T(8,128)(2,1)}, u32[]{:S(2)}, u32[]{:S(2)}) collective-permute-start(bf16[4,256,12,128]{3,1,2,0:T(8,128)(2,1)} %get-tuple-element.1181), channel_id=1, source_target_pairs={{0,1},{1,2},{2,3},{3,4},{4,5},{5,6},{6,7},{7,0}} | collective-permute-start | bytes 9437192 | tf_op jit(solution)/shard_map/while/body/eval_jaxpr/ppermute | solution.py:92
  786.5 30.2 collective-permute-done
  816.7 33.7 collective-permute-done.1
  864.7 193.1 %collective-permute-done = bf16[4,256,12,128]{3,1,2,0:T(8,128)(2,1)} collective-permute-done((bf16[4,256,12,128]{3,1,2,0:T(8,128)(2,1)}, bf16[4,256,12,128]{3,1,2,0:T(8,128)(2,1)}, u32[]{:S(2)}, u32[]{:S(2)}) %collective-permute-start) | collective-permute-done | bytes 3145760 | tf_op jit(solution)/shard_map/while/body/eval_jaxpr/ppermute | solution.py:91
  1057.7 33.7 collective-permute-done.1
  1099.3 199.5 %collective-permute-done = bf16[4,256,12,128]{3,1,2,0:T(8,128)(2,1)} collective-permute-done((bf16[4,256,12,128]{3,1,2,0:T(8,128)(2,1)}, bf16[4,256,12,128]{3,1,2,0:T(8,128)(2,1)}, u32[]{:S(2)}, u32[]{:S(2)}) %collective-permute-start) | collective-permute-done | bytes 3145760 | tf_op jit(solution)/shard_map/while/body/eval_jaxpr/ppermute | solution.py:91
  1298.8 33.7 collective-permute-done.1
  1340.3 199.5 %collective-permute-done = bf16[4,256,12,128]{3,1,2,0:T(8,128)(2,1)} collective-permute-done((bf16[4,256,12,128]{3,1,2,0:T(8,128)(2,1)}, bf16[4,256,12,128]{3,1,2,0:T(8,128)(2,1)}, u32[]{:S(2)}, u32[]{:S(2)}) %collective-permute-start) | collective-permute-done | bytes 3145760 | tf_op jit(solution)/shard_map/while/body/eval_jaxpr/ppermute | solution.py:91
  1539.8 33.7 collective-permute-done.1
  1581.3 199.5 %collective-permute-done = bf16[4,256,12,128]{3,1,2,0:T(8,128)(2,1)} collective-permute-done((bf16[4,256,12,128]{3,1,2,0:T(8,128)(2,1)}, bf16[4,256,12,128]{3,1,2,0:T(8,128)(2,1)}, u32[]{:S(2)}, u32[]{:S(2)}) %collective-permute-start) | collective-permute-done | bytes 3145760 | tf_op jit(solution)/shard_map/while/body/eval_jaxpr/ppermute | solution.py:91
  1780.8 33.7 collective-permute-done.1
  1831.5 279.3 %conditional.5 = (f32[4,256,12,128]{3,1,2,0:T(8,128)}, f32[4,256,12,128]{3,1,2,0:T(8,128)}, f32[4,256,12,128]{3,1,2,0:T(8,128)}, f32[4,256,12,128]{1,3,0,2:T(8,128)}, f32[2304,12,128]{2,0,1:T(8,128)}) conditional(s32[]{:T(128)} %convert_element_type.79, () %tuple.85, (s32[]{:T(128)}, bf16[4,256,12,128]{3,1,0,2:T(8,128)(2,1)}, ...), branch_computations={%region_11.12_spmd, %region_12.13_spmd} | conditional | flops 8886812672 | bytes 577175872 | solution.py:113
  1831.5 14.3 convolution_bitcast_fusion.2
  1845.8 24.9 copy.40
  1870.7 25.5 reshape.53
  1896.1 25.4 slice.32
  1921.6 30.0 reshape.54
  1951.6 10.9 fusion.29
  1962.5 9.5 multiply_convert_fusion
  1986.4 22.0 reshape.55
  2008.5 11.7 pad.12
  2020.2 17.3 reshape.56
  2044.0 10.9 bitcast_dynamic-update-slice_fusion
  2054.8 12.0 convolution_bitcast_fusion.3
  2110.7 3270.2 %while.51 = (s32[]{:T(128)}, bf16[4,256,12,128]{3,1,2,0:T(8,128)(2,1)}, bf16[4,256,12,128]{3,1,2,0:T(8,128)(2,1)}, f32[4,256,12,128]{3,1,2,0:T(8,128)}, f32[4,25...) while((s32[]{:T(128)}, ...), condition=%wide.region_16.17_spmd, body=%wide.region_13.16_spmd.sunk | while | flops 8893890560 | bytes 685704064 | solution.py:123
  2110.9 334.2 %collective-permute-done.2 = bf16[4,256,12,128]{3,1,2,0:T(8,128)(2,1)} collective-permute-done((bf16[4,256,12,128]{3,1,2,0:T(8,128)(2,1)}, bf16[4,256,12,128]{3,1,2,0:T(8,128)(2,1)}, u32[]{:S(2)}, u32[]{:S(2)}) %collective-permute-start.2) | collective-permute-done | bytes 3145760 | tf_op jit(solution)/shard_map/while/body/eval_jaxpr/ppermute | solution.py:120
  2449.0 29.8 collective-permute-done.3
  2495.1 95.4 %collective-permute-start.2 = (bf16[4,256,12,128]{3,1,2,0:T(8,128)(2,1)}, bf16[4,256,12,128]{3,1,2,0:T(8,128)(2,1)}, u32[]{:S(2)}, u32[]{:S(2)}) collective-permute-start(bf16[4,256,12,128]{3,1,2,0:T(8,128)(2,1)} %get-tuple-element.1237), channel_id=1, source_target_pairs={{0,1},{1,2},{2,3},{3,4},{4,5},{5,6},{6,7},{7,0}} | collective-permute-start | bytes 9437192 | tf_op jit(solution)/shard_map/while/body/eval_jaxpr/ppermute | solution.py:120
  2593.9 332.2 %collective-permute-done.2 = bf16[4,256,12,128]{3,1,2,0:T(8,128)(2,1)} collective-permute-done((bf16[4,256,12,128]{3,1,2,0:T(8,128)(2,1)}, bf16[4,256,12,128]{3,1,2,0:T(8,128)(2,1)}, u32[]{:S(2)}, u32[]{:S(2)}) %collective-permute-start.2) | collective-permute-done | bytes 3145760 | tf_op jit(solution)/shard_map/while/body/eval_jaxpr/ppermute | solution.py:120
  2929.9 29.8 collective-permute-done.3
  2976.0 30.5 collective-permute-start.5
  3006.5 98.6 %collective-permute-start.2 = (bf16[4,256,12,128]{3,1,2,0:T(8,128)(2,1)}, bf16[4,256,12,128]{3,1,2,0:T(8,128)(2,1)}, u32[]{:S(2)}, u32[]{:S(2)}) collective-permute-start(bf16[4,256,12,128]{3,1,2,0:T(8,128)(2,1)} %get-tuple-element.1237), channel_id=1, source_target_pairs={{0,1},{1,2},{2,3},{3,4},{4,5},{5,6},{6,7},{7,0}} | collective-permute-start | bytes 9437192 | tf_op jit(solution)/shard_map/while/body/eval_jaxpr/ppermute | solution.py:120
  3108.6 298.4 %collective-permute-done.2 = bf16[4,256,12,128]{3,1,2,0:T(8,128)(2,1)} collective-permute-done((bf16[4,256,12,128]{3,1,2,0:T(8,128)(2,1)}, bf16[4,256,12,128]{3,1,2,0:T(8,128)(2,1)}, u32[]{:S(2)}, u32[]{:S(2)}) %collective-permute-start.2) | collective-permute-done | bytes 3145760 | tf_op jit(solution)/shard_map/while/body/eval_jaxpr/ppermute | solution.py:120
  3410.9 29.8 collective-permute-done.3
  3457.0 132.5 %collective-permute-start.2 = (bf16[4,256,12,128]{3,1,2,0:T(8,128)(2,1)}, bf16[4,256,12,128]{3,1,2,0:T(8,128)(2,1)}, u32[]{:S(2)}, u32[]{:S(2)}) collective-permute-start(bf16[4,256,12,128]{3,1,2,0:T(8,128)(2,1)} %get-tuple-element.1237), channel_id=1, source_target_pairs={{0,1},{1,2},{2,3},{3,4},{4,5},{5,6},{6,7},{7,0}} | collective-permute-start | bytes 9437192 | tf_op jit(solution)/shard_map/while/body/eval_jaxpr/ppermute | solution.py:120
  3592.9 295.1 %collective-permute-done.2 = bf16[4,256,12,128]{3,1,2,0:T(8,128)(2,1)} collective-permute-done((bf16[4,256,12,128]{3,1,2,0:T(8,128)(2,1)}, bf16[4,256,12,128]{3,1,2,0:T(8,128)(2,1)}, u32[]{:S(2)}, u32[]{:S(2)}) %collective-permute-start.2) | collective-permute-done | bytes 3145760 | tf_op jit(solution)/shard_map/while/body/eval_jaxpr/ppermute | solution.py:120
  3891.9 29.8 collective-permute-done.3
  3938.0 139.2 %collective-permute-start.3 = (bf16[4,256,12,128]{3,1,2,0:T(8,128)(2,1)}, bf16[4,256,12,128]{3,1,2,0:T(8,128)(2,1)}, u32[]{:S(2)}, u32[]{:S(2)}) collective-permute-start(bf16[4,256,12,128]{3,1,2,0:T(8,128)(2,1)} %get-tuple-element.1238), channel_id=1, source_target_pairs={{0,1},{1,2},{2,3},{3,4},{4,5},{5,6},{6,7},{7,0}} | collective-permute-start | bytes 9437192 | tf_op jit(solution)/shard_map/while/body/eval_jaxpr/ppermute | solution.py:120
  4077.2 291.7 %collective-permute-done.2 = bf16[4,256,12,128]{3,1,2,0:T(8,128)(2,1)} collective-permute-done((bf16[4,256,12,128]{3,1,2,0:T(8,128)(2,1)}, bf16[4,256,12,128]{3,1,2,0:T(8,128)(2,1)}, u32[]{:S(2)}, u32[]{:S(2)}) %collective-permute-start.2) | collective-permute-done | bytes 3145760 | tf_op jit(solution)/shard_map/while/body/eval_jaxpr/ppermute | solution.py:120
  4372.8 29.8 collective-permute-done.3
  4419.0 430.8 %collective-permute-done.2 = bf16[4,256,12,128]{3,1,2,0:T(8,128)(2,1)} collective-permute-done((bf16[4,256,12,128]{3,1,2,0:T(8,128)(2,1)}, bf16[4,256,12,128]{3,1,2,0:T(8,128)(2,1)}, u32[]{:S(2)}, u32[]{:S(2)}) %collective-permute-start.2) | collective-permute-done | bytes 3145760 | tf_op jit(solution)/shard_map/while/body/eval_jaxpr/ppermute | solution.py:120
  4853.7 29.8 collective-permute-done.3
  4899.9 430.8 %collective-permute-done.2 = bf16[4,256,12,128]{3,1,2,0:T(8,128)(2,1)} collective-permute-done((bf16[4,256,12,128]{3,1,2,0:T(8,128)(2,1)}, bf16[4,256,12,128]{3,1,2,0:T(8,128)(2,1)}, u32[]{:S(2)}, u32[]{:S(2)}) %collective-permute-start.2) | collective-permute-done | bytes 3145760 | tf_op jit(solution)/shard_map/while/body/eval_jaxpr/ppermute | solution.py:120
  5334.6 29.8 collective-permute-done.3
  5380.9 10.2 slice.27
  5391.1 94.9 %rev.9 = f32[2048,12,128]{2,0,1:T(8,128)} reverse(f32[2048,12,128]{2,0,1:T(8,128)} %slice.27), dimensions={0} | reverse | bytes 25165824 | tf_op jit(solution)/shard_map/jit(_flip)/rev | solution.py:130
  5513.3 414.6 %all-reduce.5 = (f32[12,128]{1,0:T(8,128)}, f32[12,128]{1,0:T(8,128)}) all-reduce(f32[12,128]{1,0:T(8,128)S(1)} %get-tuple-element.971, f32[12,128]{1,0:T(8,128)S(1)} %reduce_sum.47), channel_id=1, replica_groups=mesh['cp'=8] {'cp'}, use_global_device_ids=true, to_apply=%region_18.19 | all-reduce | flops 3072 | bytes 24576 | tf_op jit(solution)/shard_map/psum | solution.py:128
  5927.9 27.1 all-reduce.8.cloned.1.call-done
  5960.5 10.2 copy.201
  (174 shorter events, 348.9 us)
Async XLA Ops:
  7.2 4.6 copy-start.14
  7.2 4.6 copy-start.15
  7.2 5947.7 %all-reduce.8.cloned.1.call-start = ((), (), s32[]{:S(2)}) async-start(), calls=%async_computation | async-start | bytes 25165824 | tf_op jit(solution)/shard_map/psum | solution.py:130
  7.2 2.8 copy-start.13
  10.1 108.2 %copy-start.6 = (bf16[4,256,12,128]{3,1,2,0:T(8,128)(2,1)}, bf16[4,256,12,128]{3,1,2,0:T(8,128)(2,1)S(1)}, u32[]{:S(2)}) copy-start(bf16[4,256,12,128]{3,1,2,0:T(8,128)(2,1)S(1)} %copy.197) | copy-start | bytes 9437188
  106.5 4.8 copy-start.9
  106.5 4.8 copy-start.11
  106.5 7.7 slice-start.2
  108.3 6.4 slice-start.3
  118.3 15.3 copy-start.7
  272.2 4.8 copy-start.12
  295.9 38.7 collective-permute-start
  296.8 71.5 %collective-permute-start.1 = (bf16[4,256,12,128]{3,1,2,0:T(8,128)(2,1)}, bf16[4,256,12,128]{3,1,2,0:T(8,128)(2,1)}, u32[]{:S(2)}, u32[]{:S(2)}) collective-permute-start(bf16[4,256,12,128]{3,1,2,0:T(8,128)(2,1)} %get-tuple-element.1181), channel_id=1, source_target_pairs={{0,1},{1,2},{2,3},{3,4},{4,5},{5,6},{6,7},{7,0}} | collective-permute-start | bytes 9437192 | tf_op jit(solution)/shard_map/while/body/eval_jaxpr/ppermute | solution.py:92
  376.2 199.5 %collective-permute-start = (bf16[4,256,12,128]{3,1,2,0:T(8,128)(2,1)}, bf16[4,256,12,128]{3,1,2,0:T(8,128)(2,1)}, u32[]{:S(2)}, u32[]{:S(2)}) collective-permute-start(bf16[4,256,12,128]{3,1,2,0:T(8,128)(2,1)} %get-tuple-element.1180), channel_id=1, source_target_pairs={{0,1},{1,2},{2,3},{3,4},{4,5},{5,6},{6,7},{7,0}} | collective-permute-start | bytes 9437192 | tf_op jit(solution)/shard_map/while/body/eval_jaxpr/ppermute | solution.py:91
  540.4 69.0 %collective-permute-start.1 = (bf16[4,256,12,128]{3,1,2,0:T(8,128)(2,1)}, bf16[4,256,12,128]{3,1,2,0:T(8,128)(2,1)}, u32[]{:S(2)}, u32[]{:S(2)}) collective-permute-start(bf16[4,256,12,128]{3,1,2,0:T(8,128)(2,1)} %get-tuple-element.1181), channel_id=1, source_target_pairs={{0,1},{1,2},{2,3},{3,4},{4,5},{5,6},{6,7},{7,0}} | collective-permute-start | bytes 9437192 | tf_op jit(solution)/shard_map/while/body/eval_jaxpr/ppermute | solution.py:92
  617.2 199.5 %collective-permute-start = (bf16[4,256,12,128]{3,1,2,0:T(8,128)(2,1)}, bf16[4,256,12,128]{3,1,2,0:T(8,128)(2,1)}, u32[]{:S(2)}, u32[]{:S(2)}) collective-permute-start(bf16[4,256,12,128]{3,1,2,0:T(8,128)(2,1)} %get-tuple-element.1180), channel_id=1, source_target_pairs={{0,1},{1,2},{2,3},{3,4},{4,5},{5,6},{6,7},{7,0}} | collective-permute-start | bytes 9437192 | tf_op jit(solution)/shard_map/while/body/eval_jaxpr/ppermute | solution.py:91
  618.7 231.8 %collective-permute-start.1 = (bf16[4,256,12,128]{3,1,2,0:T(8,128)(2,1)}, bf16[4,256,12,128]{3,1,2,0:T(8,128)(2,1)}, u32[]{:S(2)}, u32[]{:S(2)}) collective-permute-start(bf16[4,256,12,128]{3,1,2,0:T(8,128)(2,1)} %get-tuple-element.1181), channel_id=1, source_target_pairs={{0,1},{1,2},{2,3},{3,4},{4,5},{5,6},{6,7},{7,0}} | collective-permute-start | bytes 9437192 | tf_op jit(solution)/shard_map/while/body/eval_jaxpr/ppermute | solution.py:92
  858.2 199.5 %collective-permute-start = (bf16[4,256,12,128]{3,1,2,0:T(8,128)(2,1)}, bf16[4,256,12,128]{3,1,2,0:T(8,128)(2,1)}, u32[]{:S(2)}, u32[]{:S(2)}) collective-permute-start(bf16[4,256,12,128]{3,1,2,0:T(8,128)(2,1)} %get-tuple-element.1180), channel_id=1, source_target_pairs={{0,1},{1,2},{2,3},{3,4},{4,5},{5,6},{6,7},{7,0}} | collective-permute-start | bytes 9437192 | tf_op jit(solution)/shard_map/while/body/eval_jaxpr/ppermute | solution.py:91
  862.2 229.3 %collective-permute-start.1 = (bf16[4,256,12,128]{3,1,2,0:T(8,128)(2,1)}, bf16[4,256,12,128]{3,1,2,0:T(8,128)(2,1)}, u32[]{:S(2)}, u32[]{:S(2)}) collective-permute-start(bf16[4,256,12,128]{3,1,2,0:T(8,128)(2,1)} %get-tuple-element.1181), channel_id=1, source_target_pairs={{0,1},{1,2},{2,3},{3,4},{4,5},{5,6},{6,7},{7,0}} | collective-permute-start | bytes 9437192 | tf_op jit(solution)/shard_map/while/body/eval_jaxpr/ppermute | solution.py:92
  1099.3 199.5 %collective-permute-start = (bf16[4,256,12,128]{3,1,2,0:T(8,128)(2,1)}, bf16[4,256,12,128]{3,1,2,0:T(8,128)(2,1)}, u32[]{:S(2)}, u32[]{:S(2)}) collective-permute-start(bf16[4,256,12,128]{3,1,2,0:T(8,128)(2,1)} %get-tuple-element.1180), channel_id=1, source_target_pairs={{0,1},{1,2},{2,3},{3,4},{4,5},{5,6},{6,7},{7,0}} | collective-permute-start | bytes 9437192 | tf_op jit(solution)/shard_map/while/body/eval_jaxpr/ppermute | solution.py:91
  1099.3 233.2 %collective-permute-start.1 = (bf16[4,256,12,128]{3,1,2,0:T(8,128)(2,1)}, bf16[4,256,12,128]{3,1,2,0:T(8,128)(2,1)}, u32[]{:S(2)}, u32[]{:S(2)}) collective-permute-start(bf16[4,256,12,128]{3,1,2,0:T(8,128)(2,1)} %get-tuple-element.1181), channel_id=1, source_target_pairs={{0,1},{1,2},{2,3},{3,4},{4,5},{5,6},{6,7},{7,0}} | collective-permute-start | bytes 9437192 | tf_op jit(solution)/shard_map/while/body/eval_jaxpr/ppermute | solution.py:92
  1340.3 199.5 %collective-permute-start = (bf16[4,256,12,128]{3,1,2,0:T(8,128)(2,1)}, bf16[4,256,12,128]{3,1,2,0:T(8,128)(2,1)}, u32[]{:S(2)}, u32[]{:S(2)}) collective-permute-start(bf16[4,256,12,128]{3,1,2,0:T(8,128)(2,1)} %get-tuple-element.1180), channel_id=1, source_target_pairs={{0,1},{1,2},{2,3},{3,4},{4,5},{5,6},{6,7},{7,0}} | collective-permute-start | bytes 9437192 | tf_op jit(solution)/shard_map/while/body/eval_jaxpr/ppermute | solution.py:91
  1340.3 233.2 %collective-permute-start.1 = (bf16[4,256,12,128]{3,1,2,0:T(8,128)(2,1)}, bf16[4,256,12,128]{3,1,2,0:T(8,128)(2,1)}, u32[]{:S(2)}, u32[]{:S(2)}) collective-permute-start(bf16[4,256,12,128]{3,1,2,0:T(8,128)(2,1)} %get-tuple-element.1181), channel_id=1, source_target_pairs={{0,1},{1,2},{2,3},{3,4},{4,5},{5,6},{6,7},{7,0}} | collective-permute-start | bytes 9437192 | tf_op jit(solution)/shard_map/while/body/eval_jaxpr/ppermute | solution.py:92
  1581.3 199.5 %collective-permute-start = (bf16[4,256,12,128]{3,1,2,0:T(8,128)(2,1)}, bf16[4,256,12,128]{3,1,2,0:T(8,128)(2,1)}, u32[]{:S(2)}, u32[]{:S(2)}) collective-permute-start(bf16[4,256,12,128]{3,1,2,0:T(8,128)(2,1)} %get-tuple-element.1180), channel_id=1, source_target_pairs={{0,1},{1,2},{2,3},{3,4},{4,5},{5,6},{6,7},{7,0}} | collective-permute-start | bytes 9437192 | tf_op jit(solution)/shard_map/while/body/eval_jaxpr/ppermute | solution.py:91
  1581.3 233.2 %collective-permute-start.1 = (bf16[4,256,12,128]{3,1,2,0:T(8,128)(2,1)}, bf16[4,256,12,128]{3,1,2,0:T(8,128)(2,1)}, u32[]{:S(2)}, u32[]{:S(2)}) collective-permute-start(bf16[4,256,12,128]{3,1,2,0:T(8,128)(2,1)} %get-tuple-element.1181), channel_id=1, source_target_pairs={{0,1},{1,2},{2,3},{3,4},{4,5},{5,6},{6,7},{7,0}} | collective-permute-start | bytes 9437192 | tf_op jit(solution)/shard_map/while/body/eval_jaxpr/ppermute | solution.py:92
  1831.5 279.3 %copy-start.1 = (bf16[4,256,12,128]{3,1,2,0:T(8,128)(2,1)S(1)}, bf16[4,256,12,128]{3,1,2,0:T(8,128)(2,1)}, u32[]{:S(2)}) copy-start(bf16[4,256,12,128]{3,1,2,0:T(8,128)(2,1)} %get-tuple-element.1291) | copy-start | bytes 9437188
  1951.6 10.9 copy-start.2
  1972.0 2.7 copy-start.5
  2054.8 12.0 copy-start.8
  2066.9 7.5 copy-start.10
  2074.4 7.5 copy-start.3
  2110.8 372.0 %collective-permute-start.4 = (f32[4,256,12,128]{3,1,2,0:T(8,128)}, f32[4,256,12,128]{3,1,2,0:T(8,128)}, u32[]{:S(2)}, u32[]{:S(2)}) collective-permute-start(f32[4,256,12,128]{3,1,2,0:T(8,128)} %get-tuple-element.1239), channel_id=1, source_target_pairs={{0,1},{1,2},{2,3},{3,4},{4,5},{5,6},{6,7},{7,0}} | collective-permute-start | bytes 18874376 | tf_op jit(solution)/shard_map/while/body/eval_jaxpr/ppermute | solution.py:120
  2110.8 371.9 %collective-permute-start.5 = (f32[4,256,12,128]{3,1,2,0:T(8,128)}, f32[4,256,12,128]{3,1,2,0:T(8,128)}, u32[]{:S(2)}, u32[]{:S(2)}) collective-permute-start(f32[4,256,12,128]{3,1,2,0:T(8,128)} %get-tuple-element.1240), channel_id=1, source_target_pairs={{0,1},{1,2},{2,3},{3,4},{4,5},{5,6},{6,7},{7,0}} | collective-permute-start | bytes 18874376 | tf_op jit(solution)/shard_map/while/body/eval_jaxpr/ppermute | solution.py:120
  2110.8 334.3 %collective-permute-start.2 = (bf16[4,256,12,128]{3,1,2,0:T(8,128)(2,1)}, bf16[4,256,12,128]{3,1,2,0:T(8,128)(2,1)}, u32[]{:S(2)}, u32[]{:S(2)}) collective-permute-start(bf16[4,256,12,128]{3,1,2,0:T(8,128)(2,1)} %get-tuple-element.1237), channel_id=1, source_target_pairs={{0,1},{1,2},{2,3},{3,4},{4,5},{5,6},{6,7},{7,0}} | collective-permute-start | bytes 9437192 | tf_op jit(solution)/shard_map/while/body/eval_jaxpr/ppermute | solution.py:120
  2110.9 367.9 %collective-permute-start.3 = (bf16[4,256,12,128]{3,1,2,0:T(8,128)(2,1)}, bf16[4,256,12,128]{3,1,2,0:T(8,128)(2,1)}, u32[]{:S(2)}, u32[]{:S(2)}) collective-permute-start(bf16[4,256,12,128]{3,1,2,0:T(8,128)(2,1)} %get-tuple-element.1238), channel_id=1, source_target_pairs={{0,1},{1,2},{2,3},{3,4},{4,5},{5,6},{6,7},{7,0}} | collective-permute-start | bytes 9437192 | tf_op jit(solution)/shard_map/while/body/eval_jaxpr/ppermute | solution.py:120
  2495.1 468.5 %collective-permute-start.4 = (f32[4,256,12,128]{3,1,2,0:T(8,128)}, f32[4,256,12,128]{3,1,2,0:T(8,128)}, u32[]{:S(2)}, u32[]{:S(2)}) collective-permute-start(f32[4,256,12,128]{3,1,2,0:T(8,128)} %get-tuple-element.1239), channel_id=1, source_target_pairs={{0,1},{1,2},{2,3},{3,4},{4,5},{5,6},{6,7},{7,0}} | collective-permute-start | bytes 18874376 | tf_op jit(solution)/shard_map/while/body/eval_jaxpr/ppermute | solution.py:120
  2495.1 468.5 %collective-permute-start.5 = (f32[4,256,12,128]{3,1,2,0:T(8,128)}, f32[4,256,12,128]{3,1,2,0:T(8,128)}, u32[]{:S(2)}, u32[]{:S(2)}) collective-permute-start(f32[4,256,12,128]{3,1,2,0:T(8,128)} %get-tuple-element.1240), channel_id=1, source_target_pairs={{0,1},{1,2},{2,3},{3,4},{4,5},{5,6},{6,7},{7,0}} | collective-permute-start | bytes 18874376 | tf_op jit(solution)/shard_map/while/body/eval_jaxpr/ppermute | solution.py:120
  2495.1 430.9 %collective-permute-start.2 = (bf16[4,256,12,128]{3,1,2,0:T(8,128)(2,1)}, bf16[4,256,12,128]{3,1,2,0:T(8,128)(2,1)}, u32[]{:S(2)}, u32[]{:S(2)}) collective-permute-start(bf16[4,256,12,128]{3,1,2,0:T(8,128)(2,1)} %get-tuple-element.1237), channel_id=1, source_target_pairs={{0,1},{1,2},{2,3},{3,4},{4,5},{5,6},{6,7},{7,0}} | collective-permute-start | bytes 9437192 | tf_op jit(solution)/shard_map/while/body/eval_jaxpr/ppermute | solution.py:120
  2590.5 369.2 %collective-permute-start.3 = (bf16[4,256,12,128]{3,1,2,0:T(8,128)(2,1)}, bf16[4,256,12,128]{3,1,2,0:T(8,128)(2,1)}, u32[]{:S(2)}, u32[]{:S(2)}) collective-permute-start(bf16[4,256,12,128]{3,1,2,0:T(8,128)(2,1)} %get-tuple-element.1238), channel_id=1, source_target_pairs={{0,1},{1,2},{2,3},{3,4},{4,5},{5,6},{6,7},{7,0}} | collective-permute-start | bytes 9437192 | tf_op jit(solution)/shard_map/while/body/eval_jaxpr/ppermute | solution.py:120
  2976.0 468.6 %collective-permute-start.4 = (f32[4,256,12,128]{3,1,2,0:T(8,128)}, f32[4,256,12,128]{3,1,2,0:T(8,128)}, u32[]{:S(2)}, u32[]{:S(2)}) collective-permute-start(f32[4,256,12,128]{3,1,2,0:T(8,128)} %get-tuple-element.1239), channel_id=1, source_target_pairs={{0,1},{1,2},{2,3},{3,4},{4,5},{5,6},{6,7},{7,0}} | collective-permute-start | bytes 18874376 | tf_op jit(solution)/shard_map/while/body/eval_jaxpr/ppermute | solution.py:120
  2976.0 468.6 %collective-permute-start.5 = (f32[4,256,12,128]{3,1,2,0:T(8,128)}, f32[4,256,12,128]{3,1,2,0:T(8,128)}, u32[]{:S(2)}, u32[]{:S(2)}) collective-permute-start(f32[4,256,12,128]{3,1,2,0:T(8,128)} %get-tuple-element.1240), channel_id=1, source_target_pairs={{0,1},{1,2},{2,3},{3,4},{4,5},{5,6},{6,7},{7,0}} | collective-permute-start | bytes 18874376 | tf_op jit(solution)/shard_map/while/body/eval_jaxpr/ppermute | solution.py:120
  3006.5 400.5 %collective-permute-start.2 = (bf16[4,256,12,128]{3,1,2,0:T(8,128)(2,1)}, bf16[4,256,12,128]{3,1,2,0:T(8,128)(2,1)}, u32[]{:S(2)}, u32[]{:S(2)}) collective-permute-start(bf16[4,256,12,128]{3,1,2,0:T(8,128)(2,1)} %get-tuple-element.1237), channel_id=1, source_target_pairs={{0,1},{1,2},{2,3},{3,4},{4,5},{5,6},{6,7},{7,0}} | collective-permute-start | bytes 9437192 | tf_op jit(solution)/shard_map/while/body/eval_jaxpr/ppermute | solution.py:120
  3105.2 335.5 %collective-permute-start.3 = (bf16[4,256,12,128]{3,1,2,0:T(8,128)(2,1)}, bf16[4,256,12,128]{3,1,2,0:T(8,128)(2,1)}, u32[]{:S(2)}, u32[]{:S(2)}) collective-permute-start(bf16[4,256,12,128]{3,1,2,0:T(8,128)(2,1)} %get-tuple-element.1238), channel_id=1, source_target_pairs={{0,1},{1,2},{2,3},{3,4},{4,5},{5,6},{6,7},{7,0}} | collective-permute-start | bytes 9437192 | tf_op jit(solution)/shard_map/while/body/eval_jaxpr/ppermute | solution.py:120
  3457.0 468.6 %collective-permute-start.4 = (f32[4,256,12,128]{3,1,2,0:T(8,128)}, f32[4,256,12,128]{3,1,2,0:T(8,128)}, u32[]{:S(2)}, u32[]{:S(2)}) collective-permute-start(f32[4,256,12,128]{3,1,2,0:T(8,128)} %get-tuple-element.1239), channel_id=1, source_target_pairs={{0,1},{1,2},{2,3},{3,4},{4,5},{5,6},{6,7},{7,0}} | collective-permute-start | bytes 18874376 | tf_op jit(solution)/shard_map/while/body/eval_jaxpr/ppermute | solution.py:120
  3457.0 468.6 %collective-permute-start.5 = (f32[4,256,12,128]{3,1,2,0:T(8,128)}, f32[4,256,12,128]{3,1,2,0:T(8,128)}, u32[]{:S(2)}, u32[]{:S(2)}) collective-permute-start(f32[4,256,12,128]{3,1,2,0:T(8,128)} %get-tuple-element.1240), channel_id=1, source_target_pairs={{0,1},{1,2},{2,3},{3,4},{4,5},{5,6},{6,7},{7,0}} | collective-permute-start | bytes 18874376 | tf_op jit(solution)/shard_map/while/body/eval_jaxpr/ppermute | solution.py:120
  3457.0 431.0 %collective-permute-start.2 = (bf16[4,256,12,128]{3,1,2,0:T(8,128)(2,1)}, bf16[4,256,12,128]{3,1,2,0:T(8,128)(2,1)}, u32[]{:S(2)}, u32[]{:S(2)}) collective-permute-start(bf16[4,256,12,128]{3,1,2,0:T(8,128)(2,1)} %get-tuple-element.1237), channel_id=1, source_target_pairs={{0,1},{1,2},{2,3},{3,4},{4,5},{5,6},{6,7},{7,0}} | collective-permute-start | bytes 9437192 | tf_op jit(solution)/shard_map/while/body/eval_jaxpr/ppermute | solution.py:120
  3589.5 332.2 %collective-permute-start.3 = (bf16[4,256,12,128]{3,1,2,0:T(8,128)(2,1)}, bf16[4,256,12,128]{3,1,2,0:T(8,128)(2,1)}, u32[]{:S(2)}, u32[]{:S(2)}) collective-permute-start(bf16[4,256,12,128]{3,1,2,0:T(8,128)(2,1)} %get-tuple-element.1238), channel_id=1, source_target_pairs={{0,1},{1,2},{2,3},{3,4},{4,5},{5,6},{6,7},{7,0}} | collective-permute-start | bytes 9437192 | tf_op jit(solution)/shard_map/while/body/eval_jaxpr/ppermute | solution.py:120
  3938.0 468.5 %collective-permute-start.4 = (f32[4,256,12,128]{3,1,2,0:T(8,128)}, f32[4,256,12,128]{3,1,2,0:T(8,128)}, u32[]{:S(2)}, u32[]{:S(2)}) collective-permute-start(f32[4,256,12,128]{3,1,2,0:T(8,128)} %get-tuple-element.1239), channel_id=1, source_target_pairs={{0,1},{1,2},{2,3},{3,4},{4,5},{5,6},{6,7},{7,0}} | collective-permute-start | bytes 18874376 | tf_op jit(solution)/shard_map/while/body/eval_jaxpr/ppermute | solution.py:120
  3938.0 468.5 %collective-permute-start.5 = (f32[4,256,12,128]{3,1,2,0:T(8,128)}, f32[4,256,12,128]{3,1,2,0:T(8,128)}, u32[]{:S(2)}, u32[]{:S(2)}) collective-permute-start(f32[4,256,12,128]{3,1,2,0:T(8,128)} %get-tuple-element.1240), channel_id=1, source_target_pairs={{0,1},{1,2},{2,3},{3,4},{4,5},{5,6},{6,7},{7,0}} | collective-permute-start | bytes 18874376 | tf_op jit(solution)/shard_map/while/body/eval_jaxpr/ppermute | solution.py:120
  3938.0 430.9 %collective-permute-start.2 = (bf16[4,256,12,128]{3,1,2,0:T(8,128)(2,1)}, bf16[4,256,12,128]{3,1,2,0:T(8,128)(2,1)}, u32[]{:S(2)}, u32[]{:S(2)}) collective-permute-start(bf16[4,256,12,128]{3,1,2,0:T(8,128)(2,1)} %get-tuple-element.1237), channel_id=1, source_target_pairs={{0,1},{1,2},{2,3},{3,4},{4,5},{5,6},{6,7},{7,0}} | collective-permute-start | bytes 9437192 | tf_op jit(solution)/shard_map/while/body/eval_jaxpr/ppermute | solution.py:120
  3938.0 464.6 %collective-permute-start.3 = (bf16[4,256,12,128]{3,1,2,0:T(8,128)(2,1)}, bf16[4,256,12,128]{3,1,2,0:T(8,128)(2,1)}, u32[]{:S(2)}, u32[]{:S(2)}) collective-permute-start(bf16[4,256,12,128]{3,1,2,0:T(8,128)(2,1)} %get-tuple-element.1238), channel_id=1, source_target_pairs={{0,1},{1,2},{2,3},{3,4},{4,5},{5,6},{6,7},{7,0}} | collective-permute-start | bytes 9437192 | tf_op jit(solution)/shard_map/while/body/eval_jaxpr/ppermute | solution.py:120
  4418.9 468.5 %collective-permute-start.4 = (f32[4,256,12,128]{3,1,2,0:T(8,128)}, f32[4,256,12,128]{3,1,2,0:T(8,128)}, u32[]{:S(2)}, u32[]{:S(2)}) collective-permute-start(f32[4,256,12,128]{3,1,2,0:T(8,128)} %get-tuple-element.1239), channel_id=1, source_target_pairs={{0,1},{1,2},{2,3},{3,4},{4,5},{5,6},{6,7},{7,0}} | collective-permute-start | bytes 18874376 | tf_op jit(solution)/shard_map/while/body/eval_jaxpr/ppermute | solution.py:120
  4418.9 468.5 %collective-permute-start.5 = (f32[4,256,12,128]{3,1,2,0:T(8,128)}, f32[4,256,12,128]{3,1,2,0:T(8,128)}, u32[]{:S(2)}, u32[]{:S(2)}) collective-permute-start(f32[4,256,12,128]{3,1,2,0:T(8,128)} %get-tuple-element.1240), channel_id=1, source_target_pairs={{0,1},{1,2},{2,3},{3,4},{4,5},{5,6},{6,7},{7,0}} | collective-permute-start | bytes 18874376 | tf_op jit(solution)/shard_map/while/body/eval_jaxpr/ppermute | solution.py:120
  4418.9 430.9 %collective-permute-start.2 = (bf16[4,256,12,128]{3,1,2,0:T(8,128)(2,1)}, bf16[4,256,12,128]{3,1,2,0:T(8,128)(2,1)}, u32[]{:S(2)}, u32[]{:S(2)}) collective-permute-start(bf16[4,256,12,128]{3,1,2,0:T(8,128)(2,1)} %get-tuple-element.1237), channel_id=1, source_target_pairs={{0,1},{1,2},{2,3},{3,4},{4,5},{5,6},{6,7},{7,0}} | collective-permute-start | bytes 9437192 | tf_op jit(solution)/shard_map/while/body/eval_jaxpr/ppermute | solution.py:120
  4418.9 464.6 %collective-permute-start.3 = (bf16[4,256,12,128]{3,1,2,0:T(8,128)(2,1)}, bf16[4,256,12,128]{3,1,2,0:T(8,128)(2,1)}, u32[]{:S(2)}, u32[]{:S(2)}) collective-permute-start(bf16[4,256,12,128]{3,1,2,0:T(8,128)(2,1)} %get-tuple-element.1238), channel_id=1, source_target_pairs={{0,1},{1,2},{2,3},{3,4},{4,5},{5,6},{6,7},{7,0}} | collective-permute-start | bytes 9437192 | tf_op jit(solution)/shard_map/while/body/eval_jaxpr/ppermute | solution.py:120
  4899.8 468.5 %collective-permute-start.4 = (f32[4,256,12,128]{3,1,2,0:T(8,128)}, f32[4,256,12,128]{3,1,2,0:T(8,128)}, u32[]{:S(2)}, u32[]{:S(2)}) collective-permute-start(f32[4,256,12,128]{3,1,2,0:T(8,128)} %get-tuple-element.1239), channel_id=1, source_target_pairs={{0,1},{1,2},{2,3},{3,4},{4,5},{5,6},{6,7},{7,0}} | collective-permute-start | bytes 18874376 | tf_op jit(solution)/shard_map/while/body/eval_jaxpr/ppermute | solution.py:120
  4899.8 468.5 %collective-permute-start.5 = (f32[4,256,12,128]{3,1,2,0:T(8,128)}, f32[4,256,12,128]{3,1,2,0:T(8,128)}, u32[]{:S(2)}, u32[]{:S(2)}) collective-permute-start(f32[4,256,12,128]{3,1,2,0:T(8,128)} %get-tuple-element.1240), channel_id=1, source_target_pairs={{0,1},{1,2},{2,3},{3,4},{4,5},{5,6},{6,7},{7,0}} | collective-permute-start | bytes 18874376 | tf_op jit(solution)/shard_map/while/body/eval_jaxpr/ppermute | solution.py:120
  4899.8 430.9 %collective-permute-start.2 = (bf16[4,256,12,128]{3,1,2,0:T(8,128)(2,1)}, bf16[4,256,12,128]{3,1,2,0:T(8,128)(2,1)}, u32[]{:S(2)}, u32[]{:S(2)}) collective-permute-start(bf16[4,256,12,128]{3,1,2,0:T(8,128)(2,1)} %get-tuple-element.1237), channel_id=1, source_target_pairs={{0,1},{1,2},{2,3},{3,4},{4,5},{5,6},{6,7},{7,0}} | collective-permute-start | bytes 9437192 | tf_op jit(solution)/shard_map/while/body/eval_jaxpr/ppermute | solution.py:120
  4899.9 464.6 %collective-permute-start.3 = (bf16[4,256,12,128]{3,1,2,0:T(8,128)(2,1)}, bf16[4,256,12,128]{3,1,2,0:T(8,128)(2,1)}, u32[]{:S(2)}, u32[]{:S(2)}) collective-permute-start(bf16[4,256,12,128]{3,1,2,0:T(8,128)(2,1)} %get-tuple-element.1238), channel_id=1, source_target_pairs={{0,1},{1,2},{2,3},{3,4},{4,5},{5,6},{6,7},{7,0}} | collective-permute-start | bytes 9437192 | tf_op jit(solution)/shard_map/while/body/eval_jaxpr/ppermute | solution.py:120
  5490.9 436.9 %collective-permute-start.6 = (bf16[4,256,12,128]{3,1,2,0:T(8,128)(2,1)}, bf16[4,256,12,128]{3,1,2,0:T(8,128)(2,1)S(1)}, u32[]{:S(2)}, u32[]{:S(2)}) collective-permute-start(bf16[4,256,12,128]{3,1,2,0:T(8,128)(2,1)} %convert.10), channel_id=1, source_target_pairs={{0,1},{1,2},{2,3},{3,4},{4,5},{5,6},{6,7},{7,0}} | collective-permute-start | bytes 9437192 | tf_op jit(solution)/shard_map/ppermute | solution.py:124
  5495.9 432.0 %collective-permute-start.7 = (bf16[4,256,12,128]{3,1,2,0:T(8,128)(2,1)}, bf16[4,256,12,128]{3,1,2,0:T(8,128)(2,1)}, u32[]{:S(2)}, u32[]{:S(2)}) collective-permute-start(bf16[4,256,12,128]{3,1,2,0:T(8,128)(2,1)} %convert.11), channel_id=1, source_target_pairs={{0,1},{1,2},{2,3},{3,4},{4,5},{5,6},{6,7},{7,0}} | collective-permute-start | bytes 9437192 | tf_op jit(solution)/shard_map/ppermute | solution.py:125
Sparse Core Ops, SparseCore 0:
  5486.1 468.7 all-reduce.7
where the time goes:
time: 6030 us; the launch traced here: 5980 us
  waiting for transfers between devices  3770 us (63%)
  starting transfers between devices  853 us (14%)
  local copies, waits for them, and re-layouts  737 us (12%)
  blocking collectives  415 us (7%)
  matrix products  113 us (2%)
    ppermute x28, waiting for transfers between devices, bwd_body(): lax.ppermute(travel, 'cp', shift_pairs)  2620 us
    ppermute x7, waiting for transfers between devices, fwd_body(): key_blk = lax.ppermute(key_blk, 'cp', shift_pairs)  890 us
    ppermute x28, starting transfers between devices, bwd_body(): lax.ppermute(travel, 'cp', shift_pairs)  507 us
    psum x1, blocking collectives, local(): d_bias_u = lax.psum(jnp.sum(dq_cont, axis=(0, 1)), 'cp')  415 us
    ppermute x7, waiting for transfers between devices, fwd_body(): val_blk = lax.ppermute(val_blk, 'cp', shift_pairs)  236 us
    while x42, local copies, waits for them, and re-layouts  196 us
    ppermute x7, starting transfers between devices, fwd_body(): val_blk = lax.ppermute(val_blk, 'cp', shift_pairs)  175 us
    ppermute x7, starting transfers between devices, fwd_body(): key_blk = lax.ppermute(key_blk, 'cp', shift_pairs)  171 us
  transfers between devices with their start and end apart: 45, of which 29 were waited for; matrix products, arithmetic and copies ran while one was open for 1% of the time, Pallas kernels for 0%

commit v1 on v0

v1 whole, which is shorter than its diff:
```python
import jax
import jax.numpy as jnp
from jax import lax
from jax.experimental import pallas as pl
from jax.experimental.pallas import tpu as pltpu
from jax.sharding import PartitionSpec as P

T = 256
D = 128
H = 128
NT = 8
NU = 6
F32 = jnp.float32
BF = jnp.bfloat16
MESH = pl.DeviceIdType.MESH


def dot_nt(lhs, rhs):
    return lax.dot_general(lhs, rhs, (((1,), (1,)), ((), ())), preferred_element_type=F32)


def dot_nn(lhs, rhs):
    return lax.dot_general(lhs, rhs, (((1,), (0,)), ((), ())), preferred_element_type=F32)


def dot_tn(lhs, rhs):
    return lax.dot_general(lhs, rhs, (((0,), (0,)), ((), ())), preferred_element_type=F32)


def unit(x, rk, u, w, stage, drk, duw, scratch, after_tile):
    s_ref, dp_ref, r_ref, r_ref2, u_ref, dk_ref, dv_ref, a_ref, c_ref, oacc, qc_acc, qr_acc = scratch
    scale = D ** -0.5
    c2 = scale * 1.4426950408889634
    low = lax.broadcasted_iota(jnp.int32, (H, H), 1) <= lax.broadcasted_iota(jnp.int32, (H, H), 0)
    idx = (lax.broadcasted_iota(jnp.int32, (T, H), 0) - lax.broadcasted_iota(jnp.int32, (T, H), 1)) & (H - 1)

    def gather(arr):
        return jnp.take_along_axis(arr, idx, axis=1, mode="promise_in_bounds")

    dk_ref[...] = jnp.zeros_like(dk_ref)
    dv_ref[...] = jnp.zeros_like(dv_ref)

    def tile(ii, _):
        i = NT - 1 - ii
        q = x[i, 0].astype(F32)
        a_ref[...] = (q + u[...]).astype(BF)
        c_ref[...] = (q + w[...]).astype(BF)

        def logits(n, mx):
            j = i - n
            by = dot_nt(c_ref[...], rk[n])
            s = dot_nt(a_ref[...], x[j, 1])
            n0 = gather(by[:, :H])
            n1 = gather(by[:, H:])
            p0 = jnp.where(n == 0, -jnp.inf, r_ref2[...])
            p1 = jnp.where(n == 0, -jnp.inf, r_ref[...])
            lo = jnp.concatenate([jnp.where(low, n0[:H], p1[:H]), jnp.where(low, n1[H:], n0[H:])], 0)
            hi = jnp.concatenate([jnp.where(low, p1[:H], p0), jnp.where(low, n0[H:], p1[H:])], 0)
            s = s + jnp.concatenate([lo, hi], 1)
            r_ref[...] = n1
            r_ref2[...] = n0[:H]
            s_ref[j] = s
            return jnp.maximum(mx, jnp.maximum(s[:, :H], s[:, H:]))

        mx = lax.fori_loop(0, i + 1, logits, jnp.full((T, H), -jnp.inf, F32))
        m = jnp.max(mx, axis=1, keepdims=True)

        def weights(j, carry):
            total, dots = carry
            p = jnp.exp2((s_ref[j] - m) * c2)
            dp = dot_nt(x[i, 3], x[j, 2])
            s_ref[j] = p
            dp_ref[j] = dp
            pd = p * dp
            return total + (p[:, :H] + p[:, H:]), dots + (pd[:, :H] + pd[:, H:])

        zero = jnp.zeros((T, H), F32)
        total, dots = lax.fori_loop(0, i + 1, weights, (zero, zero))
        inv = 1.0 / jnp.sum(total, axis=1, keepdims=True)
        row_dot = jnp.sum(dots, axis=1, keepdims=True) * inv
        oacc[...] = zero
        qc_acc[...] = zero
        qr_acc[...] = zero
        u_ref[...] = jnp.zeros_like(u_ref)

        def grads(j, _):
            pn = s_ref[j] * inv
            pb = pn.astype(BF)
            ds = pn * (dp_ref[j] - row_dot) * scale
            dsb = ds.astype(BF)
            oacc[...] += dot_nn(pb, x[j, 2])
            dv_ref[j] += dot_tn(pb, x[i, 3])
            qc_acc[...] += dot_nn(dsb, x[j, 1])
            dk_ref[j] += dot_tn(dsb, a_ref[...])
            g0 = gather(ds[:, :H])
            g1 = gather(ds[:, H:])
            d0 = jnp.concatenate([jnp.where(low, g0[:H], u_ref[1, :H]), jnp.where(low, g1[H:], g0[H:])], 0)
            d1 = jnp.concatenate([jnp.where(low, u_ref[1, :H], u_ref[0, :H]), jnp.where(low, g0[H:], u_ref[1, H:])], 0)
            dist = jnp.concatenate([d0, d1], 1).astype(BF)
            u_ref[0] = g0
            u_ref[1] = g1
            qr_acc[...] += dot_nn(dist, rk[i - j])
            drk[i - j] += dot_tn(dist, c_ref[...])
            return 0

        lax.fori_loop(0, i + 1, grads, 0)
        qc = qc_acc[...]
        qr = qr_acc[...]
        duw[0:1] += jnp.sum(qc, axis=0, keepdims=True)
        duw[1:2] += jnp.sum(qr, axis=0, keepdims=True)
        stage[i, 0] = oacc[...].astype(BF)
        stage[i, 1] = (qc + qr).astype(BF)
        stage[i, 2] = dk_ref[i].astype(BF)
        stage[i, 3] = dv_ref[i].astype(BF)
        after_tile(i)
        return 0

    lax.fori_loop(0, NT, tile, 0)


UNIT_SCRATCH = [
    pltpu.VMEM((NT, T, T), F32), pltpu.VMEM((NT, T, T), F32), pltpu.VMEM((T, H), F32), pltpu.VMEM((H, H), F32),
    pltpu.VMEM((2, T, H), F32), pltpu.VMEM((NT, T, D), F32), pltpu.VMEM((NT, T, D), F32), pltpu.VMEM((T, D), BF),
    pltpu.VMEM((T, D), BF), pltpu.VMEM((T, D), F32), pltpu.VMEM((T, D), F32), pltpu.VMEM((T, D), F32)]


def kernel(xq, xk, xv, xd, rel, uw, oq, odq, odk, odv, drk_out, duw_out, rin, stage, drk, pbuf, dfin, duw, rk,
           in_send, in_recv, in_loc, out_send, out_recv, out_loc, half_send, half_recv,
           fin_send, fin_recv, fin_loc, rel_send, rel_recv, duw_send, duw_recv, duw_loc, rk_sem, *scratch):
    me = lax.axis_index('cp')
    chip = me // 2
    core = me % 2
    ins = (xq, xk, xv, xd)
    outs = (oq, odq, odk, odv)

    def remote(src, dst, ssem, rsem, dev):
        return pltpu.make_async_remote_copy(src_ref=src, dst_ref=dst, send_sem=ssem, recv_sem=rsem,
                                            device_id=(dev,), device_id_type=MESH)

    def spot(arr, dev, n):
        return arr.at[2 * (dev % 2) + n % 2, 3 * (dev // 2) + n // 2]

    def send_in(n, mask):
        dev = jnp.bitwise_xor(me, mask)
        for a in range(4):
            remote(spot(ins[a], dev, n), rin.at[n, me, a], in_send.at[n, mask], in_recv.at[n, mask], dev).start()

    def in_wait(n, mask):
        dev = jnp.bitwise_xor(me, mask)
        return remote(rin.at[n, dev], rin.at[n, dev], in_send.at[n, mask], in_recv.at[n, mask], dev)

    rk_copy = pltpu.make_async_copy(rel.at[pl.ds(3 * chip, 3)], rk, rk_sem)
    rk_copy.start()
    for n in range(NU):
        for a in range(4):
            pltpu.make_async_copy(spot(ins[a], me, n), rin.at[n, me, a], in_loc.at[n]).start()
        for mask in (6, 2, 4, 7, 3, 5, 1):
            send_in(n, mask)

    drk[...] = jnp.zeros_like(drk)
    duw[...] = jnp.zeros_like(duw)
    rk_copy.wait()

    def half_copy(k):
        return remote(drk.at[k, pl.ds(4 * (1 - core), 4)], pbuf.at[k], half_send.at[k], half_recv.at[k],
                      jnp.bitwise_xor(me, 1))

    def fin_copy(k, n, mask):
        return remote(dfin.at[k], drk_out.at[3 * chip + k, pl.ds(4 * core, 4)], fin_send.at[k, n], fin_recv.at[k, n],
                      jnp.bitwise_xor(me, mask))

    def fin_own(k):
        return pltpu.make_async_copy(dfin.at[k], drk_out.at[3 * chip + k, pl.ds(4 * core, 4)], fin_loc.at[k])

    fin_masks = (1, 6, 2, 4)

    def run_unit(n, _):
        k = n // 2
        pltpu.make_async_copy(rin.at[n, me], rin.at[n, me], in_loc.at[n]).wait()
        for mask in range(1, 8):
            in_wait(n, mask).wait_recv()

        def after_tile(i):
            mask = jnp.bitwise_xor(me, i)

            @pl.when(mask != 0)
            def _():
                for a in range(4):
                    remote(stage.at[n, i, a], spot(outs[a], me, n), out_send.at[n, i], out_recv.at[n, mask], i).start()

            @pl.when(mask == 0)
            def _():
                for a in range(4):
                    pltpu.make_async_copy(stage.at[n, i, a], spot(outs[a], me, n), out_loc.at[n]).start()

        unit(rin.at[n], rk.at[k], uw.at[k, 0:1], uw.at[k, 1:2], stage.at[n], drk.at[k], duw.at[k], scratch, after_tile)

        @pl.when(n % 2 == 1)
        def _():
            copy = half_copy(k)
            copy.start()
            copy.wait()
            dfin[k] = drk[k, pl.ds(4 * core, 4)] + pbuf[k]
            for s, mask in enumerate(fin_masks):
                fin_copy(k, s, mask).start()
            fin_own(k).start()
        return 0

    lax.fori_loop(0, NU, run_unit, 0)

    def duw_copy(mask):
        return remote(duw, duw_out.at[me], duw_send.at[mask], duw_recv.at[mask], jnp.bitwise_xor(me, mask))

    for mask in range(1, 8):
        duw_copy(mask).start()
    duw_own = pltpu.make_async_copy(duw, duw_out.at[me], duw_loc)
    duw_own.start()

    def relay(k, s):
        part = drk_out.at[3 * jnp.bitwise_xor(chip, fin_masks[s] // 2) + k, pl.ds(4 * core, 4)]
        return remote(part, part, rel_send.at[k, s], rel_recv.at[k, s], jnp.bitwise_xor(me, 1))

    for k in range(3):
        for s in range(1, 4):
            fin_copy(k, s, fin_masks[s]).wait_recv()
            relay(k, s).start()

    def finish(n, _):
        for mask in range(1, 8):
            dev = jnp.bitwise_xor(me, mask)
            in_wait(n, mask).wait_send()
            remote(stage.at[n, dev], stage.at[n, dev], out_send.at[n, dev], out_recv.at[n, mask], dev).wait()
        pltpu.make_async_copy(stage.at[n, me], stage.at[n, me], out_loc.at[n]).wait()
        return 0

    lax.fori_loop(0, NU, finish, 0)
    for k in range(3):
        fin_copy(k, 0, 1).wait()
        fin_own(k).wait()
        for s in range(1, 4):
            fin_copy(k, s, fin_masks[s]).wait_send()
            relay(k, s).wait()
    for mask in range(1, 8):
        duw_copy(mask).wait()
    duw_own.wait()


def exchange_attend(xq, xk, xv, xd, rel, uw):
    any_spec = pl.BlockSpec(memory_space=pl.ANY)
    vmem_spec = pl.BlockSpec(memory_space=pltpu.VMEM)
    dma = pltpu.SemaphoreType.DMA
    act = jax.ShapeDtypeStruct((4, 12, T, D), BF)
    return pl.pallas_call(
        kernel,
        out_shape=(act, act, act, act, jax.ShapeDtypeStruct((12, NT, T, D), F32),
                   jax.ShapeDtypeStruct((8, 3, 8, D), F32)),
        in_specs=[any_spec] * 5 + [vmem_spec],
        out_specs=(any_spec,) * 6,
        scratch_shapes=[
            pltpu.VMEM((NU, 8, 4, T, D), BF), pltpu.VMEM((NU, NT, 4, T, D), BF), pltpu.VMEM((3, NT, T, D), F32),
            pltpu.VMEM((3, 4, T, D), F32), pltpu.VMEM((3, 4, T, D), F32), pltpu.VMEM((3, 8, D), F32),
            pltpu.VMEM((3, NT, T, D), BF),
            dma((NU, 8)), dma((NU, 8)), dma((NU,)), dma((NU, 8)), dma((NU, 8)), dma((NU,)), dma((3,)), dma((3,)),
            dma((3, 4)), dma((3, 4)), dma((3,)), dma((3, 4)), dma((3, 4)), dma((8,)), dma((8,)), dma(()), dma(())]
        + UNIT_SCRATCH,
        compiler_params=pltpu.CompilerParams(has_side_effects=True, vmem_limit_bytes=62 * 1024 * 1024),
    )(xq, xk, xv, xd, rel, uw)


def solution(mesh):
    seq_spec = P(None, 'cp', None, None)

    def local(query, key_in, value, bias_u, bias_w, rel_k, d_out):
        chip = lax.axis_index('cp') // 2

        def by_head(arr):
            return arr.transpose(0, 2, 1, 3)

        rel = rel_k.transpose(1, 0, 2).reshape(12, NT, T, D)
        both = jnp.stack([bias_u, bias_w], axis=1).astype(F32)
        uw = lax.dynamic_slice_in_dim(both, 3 * chip, 3, 0)
        res = exchange_attend(by_head(query), by_head(key_in), by_head(value), by_head(d_out), rel, uw)
        d_rel = res[4].reshape(12, NT * T, D).transpose(1, 0, 2)
        duw = res[5].reshape(4, 2, 3, 8, D).sum(axis=1).reshape(12, 8, D)
        return tuple(by_head(arr) for arr in res[:4]) + (duw[:, 0], duw[:, 1], d_rel)

    return jax.shard_map(local, mesh=mesh,
                         in_specs=(seq_spec, seq_spec, seq_spec, P(), P(), P(), seq_spec),
                         out_specs=(seq_spec, seq_spec, seq_spec, seq_spec, P(), P(), P()),
                         check_vma=False)
```

time: 6030 us -> 377 us (0.06)
  waiting for transfers between devices: 3770 us -> 0 us
  starting transfers between devices: 853 us -> 0 us
  local copies, waits for them, and re-layouts: 737 us -> 23.9 us
  blocking collectives: 415 us -> 0 us
  Pallas kernels: 0 us -> 351 us
  matrix products: 113 us -> 0 us
    ppermute x44 -> x0, waiting for transfers between devices: 3750 us -> none  [the longest x28 2620 us: bwd_body(): lax.ppermute(travel, 'cp', shift_pairs)]
    ppermute x44 -> x0, starting transfers between devices: 853 us -> none  [the longest x28 507 us: bwd_body(): lax.ppermute(travel, 'cp', shift_pairs)]
    psum x1 -> x0, blocking collectives: 415 us -> none  [local(): d_bias_u = lax.psum(jnp.sum(dq_cont, axis=(0, 1)), 'cp')]
    pallas_call x0 -> x1, Pallas kernels: none -> 351 us  [exchange_attend(): pl.pallas_call(kernel, out_shape=(act, act, act, act, jax.ShapeDtypeStruc...]
    while x44 -> x0, local copies, waits for them, and re-layouts: 204 us -> none
    rev x2 -> x0, local copies, waits for them, and re-layouts: 185 us -> none  [the longest x1 94.9 us: local(): d_rel_k = lax.psum(jnp.flip(drk_rev[:rel_k.shape[0]], axis=0), 'cp')]
    reshape x6 -> x0, local copies, waits for them, and re-layouts: 150 us -> none  [the longest x2 60 us: skew_rel(): return flattened.reshape(lead_dims + (rows, 2 * rows - 1))[..., :rows]]
    dot_general x11 -> x0, matrix products: 113 us -> none  [the longest x2 29.6 us: block_logits(): jnp.einsum('bihd,chd->bhic', q_w, window, preferred_element_type=jnp.floa...]
  transfers between devices with their start and end apart: 45 -> 0, of which waited for: 29 -> 0; matrix products, arithmetic and copies ran while one was open for 1% -> 0% of each run, Pallas kernels for 0% -> 0%
where the time goes in v1:
time: 377 us
  Pallas kernels  351 us (93%)
  local copies, waits for them, and re-layouts  23.9 us (6%)
    pallas_call x1, Pallas kernels, exchange_attend(): pl.pallas_call(kernel, out_shape=(act, act, act, act, jax.ShapeDtypeStruc...  351 us
    unnamed x12, local copies, waits for them, and re-layouts  22.5 us

profile of v1, /device:TPU:0, one launch (start us, length us, event | category | flops | bytes accessed | tf_op | source)
XLA Modules:
  0.0 377.0 jit_solution(15054958069796918560)
XLA Ops:
  0.7 0.7 copy.14
  1.3 0.7 copy.15
  2.0 0.6 fusion.1.uw
  2.6 350.9 %shard_map.126 = (bf16[4,12,256,128]{3,2,1,0:T(8,128)(2,1)}, bf16[4,12,256,128]{3,2,1,0:T(8,128)(2,1)}, bf16[4,12,256,128]{3,2,1,0:T(8,128)(2,1)}, bf16[4,12,256...) custom-call(bf16[4,12,256,128]{3,2,1,0:T(8,128)(2,1)} %bitcast.25, ...), custom_call_target="tpu_custom_call" | custom-call | tf_op jit(solution)/shard_map/pallas_call | solution.py:253
  353.5 0.9 bitcast_reduce_fusion
  354.5 0.6 copy_bitcast_fusion
  355.1 0.0 copy-start.2
  355.1 4.1 %copy.25 = bf16[4,256,12,128]{3,1,2,0:T(8,128)(2,1)} copy(bf16[4,256,12,128]{3,1,2,0:T(8,128)(2,1)} %bitcast.32) | data formatting | bytes 6291456
  359.1 0.0 copy-done.2
  359.1 0.0 copy-start.1
  359.1 1.7 copy.26
  360.8 1.4 copy-done.1
  362.2 0.0 copy-start
  362.2 1.7 copy.27
  363.8 1.4 copy-done
  365.2 1.7 copy.28
  366.8 10.2 %copy.29 = f32[2048,12,128]{2,0,1:T(8,128)} copy(f32[2048,12,128]{2,0,1:T(8,128)} %bitcast.23) | data formatting | bytes 25165824
  (1 shorter events, 0.0 us)
Async XLA Ops:
  355.1 4.1 %copy-start.2 = (bf16[4,12,256,128]{3,2,1,0:T(8,128)(2,1)S(1)}, bf16[4,12,256,128]{3,2,1,0:T(8,128)(2,1)}, u32[]{:S(2)}) copy-start(bf16[4,12,256,128]{3,2,1,0:T(8,128)(2,1)} %get-tuple-element.14) | copy-start | bytes 9437188
  359.1 3.0 copy-start.1
  362.2 3.0 copy-start

commit v2 on v1

--- a/solution.py
+++ b/solution.py
@@ -10,6 +10,7 @@
 H = 128
 NT = 8
 NU = 6
+VMEM_LIMIT = 36 * 1024 * 1024
 F32 = jnp.float32
 BF = jnp.bfloat16
 MESH = pl.DeviceIdType.MESH
@@ -27,7 +28,7 @@
     return lax.dot_general(lhs, rhs, (((0,), (0,)), ((), ())), preferred_element_type=F32)
 
 
-def unit(x, rk, u, w, stage, drk, duw, scratch, after_tile):
+def unit(x, rk, u, w, drk, duw, scratch, after_tile):
     s_ref, dp_ref, r_ref, r_ref2, u_ref, dk_ref, dv_ref, a_ref, c_ref, oacc, qc_acc, qr_acc = scratch
     scale = D ** -0.5
     c2 = scale * 1.4426950408889634
@@ -43,8 +44,8 @@
     def tile(ii, _):
         i = NT - 1 - ii
         q = x[i, 0].astype(F32)
-        a_ref[...] = (q + u[...]).astype(BF)
-        c_ref[...] = (q + w[...]).astype(BF)
+        a_ref[...] = (q + u).astype(BF)
+        c_ref[...] = (q + w).astype(BF)
 
         def logits(n, mx):
             j = i - n
@@ -108,10 +109,10 @@
         qr = qr_acc[...]
         duw[0:1] += jnp.sum(qc, axis=0, keepdims=True)
         duw[1:2] += jnp.sum(qr, axis=0, keepdims=True)
-        stage[i, 0] = oacc[...].astype(BF)
-        stage[i, 1] = (qc + qr).astype(BF)
-        stage[i, 2] = dk_ref[i].astype(BF)
-        stage[i, 3] = dv_ref[i].astype(BF)
+        x[i, 0] = oacc[...].astype(BF)
+        x[i, 1] = (qc + qr).astype(BF)
+        x[i, 2] = dk_ref[i].astype(BF)
+        x[i, 3] = dv_ref[i].astype(BF)
         after_tile(i)
         return 0
 
@@ -124,9 +125,10 @@
     pltpu.VMEM((T, D), BF), pltpu.VMEM((T, D), F32), pltpu.VMEM((T, D), F32), pltpu.VMEM((T, D), F32)]
 
 
-def kernel(xq, xk, xv, xd, rel, uw, oq, odq, odk, odv, drk_out, duw_out, rin, stage, drk, pbuf, dfin, duw, rk,
-           in_send, in_recv, in_loc, out_send, out_recv, out_loc, half_send, half_recv,
-           fin_send, fin_recv, fin_loc, rel_send, rel_recv, duw_send, duw_recv, duw_loc, rk_sem, *scratch):
+def kernel(xq, xk, xv, xd, bias_u, bias_w, rel, oq, odq, odk, odv, drk_out, du_out, dw_out,
+           rin, drk, pbuf, duw, duw_all, rk, bu, bw,
+           in_send, in_recv, in_loc, out_send, out_recv, half_send, half_recv,
+           fin_send, fin_recv, hop_send, hop_recv, rel_send, rel_recv, duw_send, duw_recv, rk_sem, *scratch):
     me = lax.axis_index('cp')
     chip = me // 2
     core = me % 2
@@ -157,6 +159,8 @@
         for mask in (6, 2, 4, 7, 3, 5, 1):
             send_in(n, mask)
 
+    bu[...] = bias_u[...].astype(F32)
+    bw[...] = bias_w[...].astype(F32)
     drk[...] = jnp.zeros_like(drk)
     duw[...] = jnp.zeros_like(duw)
     rk_copy.wait()
@@ -165,14 +169,38 @@
         return remote(drk.at[k, pl.ds(4 * (1 - core), 4)], pbuf.at[k], half_send.at[k], half_recv.at[k],
                       jnp.bitwise_xor(me, 1))
 
-    def fin_copy(k, n, mask):
-        return remote(dfin.at[k], drk_out.at[3 * chip + k, pl.ds(4 * core, 4)], fin_send.at[k, n], fin_recv.at[k, n],
-                      jnp.bitwise_xor(me, mask))
-
-    def fin_own(k):
-        return pltpu.make_async_copy(dfin.at[k], drk_out.at[3 * chip + k, pl.ds(4 * core, 4)], fin_loc.at[k])
-
-    fin_masks = (1, 6, 2, 4)
+    def part(src_chip, k, lo, size):
+        return drk_out.at[3 * src_chip + k, pl.ds(4 * core + lo, size)]
+
+    def fin_copy(k, s):
+        mine = part(chip, k, 0, 4)
+        return remote(mine, mine, fin_send.at[k, s], fin_recv.at[k, s], jnp.bitwise_xor(me, (1, 2, 4)[s]))
+
+    def fin_arrived(k, s):
+        theirs = part(jnp.bitwise_xor(chip, s), k, 0, 4)
+        return remote(theirs, theirs, fin_send.at[k, s], fin_recv.at[k, s], jnp.bitwise_xor(me, (1, 2, 4)[s]))
+
+    def hop(k, s):
+        piece = part(jnp.bitwise_xor(chip, s), k, 2 * (s - 1), 2)
+        return remote(piece, piece, hop_send.at[k, s], hop_recv.at[k, s], jnp.bitwise_xor(me, (1, 4, 2)[s]))
+
+    def hop_arrived(k, s):
+        piece = part(jnp.bitwise_xor(chip, 3), k, 2 * (s - 1), 2)
+        return remote(piece, piece, hop_send.at[k, s], hop_recv.at[k, s], jnp.bitwise_xor(me, (1, 4, 2)[s]))
+
+    def relay(k, s):
+        piece = part(jnp.bitwise_xor(chip, s), k, 0, 4)
+        return remote(piece, piece, rel_send.at[k, s], rel_recv.at[k, s], jnp.bitwise_xor(me, 1))
+
+    def relay_arrived(k, s):
+        piece = drk_out.at[3 * jnp.bitwise_xor(chip, s) + k, pl.ds(4 * (1 - core), 4)]
+        return remote(piece, piece, rel_send.at[k, s], rel_recv.at[k, s], jnp.bitwise_xor(me, 1))
+
+    def pass_on(k):
+        for s in (1, 2):
+            fin_arrived(k, s).wait_recv()
+            hop(k, s).start()
+            relay(k, s).start()
 
     def run_unit(n, _):
         k = n // 2
@@ -186,103 +214,107 @@
             @pl.when(mask != 0)
             def _():
                 for a in range(4):
-                    remote(stage.at[n, i, a], spot(outs[a], me, n), out_send.at[n, i], out_recv.at[n, mask], i).start()
+                    remote(rin.at[n, i, a], spot(outs[a], me, n), out_send.at[n, i], out_recv.at[n, mask], i).start()
 
             @pl.when(mask == 0)
             def _():
                 for a in range(4):
-                    pltpu.make_async_copy(stage.at[n, i, a], spot(outs[a], me, n), out_loc.at[n]).start()
-
-        unit(rin.at[n], rk.at[k], uw.at[k, 0:1], uw.at[k, 1:2], stage.at[n], drk.at[k], duw.at[k], scratch, after_tile)
+                    spot(outs[a], me, n)[...] = rin[n, i, a]
+
+        head = pl.ds(3 * chip + k, 1)
+        unit(rin.at[n], rk.at[k], bu[head], bw[head], drk.at[k], duw.at[k], scratch, after_tile)
 
         @pl.when(n % 2 == 1)
         def _():
             copy = half_copy(k)
             copy.start()
             copy.wait()
-            dfin[k] = drk[k, pl.ds(4 * core, 4)] + pbuf[k]
-            for s, mask in enumerate(fin_masks):
-                fin_copy(k, s, mask).start()
-            fin_own(k).start()
+            part(chip, k, 0, 4)[...] = drk[k, pl.ds(4 * core, 4)] + pbuf[k]
+            for s in range(3):
+                fin_copy(k, s).start()
+
+        @pl.when((n % 2 == 1) & (n > 1))
+        def _():
+            pass_on(k - 1)
         return 0
 
     lax.fori_loop(0, NU, run_unit, 0)
 
-    def duw_copy(mask):
-        return remote(duw, duw_out.at[me], duw_send.at[mask], duw_recv.at[mask], jnp.bitwise_xor(me, mask))
+    def duw_copy(mask, arrived):
+        dev = jnp.bitwise_xor(me, mask)
+        return remote(duw, duw_all.at[dev if arrived else me], duw_send.at[mask], duw_recv.at[mask], dev)
 
     for mask in range(1, 8):
-        duw_copy(mask).start()
-    duw_own = pltpu.make_async_copy(duw, duw_out.at[me], duw_loc)
-    duw_own.start()
-
-    def relay(k, s):
-        part = drk_out.at[3 * jnp.bitwise_xor(chip, fin_masks[s] // 2) + k, pl.ds(4 * core, 4)]
-        return remote(part, part, rel_send.at[k, s], rel_recv.at[k, s], jnp.bitwise_xor(me, 1))
-
+        duw_copy(mask, False).start()
+    duw_all[me] = duw[...]
+
+    pass_on(2)
     for k in range(3):
-        for s in range(1, 4):
-            fin_copy(k, s, fin_masks[s]).wait_recv()
-            relay(k, s).start()
+        hop_arrived(k, 1).wait_recv()
+        hop_arrived(k, 2).wait_recv()
+        relay(k, 3).start()
+
+    for mask in range(1, 8):
+        duw_copy(mask, False).wait_send()
+        duw_copy(mask, True).wait_recv()
+    for h in range(12):
+        both = duw_all[2 * (h // 3), h % 3] + duw_all[2 * (h // 3) + 1, h % 3]
+        du_out[h:h + 1] = both[0:1]
+        dw_out[h:h + 1] = both[1:2]
 
     def finish(n, _):
         for mask in range(1, 8):
             dev = jnp.bitwise_xor(me, mask)
             in_wait(n, mask).wait_send()
-            remote(stage.at[n, dev], stage.at[n, dev], out_send.at[n, dev], out_recv.at[n, mask], dev).wait()
-        pltpu.make_async_copy(stage.at[n, me], stage.at[n, me], out_loc.at[n]).wait()
+            remote(rin.at[n, dev], rin.at[n, dev], out_send.at[n, dev], out_recv.at[n, mask], dev).wait()
         return 0
 
     lax.fori_loop(0, NU, finish, 0)
     for k in range(3):
-        fin_copy(k, 0, 1).wait()
-        fin_own(k).wait()
-        for s in range(1, 4):
-            fin_copy(k, s, fin_masks[s]).wait_send()
-            relay(k, s).wait()
-    for mask in range(1, 8):
-        duw_copy(mask).wait()
-    duw_own.wait()
-
-
-def exchange_attend(xq, xk, xv, xd, rel, uw):
+        fin_copy(k, 0).wait_send()
+        theirs = drk_out.at[3 * chip + k, pl.ds(4 * (1 - core), 4)]
+        remote(theirs, theirs, fin_send.at[k, 0], fin_recv.at[k, 0], jnp.bitwise_xor(me, 1)).wait_recv()
+        for s in (1, 2):
+            fin_copy(k, s).wait_send()
+            hop(k, s).wait_send()
+        for s in (1, 2, 3):
+            relay(k, s).wait_send()
+            relay_arrived(k, s).wait_recv()
+
+
+def exchange_attend(xq, xk, xv, xd, bias_u, bias_w, rel):
     any_spec = pl.BlockSpec(memory_space=pl.ANY)
     vmem_spec = pl.BlockSpec(memory_space=pltpu.VMEM)
     dma = pltpu.SemaphoreType.DMA
-    act = jax.ShapeDtypeStruct((4, 12, T, D), BF)
+    act = pltpu.VMEM((4, 12, T, D), BF)
+    bias = pltpu.VMEM((12, D), F32)
     return pl.pallas_call(
         kernel,
-        out_shape=(act, act, act, act, jax.ShapeDtypeStruct((12, NT, T, D), F32),
-                   jax.ShapeDtypeStruct((8, 3, 8, D), F32)),
-        in_specs=[any_spec] * 5 + [vmem_spec],
-        out_specs=(any_spec,) * 6,
+        out_shape=(act, act, act, act, pltpu.VMEM((12, NT, T, D), F32), bias, bias),
+        in_specs=[any_spec] * 4 + [vmem_spec] * 2 + [any_spec],
+        out_specs=(vmem_spec,) * 7,
         scratch_shapes=[
-            pltpu.VMEM((NU, 8, 4, T, D), BF), pltpu.VMEM((NU, NT, 4, T, D), BF), pltpu.VMEM((3, NT, T, D), F32),
-            pltpu.VMEM((3, 4, T, D), F32), pltpu.VMEM((3, 4, T, D), F32), pltpu.VMEM((3, 8, D), F32),
-            pltpu.VMEM((3, NT, T, D), BF),
-            dma((NU, 8)), dma((NU, 8)), dma((NU,)), dma((NU, 8)), dma((NU, 8)), dma((NU,)), dma((3,)), dma((3,)),
-            dma((3, 4)), dma((3, 4)), dma((3,)), dma((3, 4)), dma((3, 4)), dma((8,)), dma((8,)), dma(()), dma(())]
+            pltpu.VMEM((NU, 8, 4, T, D), BF), pltpu.VMEM((3, NT, T, D), F32),
+            pltpu.VMEM((3, 4, T, D), F32), pltpu.VMEM((3, 8, D), F32), pltpu.VMEM((8, 3, 8, D), F32),
+            pltpu.VMEM((3, NT, T, D), BF), pltpu.VMEM((12, D), F32), pltpu.VMEM((12, D), F32),
+            dma((NU, 8)), dma((NU, 8)), dma((NU,)), dma((NU, 8)), dma((NU, 8)), dma((3,)), dma((3,)),
+            dma((3, 3)), dma((3, 3)), dma((3, 3)), dma((3, 3)), dma((3, 4)), dma((3, 4)), dma((8,)), dma((8,)), dma(())]
         + UNIT_SCRATCH,
-        compiler_params=pltpu.CompilerParams(has_side_effects=True, vmem_limit_bytes=62 * 1024 * 1024),
-    )(xq, xk, xv, xd, rel, uw)
+        compiler_params=pltpu.CompilerParams(has_side_effects=True, vmem_limit_bytes=VMEM_LIMIT),
+    )(xq, xk, xv, xd, bias_u, bias_w, rel)
 
 
 def solution(mesh):
     seq_spec = P(None, 'cp', None, None)
 
     def local(query, key_in, value, bias_u, bias_w, rel_k, d_out):
-        chip = lax.axis_index('cp') // 2
-
         def by_head(arr):
             return arr.transpose(0, 2, 1, 3)
 
         rel = rel_k.transpose(1, 0, 2).reshape(12, NT, T, D)
-        both = jnp.stack([bias_u, bias_w], axis=1).astype(F32)
-        uw = lax.dynamic_slice_in_dim(both, 3 * chip, 3, 0)
-        res = exchange_attend(by_head(query), by_head(key_in), by_head(value), by_head(d_out), rel, uw)
+        res = exchange_attend(by_head(query), by_head(key_in), by_head(value), by_head(d_out), bias_u, bias_w, rel)
         d_rel = res[4].reshape(12, NT * T, D).transpose(1, 0, 2)
-        duw = res[5].reshape(4, 2, 3, 8, D).sum(axis=1).reshape(12, 8, D)
-        return tuple(by_head(arr) for arr in res[:4]) + (duw[:, 0], duw[:, 1], d_rel)
+        return tuple(by_head(arr) for arr in res[:4]) + (res[5], res[6], d_rel)
 
     return jax.shard_map(local, mesh=mesh,
                          in_specs=(seq_spec, seq_spec, seq_spec, P(), P(), P(), seq_spec),

time: 377 us -> 359 us (0.952)
  local copies, waits for them, and re-layouts: 23.9 us -> 12.6 us
  Pallas kernels: 351 us -> 345 us
    unnamed x12 -> x7, local copies, waits for them, and re-layouts: 22.5 us -> 12.6 us
    pallas_call x1, Pallas kernels: 351 us -> 345 us  [exchange_attend(): pl.pallas_call(kernel, out_shape=(act, act, act, act, pltpu.VMEM((12, NT,...]
where the time goes in v2:
time: 359 us
  Pallas kernels  345 us (96%)
  local copies, waits for them, and re-layouts  12.6 us (4%)
    pallas_call x1, Pallas kernels, exchange_attend(): pl.pallas_call(kernel, out_shape=(act, act, act, act, pltpu.VMEM((12, NT,...  345 us
    unnamed x7, local copies, waits for them, and re-layouts  12.6 us

profile of v2, /device:TPU:0, one launch (start us, length us, event | category | flops | bytes accessed | tf_op | source)
XLA Modules:
  0.0 358.8 jit_solution(8152556292418479024)
XLA Ops:
  0.6 345.5 %shard_map.126 = (bf16[4,12,256,128]{3,2,1,0:T(8,128)(2,1)S(1)}, bf16[4,12,256,128]{3,2,1,0:T(8,128)(2,1)S(1)}, bf16[4,12,256,128]{3,2,1,0:T(8,128)(2,1)S(1)}, b...) custom-call(bf16[4,12,256,128]{3,2,1,0:T(8,128)(2,1)} %bitcast.20, ...), custom_call_target="tpu_custom_call" | custom-call | tf_op jit(solution)/shard_map/pallas_call | solution.py:291
  346.1 1.7 copy.21
  347.8 1.7 copy.22
  349.5 0.6 copy.25
  350.1 0.6 copy.26
  350.7 1.7 copy.23
  352.3 1.7 copy.24
  354.0 4.8 %copy.27 = f32[2048,12,128]{2,0,1:T(8,128)} copy(f32[2048,12,128]{2,0,1:T(8,128)S(1)} %bitcast.14) | data formatting | bytes 25165824

commit v3 on v2

--- a/solution.py
+++ b/solution.py
@@ -24,109 +24,130 @@
     return lax.dot_general(lhs, rhs, (((1,), (0,)), ((), ())), preferred_element_type=F32)
 
 
-def dot_tn(lhs, rhs):
-    return lax.dot_general(lhs, rhs, (((0,), (0,)), ((), ())), preferred_element_type=F32)
-
-
-def unit(x, rk, u, w, drk, duw, scratch, after_tile):
-    s_ref, dp_ref, r_ref, r_ref2, u_ref, dk_ref, dv_ref, a_ref, c_ref, oacc, qc_acc, qr_acc = scratch
+def unit(x, rk, rkr, u, w, drk, duw, scratch, after_tile):
+    (s_ref, dp_ref, r_ref, mx_ref, l_ref, d_ref, u_ref, dk_ref, dv_ref, a_ref, c_ref, t_ref,
+     oacc, qc_acc, qr_acc) = scratch
+    nt = NT
     scale = D ** -0.5
     c2 = scale * 1.4426950408889634
     low = lax.broadcasted_iota(jnp.int32, (H, H), 1) <= lax.broadcasted_iota(jnp.int32, (H, H), 0)
     idx = (lax.broadcasted_iota(jnp.int32, (T, H), 0) - lax.broadcasted_iota(jnp.int32, (T, H), 1)) & (H - 1)
 
-    def gather(arr):
-        return jnp.take_along_axis(arr, idx, axis=1, mode="promise_in_bounds")
-
+    def gather(t):
+        return jnp.take_along_axis(t, idx, axis=1, mode="promise_in_bounds")
     dk_ref[...] = jnp.zeros_like(dk_ref)
     dv_ref[...] = jnp.zeros_like(dv_ref)
 
+
+    def prep(i, sl):
+        q = x[i, 0].astype(F32)
+        a_ref[sl] = (q + u).astype(BF)
+        c_ref[sl] = (q + w).astype(BF)
+        mx_ref[...] = jnp.full((T, H), -jnp.inf, F32)
+        r_ref[...] = jnp.full((2, T, H), -jnp.inf, F32)
+
+
+    def logits(i, sl, n):
+        j = i - n
+        by = dot_nt(c_ref[sl], rkr[n])
+        sc = dot_nt(a_ref[sl], x[j, 1])
+        dp_ref[sl, j] = dot_nt(x[i, 3], x[j, 2])
+        r0 = pltpu.roll(by[:, :H], 1, 1, stride=1, stride_axis=0)
+        r1 = pltpu.roll(by[:, H:], 1, 1, stride=1, stride_axis=0)
+        lo = sc[:, :H] + jnp.concatenate([jnp.where(low, r1[:H], r_ref[0, :H]), jnp.where(low, r0[H:], r1[H:])], 0)
+        hi = sc[:, H:] + jnp.concatenate([jnp.where(low, r_ref[0, :H], r_ref[1, :H]), jnp.where(low, r1[H:], r_ref[0, H:])], 0)
+        r_ref[0] = r0
+        r_ref[1] = r1
+        s_ref[sl, j, :, :H] = lo
+        s_ref[sl, j, :, H:] = hi
+        mx_ref[...] = jnp.maximum(mx_ref[...], jnp.maximum(lo, hi))
+
+
+    def softmax(i, sl):
+        m = jnp.max(mx_ref[...], axis=1, keepdims=True)
+        l_ref[...] = jnp.zeros_like(l_ref)
+        d_ref[...] = jnp.zeros_like(d_ref)
+        def body(j, _):
+            p = jnp.exp2((s_ref[sl, j] - m) * c2)
+            s_ref[sl, j] = p
+            pd = p * dp_ref[sl, j]
+            l_ref[...] += p[:, :H] + p[:, H:]
+            d_ref[...] += pd[:, :H] + pd[:, H:]
+            return 0
+        lax.fori_loop(0, i + 1, body, 0)
+        inv = 1.0 / jnp.sum(l_ref[...], axis=1, keepdims=True)
+        rd = jnp.sum(d_ref[...], axis=1, keepdims=True) * inv
+        return inv, rd
+
+
+    def grads(i, sl, j, inv, rd):
+        pn = s_ref[sl, j] * inv
+        pb = pn.astype(BF)
+        ds = pn * (dp_ref[sl, j] - rd) * scale
+        dsb = ds.astype(BF)
+        oacc[...] += dot_nn(pb, x[j, 2])
+        dv_ref[j] += dot_nn(t_ref[0], pb)
+        qc_acc[...] += dot_nn(dsb, x[j, 1])
+        dk_ref[j] += dot_nn(t_ref[1], dsb)
+        g0 = gather(ds[:, :H])
+        g1 = gather(ds[:, H:])
+        d0 = jnp.concatenate([jnp.where(low, g0[:H], u_ref[1, :H]), jnp.where(low, g1[H:], g0[H:])], 0)
+        d1 = jnp.concatenate([jnp.where(low, u_ref[1, :H], u_ref[0, :H]), jnp.where(low, g0[H:], u_ref[1, H:])], 0)
+        dist = jnp.concatenate([d0, d1], 1).astype(BF)
+        u_ref[0] = g0
+        u_ref[1] = g1
+        qr_acc[...] += dot_nn(dist, rk[i - j])
+        drk[i - j] += dot_nn(t_ref[2], dist)
+
+    prep(nt - 1, (nt - 1) % 2)
+
+    def first(n, _):
+        logits(nt - 1, (nt - 1) % 2, n)
+        return 0
+    lax.fori_loop(0, nt, first, 0)
+
+
     def tile(ii, _):
-        i = NT - 1 - ii
-        q = x[i, 0].astype(F32)
-        a_ref[...] = (q + u).astype(BF)
-        c_ref[...] = (q + w).astype(BF)
-
-        def logits(n, mx):
-            j = i - n
-            by = dot_nt(c_ref[...], rk[n])
-            s = dot_nt(a_ref[...], x[j, 1])
-            n0 = gather(by[:, :H])
-            n1 = gather(by[:, H:])
-            p0 = jnp.where(n == 0, -jnp.inf, r_ref2[...])
-            p1 = jnp.where(n == 0, -jnp.inf, r_ref[...])
-            lo = jnp.concatenate([jnp.where(low, n0[:H], p1[:H]), jnp.where(low, n1[H:], n0[H:])], 0)
-            hi = jnp.concatenate([jnp.where(low, p1[:H], p0), jnp.where(low, n0[H:], p1[H:])], 0)
-            s = s + jnp.concatenate([lo, hi], 1)
-            r_ref[...] = n1
-            r_ref2[...] = n0[:H]
-            s_ref[j] = s
-            return jnp.maximum(mx, jnp.maximum(s[:, :H], s[:, H:]))
-
-        mx = lax.fori_loop(0, i + 1, logits, jnp.full((T, H), -jnp.inf, F32))
-        m = jnp.max(mx, axis=1, keepdims=True)
-
-        def weights(j, carry):
-            total, dots = carry
-            p = jnp.exp2((s_ref[j] - m) * c2)
-            dp = dot_nt(x[i, 3], x[j, 2])
-            s_ref[j] = p
-            dp_ref[j] = dp
-            pd = p * dp
-            return total + (p[:, :H] + p[:, H:]), dots + (pd[:, :H] + pd[:, H:])
-
-        zero = jnp.zeros((T, H), F32)
-        total, dots = lax.fori_loop(0, i + 1, weights, (zero, zero))
-        inv = 1.0 / jnp.sum(total, axis=1, keepdims=True)
-        row_dot = jnp.sum(dots, axis=1, keepdims=True) * inv
-        oacc[...] = zero
-        qc_acc[...] = zero
-        qr_acc[...] = zero
+        i = nt - 1 - ii
+        sl = i % 2
+        inv, rd = softmax(i, sl)
+        nxt = jnp.maximum(i - 1, 0)
+        t_ref[0] = x[i, 3].T
+        t_ref[1] = a_ref[sl].T
+        t_ref[2] = c_ref[sl].T
+        oacc[...] = jnp.zeros_like(oacc)
+        qc_acc[...] = jnp.zeros_like(qc_acc)
+        qr_acc[...] = jnp.zeros_like(qr_acc)
         u_ref[...] = jnp.zeros_like(u_ref)
-
-        def grads(j, _):
-            pn = s_ref[j] * inv
-            pb = pn.astype(BF)
-            ds = pn * (dp_ref[j] - row_dot) * scale
-            dsb = ds.astype(BF)
-            oacc[...] += dot_nn(pb, x[j, 2])
-            dv_ref[j] += dot_tn(pb, x[i, 3])
-            qc_acc[...] += dot_nn(dsb, x[j, 1])
-            dk_ref[j] += dot_tn(dsb, a_ref[...])
-            g0 = gather(ds[:, :H])
-            g1 = gather(ds[:, H:])
-            d0 = jnp.concatenate([jnp.where(low, g0[:H], u_ref[1, :H]), jnp.where(low, g1[H:], g0[H:])], 0)
-            d1 = jnp.concatenate([jnp.where(low, u_ref[1, :H], u_ref[0, :H]), jnp.where(low, g0[H:], u_ref[1, H:])], 0)
-            dist = jnp.concatenate([d0, d1], 1).astype(BF)
-            u_ref[0] = g0
-            u_ref[1] = g1
-            qr_acc[...] += dot_nn(dist, rk[i - j])
-            drk[i - j] += dot_tn(dist, c_ref[...])
+        prep(nxt, 1 - sl)
+        def both(n, _):
+            grads(i, sl, n, inv, rd)
+            logits(nxt, 1 - sl, n)
             return 0
-
-        lax.fori_loop(0, i + 1, grads, 0)
+        lax.fori_loop(0, i, both, 0)
+        grads(i, sl, i, inv, rd)
         qc = qc_acc[...]
         qr = qr_acc[...]
         duw[0:1] += jnp.sum(qc, axis=0, keepdims=True)
         duw[1:2] += jnp.sum(qr, axis=0, keepdims=True)
         x[i, 0] = oacc[...].astype(BF)
         x[i, 1] = (qc + qr).astype(BF)
-        x[i, 2] = dk_ref[i].astype(BF)
-        x[i, 3] = dv_ref[i].astype(BF)
+        x[i, 2] = dk_ref[i].T.astype(BF)
+        x[i, 3] = dv_ref[i].T.astype(BF)
         after_tile(i)
         return 0
-
-    lax.fori_loop(0, NT, tile, 0)
+    lax.fori_loop(0, nt, tile, 0)
 
 
 UNIT_SCRATCH = [
-    pltpu.VMEM((NT, T, T), F32), pltpu.VMEM((NT, T, T), F32), pltpu.VMEM((T, H), F32), pltpu.VMEM((H, H), F32),
-    pltpu.VMEM((2, T, H), F32), pltpu.VMEM((NT, T, D), F32), pltpu.VMEM((NT, T, D), F32), pltpu.VMEM((T, D), BF),
-    pltpu.VMEM((T, D), BF), pltpu.VMEM((T, D), F32), pltpu.VMEM((T, D), F32), pltpu.VMEM((T, D), F32)]
+    pltpu.VMEM((2, NT, T, T), F32), pltpu.VMEM((2, NT, T, T), F32), pltpu.VMEM((2, T, H), F32), pltpu.VMEM((T, H), F32),
+    pltpu.VMEM((T, H), F32), pltpu.VMEM((T, H), F32), pltpu.VMEM((2, T, H), F32), pltpu.VMEM((NT, D, T), F32),
+    pltpu.VMEM((NT, D, T), F32), pltpu.VMEM((2, T, D), BF), pltpu.VMEM((2, T, D), BF), pltpu.VMEM((3, D, T), BF),
+    pltpu.VMEM((T, D), F32), pltpu.VMEM((T, D), F32), pltpu.VMEM((T, D), F32)]
 
 
 def kernel(xq, xk, xv, xd, bias_u, bias_w, rel, oq, odq, odk, odv, drk_out, du_out, dw_out,
-           rin, drk, pbuf, duw, duw_all, rk, bu, bw,
+           rin, drk, pbuf, duw, duw_all, rk, rkr, bu, bw,
            in_send, in_recv, in_loc, out_send, out_recv, half_send, half_recv,
            fin_send, fin_recv, hop_send, hop_recv, rel_send, rel_recv, duw_send, duw_recv, rk_sem, *scratch):
     me = lax.axis_index('cp')
@@ -164,6 +185,10 @@
     drk[...] = jnp.zeros_like(drk)
     duw[...] = jnp.zeros_like(duw)
     rk_copy.wait()
+    flip = (lax.broadcasted_iota(jnp.int32, (T, T), 0) + lax.broadcasted_iota(jnp.int32, (T, T), 1) == T - 1).astype(BF)
+    for k in range(3):
+        for n in range(NT):
+            rkr[k, n] = dot_nn(flip, rk[k, n]).astype(BF)
 
     def half_copy(k):
         return remote(drk.at[k, pl.ds(4 * (1 - core), 4)], pbuf.at[k], half_send.at[k], half_recv.at[k],
@@ -222,14 +247,15 @@
                     spot(outs[a], me, n)[...] = rin[n, i, a]
 
         head = pl.ds(3 * chip + k, 1)
-        unit(rin.at[n], rk.at[k], bu[head], bw[head], drk.at[k], duw.at[k], scratch, after_tile)
+        unit(rin.at[n], rk.at[k], rkr.at[k], bu[head], bw[head], drk.at[k], duw.at[k], scratch, after_tile)
 
         @pl.when(n % 2 == 1)
         def _():
             copy = half_copy(k)
             copy.start()
             copy.wait()
-            part(chip, k, 0, 4)[...] = drk[k, pl.ds(4 * core, 4)] + pbuf[k]
+            for r in range(4):
+                part(chip, k, r, 1)[0] = (drk[k, 4 * core + r] + pbuf[k, r]).T
             for s in range(3):
                 fin_copy(k, s).start()
 
@@ -294,9 +320,9 @@
         in_specs=[any_spec] * 4 + [vmem_spec] * 2 + [any_spec],
         out_specs=(vmem_spec,) * 7,
         scratch_shapes=[
-            pltpu.VMEM((NU, 8, 4, T, D), BF), pltpu.VMEM((3, NT, T, D), F32),
-            pltpu.VMEM((3, 4, T, D), F32), pltpu.VMEM((3, 8, D), F32), pltpu.VMEM((8, 3, 8, D), F32),
-            pltpu.VMEM((3, NT, T, D), BF), pltpu.VMEM((12, D), F32), pltpu.VMEM((12, D), F32),
+            pltpu.VMEM((NU, 8, 4, T, D), BF), pltpu.VMEM((3, NT, D, T), F32),
+            pltpu.VMEM((3, 4, D, T), F32), pltpu.VMEM((3, 8, D), F32), pltpu.VMEM((8, 3, 8, D), F32),
+            pltpu.VMEM((3, NT, T, D), BF), pltpu.VMEM((3, NT, T, D), BF), pltpu.VMEM((12, D), F32), pltpu.VMEM((12, D), F32),
             dma((NU, 8)), dma((NU, 8)), dma((NU,)), dma((NU, 8)), dma((NU, 8)), dma((3,)), dma((3,)),
             dma((3, 3)), dma((3, 3)), dma((3, 3)), dma((3, 3)), dma((3, 4)), dma((3, 4)), dma((8,)), dma((8,)), dma(())]
         + UNIT_SCRATCH,

time: 359 us -> 347 us (0.967)
  Pallas kernels: 345 us -> 334 us
    pallas_call x1, Pallas kernels: 345 us -> 334 us  [exchange_attend(): pl.pallas_call(kernel, out_shape=(act, act, act, act, pltpu.VMEM((12, NT,...]
where the time goes in v3:
time: 347 us
  Pallas kernels  334 us (96%)
  local copies, waits for them, and re-layouts  12.6 us (4%)
    pallas_call x1, Pallas kernels, exchange_attend(): pl.pallas_call(kernel, out_shape=(act, act, act, act, pltpu.VMEM((12, NT,...  334 us
    unnamed x7, local copies, waits for them, and re-layouts  12.6 us

profile of v3, /device:TPU:0, one launch (start us, length us, event | category | flops | bytes accessed | tf_op | source)
XLA Modules:
  0.0 347.0 jit_solution(15150596809316764019)
XLA Ops:
  0.6 333.7 %shard_map.126 = (bf16[4,12,256,128]{3,2,1,0:T(8,128)(2,1)S(1)}, bf16[4,12,256,128]{3,2,1,0:T(8,128)(2,1)S(1)}, bf16[4,12,256,128]{3,2,1,0:T(8,128)(2,1)S(1)}, b...) custom-call(bf16[4,12,256,128]{3,2,1,0:T(8,128)(2,1)} %bitcast.20, ...), custom_call_target="tpu_custom_call" | custom-call | tf_op jit(solution)/shard_map/pallas_call | solution.py:317
  334.4 1.7 copy.21
  336.0 1.7 copy.22
  337.7 0.6 copy.25
  338.3 0.6 copy.26
  338.9 1.7 copy.23
  340.6 1.7 copy.24
  342.2 4.8 %copy.27 = f32[2048,12,128]{2,0,1:T(8,128)} copy(f32[2048,12,128]{2,0,1:T(8,128)S(1)} %bitcast.14) | data formatting | bytes 25165824

commit v4 on v3

--- a/solution.py
+++ b/solution.py
@@ -330,6 +330,27 @@
     )(xq, xk, xv, xd, bias_u, bias_w, rel)
 
 
+def write_kernel(*refs):
+    half = len(refs) // 2
+    sem = refs[-1]
+    copies = [pltpu.make_async_copy(refs[n], refs[half + n], sem.at[n]) for n in range(half)]
+    for copy in copies:
+        copy.start()
+    for copy in copies:
+        copy.wait()
+
+
+def write_out(arrs):
+    return pl.pallas_call(
+        write_kernel,
+        out_shape=tuple(jax.ShapeDtypeStruct(arr.shape, arr.dtype) for arr in arrs),
+        in_specs=[pl.BlockSpec(memory_space=pltpu.VMEM)] * len(arrs),
+        out_specs=(pl.BlockSpec(memory_space=pl.ANY),) * len(arrs),
+        scratch_shapes=[pltpu.SemaphoreType.DMA((len(arrs),))],
+        compiler_params=pltpu.CompilerParams(vmem_limit_bytes=1024 * 1024),
+    )(*[pltpu.with_memory_space_constraint(arr, pltpu.VMEM) for arr in arrs])
+
+
 def solution(mesh):
     seq_spec = P(None, 'cp', None, None)
 
@@ -339,6 +360,7 @@
 
         rel = rel_k.transpose(1, 0, 2).reshape(12, NT, T, D)
         res = exchange_attend(by_head(query), by_head(key_in), by_head(value), by_head(d_out), bias_u, bias_w, rel)
+        res = write_out(res)
         d_rel = res[4].reshape(12, NT * T, D).transpose(1, 0, 2)
         return tuple(by_head(arr) for arr in res[:4]) + (res[5], res[6], d_rel)
 

time: 347 us -> 343 us (0.988)
  local copies, waits for them, and re-layouts: 12.6 us -> 0 us
  Pallas kernels: 334 us -> 343 us
    unnamed x7 -> x0, local copies, waits for them, and re-layouts: 12.6 us -> none
    pallas_call x0 -> x1, Pallas kernels: none -> 8.81 us  [write_out(): pl.pallas_call(write_kernel, out_shape=tuple((jax.ShapeDtypeStruct(arr.sh...]
where the time goes in v4:
time: 343 us
  Pallas kernels  343 us (100%)
    pallas_call x1, Pallas kernels, exchange_attend(): pl.pallas_call(kernel, out_shape=(act, act, act, act, pltpu.VMEM((12, NT,...  334 us
    pallas_call x1, Pallas kernels, write_out(): pl.pallas_call(write_kernel, out_shape=tuple((jax.ShapeDtypeStruct(arr.sh...  8.81 us

profile of v4, /device:TPU:0, one launch (start us, length us, event | category | flops | bytes accessed | tf_op | source)
XLA Modules:
  0.0 343.2 jit_solution(9841184462619638183)
XLA Ops:
  0.6 333.7 %shard_map.126 = (bf16[4,12,256,128]{3,2,1,0:T(8,128)(2,1)S(1)}, bf16[4,12,256,128]{3,2,1,0:T(8,128)(2,1)S(1)}, bf16[4,12,256,128]{3,2,1,0:T(8,128)(2,1)S(1)}, b...) custom-call(bf16[4,12,256,128]{3,2,1,0:T(8,128)(2,1)} %bitcast.15, ...), custom_call_target="tpu_custom_call" | custom-call | tf_op jit(solution)/shard_map/pallas_call | solution.py:317
  334.4 8.8 %shard_map.127 = (bf16[4,12,256,128]{3,2,1,0:T(8,128)(2,1)}, bf16[4,12,256,128]{3,2,1,0:T(8,128)(2,1)}, bf16[4,12,256,128]{3,2,1,0:T(8,128)(2,1)}, bf16[4,12,256...) custom-call(bf16[4,12,256,128]{3,2,1,0:T(8,128)(2,1)S(1)} %get-tuple-element.21.refs_, ...), custom_call_target="tpu_custom_call" | custom-call | tf_op jit(solution)/shard_map/pallas_call | solution.py:344

commit v5 on v4

v5 whole, which is shorter than its diff:
```python
import jax
import jax.numpy as jnp
from jax import lax
from jax.experimental import pallas as pl
from jax.experimental.pallas import tpu as pltpu
from jax.sharding import PartitionSpec as P

T = 256
D = 128
H = 128
NT = 8
NU = 6
EARLY = 6
HOLD = 4
VMEM_LIMIT = 38 * 1024 * 1024
F32 = jnp.float32
BF = jnp.bfloat16
SCALE = D ** -0.5
C2 = SCALE * 1.4426950408889634
MESH = pl.DeviceIdType.MESH


def dot_nt(lhs, rhs):
    return lax.dot_general(lhs, rhs, (((1,), (1,)), ((), ())), preferred_element_type=F32)


def row_max(arr):
    return jnp.max(arr, axis=1, keepdims=True)


def row_sum(arr):
    return jnp.sum(arr, axis=1, keepdims=True)


def dot_nn(lhs, rhs):
    return lax.dot_general(lhs, rhs, (((1,), (0,)), ((), ())), preferred_element_type=F32)


def unit(x, rk, rkr, u, w, drk, duw, scratch, after_softmax, after_tile):
    (s_ref, dp_ref, r_ref, mx_ref, l_ref, d_ref, u_ref, dk_ref, dv_ref, a_ref, c_ref, t_ref,
     oacc, qc_acc, qr_acc) = scratch
    nt = NT
    low = lower_mask()
    gather = gather_fn()
    dk_ref[:] = jnp.zeros_like(dk_ref)
    dv_ref[:] = jnp.zeros_like(dv_ref)


    def prep(i, sl):
        q = x[i, 0].astype(F32)
        a_ref[sl] = (q + u).astype(BF)
        c_ref[sl] = (q + w).astype(BF)
        mx_ref[:] = jnp.full((T, H), -jnp.inf, F32)
        r_ref[:] = jnp.full((2, T, H), -jnp.inf, F32)


    def logits(i, sl, n):
        j = i - n
        by = dot_nt(c_ref[sl], rkr[n])
        sc = dot_nt(a_ref[sl], x[j, 1])
        dp_ref[sl, j] = dot_nt(x[i, 3], x[j, 2])
        r0 = pltpu.roll(by[:, :H], 1, 1, stride=1, stride_axis=0)
        r1 = pltpu.roll(by[:, H:], 1, 1, stride=1, stride_axis=0)
        sc += shifted(low, r1, r0, r_ref[1], r_ref[0])
        r_ref[0] = r0
        r_ref[1] = r1
        s_ref[sl, j] = sc
        mx_ref[:] = jnp.maximum(mx_ref[:], jnp.maximum(sc[:, :H], sc[:, H:]))


    def softmax(i, sl):
        m = row_max(mx_ref[:])
        l_ref[:] = jnp.zeros_like(l_ref)
        d_ref[:] = jnp.zeros_like(d_ref)
        def body(j, _):
            p = jnp.exp2((s_ref[sl, j] - m) * C2)
            s_ref[sl, j] = p
            pd = p * dp_ref[sl, j]
            l_ref[:] += p[:, :H] + p[:, H:]
            d_ref[:] += pd[:, :H] + pd[:, H:]
            return 0
        lax.fori_loop(0, i + 1, body, 0)
        inv = 1.0 / row_sum(l_ref[:])
        rd = row_sum(d_ref[:]) * inv
        after_softmax(i, m, inv, rd)
        return inv, rd


    def grads(i, sl, j, inv, rd):
        pn = s_ref[sl, j] * inv
        pb = pn.astype(BF)
        ds = pn * (dp_ref[sl, j] - rd) * SCALE
        dsb = ds.astype(BF)
        oacc[:] += dot_nn(pb, x[j, 2])
        dv_ref[j] += dot_nn(t_ref[0], pb)
        qc_acc[:] += dot_nn(dsb, x[j, 1])
        dk_ref[j] += dot_nn(t_ref[1], dsb)
        g0 = gather(ds[:, :H])
        g1 = gather(ds[:, H:])
        dist = shifted(low, g0, g1, u_ref[0], u_ref[1]).astype(BF)
        u_ref[0] = g0
        u_ref[1] = g1
        qr_acc[:] += dot_nn(dist, rk[i - j])
        drk[i - j] += dot_nn(t_ref[2], dist)

    prep(nt - 1, (nt - 1) % 2)

    def first(n, _):
        logits(nt - 1, (nt - 1) % 2, n)
        return 0
    lax.fori_loop(0, nt, first, 0)


    def tile(ii, _):
        i = nt - 1 - ii
        sl = i % 2
        inv, rd = softmax(i, sl)
        nxt = jnp.maximum(i - 1, 0)
        t_ref[0] = x[i, 3].T
        t_ref[1] = a_ref[sl].T
        t_ref[2] = c_ref[sl].T
        oacc[:] = jnp.zeros_like(oacc)
        qc_acc[:] = jnp.zeros_like(qc_acc)
        qr_acc[:] = jnp.zeros_like(qr_acc)
        u_ref[:] = jnp.zeros_like(u_ref)
        prep(nxt, 1 - sl)
        def both(n, _):
            grads(i, sl, n, inv, rd)
            logits(nxt, 1 - sl, n)
            return 0
        lax.fori_loop(0, i, both, 0)
        grads(i, sl, i, inv, rd)
        qc = qc_acc[:]
        qr = qr_acc[:]
        duw[0:1] += jnp.sum(qc, axis=0, keepdims=True)
        duw[1:2] += jnp.sum(qr, axis=0, keepdims=True)
        x[i, 0] = oacc[:].astype(BF)
        x[i, 1] = (qc + qr).astype(BF)
        x[i, 2] = dk_ref[i].T.astype(BF)
        x[i, 3] = dv_ref[i].T.astype(BF)
        after_tile(i)
        return 0
    lax.fori_loop(0, nt, tile, 0)


def gather_fn():
    idx = (lax.broadcasted_iota(jnp.int32, (T, H), 0) - lax.broadcasted_iota(jnp.int32, (T, H), 1)) & (H - 1)
    return lambda arr: jnp.take_along_axis(arr, idx, axis=1, mode="promise_in_bounds")


def lower_mask():
    return lax.broadcasted_iota(jnp.int32, (H, H), 1) <= lax.broadcasted_iota(jnp.int32, (H, H), 0)


def shifted(low, n0, n1, p0, p1):
    lo = jnp.concatenate([jnp.where(low, n0[:H], p1[:H]), jnp.where(low, n1[H:], n0[H:])], 0)
    hi = jnp.concatenate([jnp.where(low, p1[:H], p0[:H]), jnp.where(low, n0[H:], p1[H:])], 0)
    return jnp.concatenate([lo, hi], 1)


def block_scores(q, key, rk, u, w, gather, low):
    qf = jnp.concatenate([q[0].astype(F32), q[1].astype(F32)], 0)
    a = (qf + u).astype(BF)
    c = (qf + w).astype(BF)
    by0 = dot_nt(c, rk[0])
    by1 = dot_nt(c[T:], rk[1])
    s0 = dot_nt(a, key[0])
    s11 = dot_nt(a[T:], key[1])
    g00, g01 = gather(by0[:T, :H]), gather(by0[:T, H:])
    g10, g11 = gather(by0[T:, :H]), gather(by0[T:, H:])
    h10, h11 = gather(by1[:, :H]), gather(by1[:, H:])
    none = jnp.full((T, H), -jnp.inf, F32)
    s00 = s0[:T] + shifted(low, g00, g01, none, none)
    s11 = s11 + shifted(low, g10, g11, none, none)
    s10 = s0[T:] + shifted(low, h10, h11, g10, g11)
    return a, c, s00, s10, s11


def row_block(q, d_out, key, val, rk, u, w, outs, d_qs):
    low = lower_mask()
    gather = gather_fn()
    a, c, s00, s10, s11 = block_scores(q, key, rk, u, w, gather, low)
    dob = jnp.concatenate([d_out[0], d_out[1]], 0)
    dp0 = dot_nt(dob, val[0])
    dp11 = dot_nt(d_out[1], val[1])
    m0 = row_max(s00)
    m1 = row_max(jnp.maximum(s10, s11))
    p00 = jnp.exp2((s00 - m0) * C2)
    p10 = jnp.exp2((s10 - m1) * C2)
    p11 = jnp.exp2((s11 - m1) * C2)
    i0 = 1.0 / row_sum(p00)
    i1 = 1.0 / row_sum(p10 + p11)
    r0 = row_sum(p00 * dp0[:T]) * i0
    r1 = row_sum(p10 * dp0[T:] + p11 * dp11) * i1
    p00 *= i0
    p10 *= i1
    p11 *= i1
    d00 = p00 * (dp0[:T] - r0) * SCALE
    d10 = p10 * (dp0[T:] - r1) * SCALE
    d11 = p11 * (dp11 - r1) * SCALE
    o = dot_nn(jnp.concatenate([p00, p10], 0).astype(BF), val[0])
    o1 = o[T:] + dot_nn(p11.astype(BF), val[1])
    outs[0][:] = o[:T].astype(BF)
    outs[1][:] = o1.astype(BF)
    dq = dot_nn(jnp.concatenate([d00, d10], 0).astype(BF), key[0])
    dq1 = dot_nn(d11.astype(BF), key[1])
    zero = jnp.zeros((T, H), F32)
    a0, a1 = gather(d00[:, :H]), gather(d00[:, H:])
    b0, b1 = gather(d10[:, :H]), gather(d10[:, H:])
    e0, e1 = gather(d11[:, :H]), gather(d11[:, H:])
    t00 = shifted(low, a0, a1, zero, zero)
    t11 = shifted(low, b0, b1, zero, zero)
    t10 = shifted(low, e0, e1, b0, b1)
    dr = dot_nn(jnp.concatenate([t00, t10], 0).astype(BF), rk[0])
    dr1 = dot_nn(t11.astype(BF), rk[1])
    d_qs[0][:] = (dq[:T] + dr[:T]).astype(BF)
    d_qs[1][:] = (dq[T:] + dq1 + dr[T:] + dr1).astype(BF)


def col_block(q, d_out, key, val, rk, stats, u, w, d_ks, d_vs):
    low = lower_mask()
    gather = gather_fn()
    a, c, s00, s10, s11 = block_scores(q, key, rk, u, w, gather, low)
    dob = jnp.concatenate([d_out[0], d_out[1]], 0)
    dp0 = dot_nt(dob, val[0])
    dp11 = dot_nt(d_out[1], val[1])
    z = jnp.zeros((H - 8, T), F32)
    t0 = jnp.concatenate([stats[0], z], 0).T
    t1 = jnp.concatenate([stats[1], z], 0).T
    p00 = jnp.exp2((s00 - t0[:, 0:1]) * C2) * t0[:, 1:2]
    p10 = jnp.exp2((s10 - t1[:, 0:1]) * C2) * t1[:, 1:2]
    p11 = jnp.exp2((s11 - t1[:, 0:1]) * C2) * t1[:, 1:2]
    d00 = p00 * (dp0[:T] - t0[:, 2:3]) * SCALE
    d10 = p10 * (dp0[T:] - t1[:, 2:3]) * SCALE
    d11 = p11 * (dp11 - t1[:, 2:3]) * SCALE
    at = a.T
    dot = dob.T
    dv0 = dot_nn(dot, jnp.concatenate([p00, p10], 0).astype(BF))
    dk0 = dot_nn(at, jnp.concatenate([d00, d10], 0).astype(BF))
    dv1 = dot_nn(dot[:, T:], p11.astype(BF))
    dk1 = dot_nn(at[:, T:], d11.astype(BF))
    d_ks[0][:] = dk0.T.astype(BF)
    d_vs[0][:] = dv0.T.astype(BF)
    d_ks[1][:] = dk1.T.astype(BF)
    d_vs[1][:] = dv1.T.astype(BF)


UNIT_SCRATCH = [
    pltpu.VMEM((2, NT, T, T), F32), pltpu.VMEM((2, NT, T, T), F32), pltpu.VMEM((2, T, H), F32), pltpu.VMEM((T, H), F32),
    pltpu.VMEM((T, H), F32), pltpu.VMEM((T, H), F32), pltpu.VMEM((2, T, H), F32), pltpu.VMEM((NT, D, T), F32),
    pltpu.VMEM((NT, D, T), F32), pltpu.VMEM((2, T, D), BF), pltpu.VMEM((2, T, D), BF), pltpu.VMEM((3, D, T), BF),
    pltpu.VMEM((T, D), F32), pltpu.VMEM((T, D), F32), pltpu.VMEM((T, D), F32)]


def kernel(xq, xk, xv, xd, bias_u, bias_w, rel, oq, odq, odk, odv, drk_out, du_out, dw_out, lx,
           rin, drk, pbuf, duw, duw_all, rk, rkr, bu, bw, lblk, lrk, lres, st_out, st_in,
           in_send, in_recv, in_loc, out_send, out_recv, half_send, half_recv,
           fin_send, fin_recv, hop_send, hop_recv, rel_send, rel_recv, duw_send, duw_recv, rk_sem, px_send, px_recv,
           st_send, st_recv, l_sem, lr_send, lr_recv, *scratch):
    me = lax.axis_index('cp')
    chip = me // 2
    core = me % 2
    ins = (xq, xk, xv, xd)
    outs = (oq, odq, odk, odv)

    def remote(src, dst, ssem, rsem, dev):
        return pltpu.make_async_remote_copy(src_ref=src, dst_ref=dst, send_sem=ssem, recv_sem=rsem,
                                            device_id=(dev,), device_id_type=MESH)

    def spot(arr, dev, n):
        return arr.at[2 * (dev % 2) + n % 2, 3 * (dev // 2) + n // 2]

    def send_in(n, mask):
        dev = jnp.bitwise_xor(me, mask)
        for a in range(4):
            remote(spot(ins[a], dev, n), rin.at[n, me, a], in_send.at[n, mask], in_recv.at[n, mask], dev).start()

    def in_wait(n, mask):
        dev = jnp.bitwise_xor(me, mask)
        return remote(rin.at[n, dev], rin.at[n, dev], in_send.at[n, mask], in_recv.at[n, mask], dev)

    rk_copy = pltpu.make_async_copy(rel.at[pl.ds(3 * chip, 3)], rk, rk_sem)
    rk_copy.start()
    rows_here = chip == 0
    cols_here = chip == 3
    partner = jnp.bitwise_xor(me, 1)

    def pair_copies(low_end):
        heads = pl.ds(3 if low_end else 0, 9)
        return [remote(ins[a].at[pl.ds(2 * (1 - core), 2), heads], lx.at[a, :, heads], px_send.at[a], px_recv.at[a], partner)
                for a in range(4)]

    def pair(act):
        for low_end in (True, False):
            @pl.when(rows_here if low_end else cols_here)
            def _():
                for copy in pair_copies(low_end):
                    getattr(copy, act)()

    for n in range(NU):
        for a in range(4):
            pltpu.make_async_copy(spot(ins[a], me, n), rin.at[n, me, a], in_loc.at[n]).start()
        for mask in (6, 2, 4, 7, 3, 5, 1):
            send_in(n, mask)
        if n == 0:
            pair("start")

    bu[:] = bias_u[:].astype(F32)
    bw[:] = bias_w[:].astype(F32)
    drk[:] = jnp.zeros_like(drk)
    duw[:] = jnp.zeros_like(duw)
    rk_copy.wait()
    flip = (lax.broadcasted_iota(jnp.int32, (T, T), 0) + lax.broadcasted_iota(jnp.int32, (T, T), 1) == T - 1).astype(BF)
    for k in range(3):
        for n in range(NT):
            rkr[k, n] = dot_nn(flip, rk[k, n]).astype(BF)

    def half_copy(k):
        return remote(drk.at[k, pl.ds(4 * (1 - core), 4)], pbuf.at[k], half_send.at[k], half_recv.at[k],
                      jnp.bitwise_xor(me, 1))

    def part(src_chip, k, lo, size):
        return drk_out.at[3 * src_chip + k, pl.ds(4 * core + lo, size)]

    def fin_copy(k, s):
        mine = part(chip, k, 0, 4)
        return remote(mine, mine, fin_send.at[k, s], fin_recv.at[k, s], jnp.bitwise_xor(me, (1, 2, 4)[s]))

    def fin_arrived(k, s):
        theirs = part(jnp.bitwise_xor(chip, s), k, 0, 4)
        return remote(theirs, theirs, fin_send.at[k, s], fin_recv.at[k, s], jnp.bitwise_xor(me, (1, 2, 4)[s]))

    outer = (chip == 0) | (chip == 3)
    hop_from = jnp.where(outer, 2, 1)
    hop_to = jnp.bitwise_xor(me, jnp.where(outer, 2, 4))
    hop_via = jnp.bitwise_xor(me, jnp.where(outer, 4, 2))

    def hop(k):
        piece = part(jnp.bitwise_xor(chip, hop_from), k, 0, 4)
        return remote(piece, piece, hop_send.at[k], hop_recv.at[k], hop_to)

    def hop_arrived(k):
        piece = part(jnp.bitwise_xor(chip, 3), k, 0, 4)
        return remote(piece, piece, hop_send.at[k], hop_recv.at[k], hop_via)

    def relay(k, s):
        piece = part(jnp.bitwise_xor(chip, s), k, 0, 4)
        return remote(piece, piece, rel_send.at[k, s], rel_recv.at[k, s], jnp.bitwise_xor(me, 1))

    def relay_arrived(k, s):
        piece = drk_out.at[3 * jnp.bitwise_xor(chip, s) + k, pl.ds(4 * (1 - core), 4)]
        return remote(piece, piece, rel_send.at[k, s], rel_recv.at[k, s], jnp.bitwise_xor(me, 1))

    def pass_on(k):
        for first in (True, False):
            for s in (1, 2):
                @pl.when((hop_from == s) == first)
                def _():
                    fin_arrived(k, s).wait_recv()
                    if first:
                        hop(k).start()
                    relay(k, s).start()

    def made_there(a, dev, owner):
        if a < 2:
            return (dev < 2) & (owner != 0)
        return (dev >= 6) & (owner != 3)

    def stat_copy(n):
        return remote(st_out.at[n], st_in.at[chip, n], st_send.at[n], st_recv.at[chip, n], 6 + core)

    def after_softmax(n, i, m, inv, rd):
        @pl.when((i >= 6) & (chip != 3))
        def _():
            lane = lax.broadcasted_iota(jnp.int32, (T, H), 1)
            table = jnp.where(lane == 0, m, jnp.where(lane == 1, inv, jnp.where(lane == 2, rd, 0.0)))
            st_out[n, i - 6] = table.T[:8]

        @pl.when((i == 6) & (chip != 3))
        def _():
            stat_copy(n).start()

    def local_pair(x):
        owner = jnp.where(rows_here, 1, 0) + x % 3
        return owner, 2 * core + (x // 3) % 2, 3 * owner + x // 6

    def local_loads(x, sl):
        _, bat, head = local_pair(x)
        copies = [pltpu.make_async_copy(rel.at[head, pl.ds(0, 2)], lrk.at[sl], l_sem.at[sl, 0])]
        for a in range(4):
            copies.append(pltpu.make_async_copy(ins[a].at[bat, head], lblk.at[sl, core, a], l_sem.at[sl, 1 + a]))
            copies.append(pltpu.make_async_copy(lx.at[a, bat % 2, head], lblk.at[sl, 1 - core, a], l_sem.at[sl, 5 + a]))
        return copies

    def local_sends(x, sl, low_end):
        _, bat, head = local_pair(x)
        dsts = outs[:2] if low_end else outs[2:]
        return [remote(lres.at[sl, 1 - core, a], dsts[a].at[bat, head], lr_send.at[sl, a], lr_recv, partner)
                for a in range(2)]

    def local_work(lo, hi, low_end):
        for copy in local_loads(lo, lo % 2):
            copy.start()

        def one(x, _):
            sl = x % 2

            @pl.when(x + 1 < hi)
            def _():
                for copy in local_loads(x + 1, 1 - sl):
                    copy.start()

            for copy in local_loads(x, sl):
                copy.wait()
            owner, bat, head = local_pair(x)
            u = bu[pl.ds(head, 1)]
            w = bw[pl.ds(head, 1)]

            @pl.when(x > 1)
            def _():
                for copy in local_sends(x, sl, low_end):
                    copy.wait_send()

            q, key, val, do = [[lblk[sl, r, a] for r in range(2)] for a in range(4)]
            res = [[lres.at[sl, r, a] for r in range(2)] for a in range(2)]
            if low_end:
                row_block(q, do, key, val, lrk[sl], u, w, *res)
            else:
                n = x // 3
                piece = st_in.at[owner, n]
                remote(piece, piece, st_send.at[n], st_recv.at[owner, n], 2 * owner + core).wait_recv()
                col_block(q, do, key, val, lrk[sl], piece, u, w, *res)
            for copy in local_sends(x, sl, low_end):
                copy.start()
            dsts = outs[:2] if low_end else outs[2:]
            for a in range(2):
                dsts[a][bat, head] = lres[sl, core, a]
            return 0

        lax.fori_loop(lo, hi, one, 0)

    @pl.when(rows_here)
    def _():
        for copy in pair_copies(True):
            copy.wait_recv()
        local_work(0, EARLY, True)

    def send_tile(n, i):
        mask = jnp.bitwise_xor(me, i)

        def send(a):
            remote(rin.at[n, i, a], spot(outs[a], me, n), out_send.at[n, i, a // 2], out_recv.at[n, mask, a // 2],
                       i).start()

        for first in (0, 2):
            @pl.when((mask != 0) & ~made_there(first, i, chip))
            def _():
                send(first)
                send(first + 1)

        @pl.when(mask == 0)
        def _():
            for a in range(4):
                spot(outs[a], me, n)[:] = rin[n, i, a]

    def run_unit(n, _):
        k = n // 2
        pltpu.make_async_copy(rin.at[n, me], rin.at[n, me], in_loc.at[n]).wait()
        for mask in range(1, 8):
            in_wait(n, mask).wait_recv()

        def after_tile(i):
            @pl.when(n < HOLD)
            def _():
                send_tile(n, i)

        head = pl.ds(3 * chip + k, 1)
        unit(rin.at[n], rk.at[k], rkr.at[k], bu[head], bw[head], drk.at[k], duw.at[k], scratch,
             lambda i, m, inv, rd: after_softmax(n, i, m, inv, rd), after_tile)

        @pl.when(n % 2 == 1)
        def _():
            copy = half_copy(k)
            copy.start()
            copy.wait()
            for r in range(4):
                part(chip, k, r, 1)[0] = (drk[k, 4 * core + r] + pbuf[k, r]).T
            for s in range(3):
                fin_copy(k, s).start()

        return 0

    lax.fori_loop(0, NU, run_unit, 0)

    def late_sends(x, _):
        send_tile(HOLD + x // NT, NT - 1 - x % NT)
        return 0

    lax.fori_loop(0, (NU - HOLD) * NT, late_sends, 0)
    pass_on(0)
    pass_on(1)

    def duw_copy(mask, arrived):
        dev = jnp.bitwise_xor(me, mask)
        return remote(duw, duw_all.at[dev if arrived else me], duw_send.at[mask], duw_recv.at[mask], dev)

    for mask in range(1, 8):
        duw_copy(mask, False).start()
    duw_all[me] = duw[:]

    @pl.when(rows_here)
    def _():
        local_work(EARLY, 18, True)

    @pl.when(cols_here)
    def _():
        for copy in pair_copies(False):
            copy.wait_recv()
        local_work(0, 18, False)

    pass_on(2)
    for k in range(3):
        hop_arrived(k).wait_recv()
        relay(k, 3).start()

    for mask in range(1, 8):
        duw_copy(mask, False).wait_send()
        duw_copy(mask, True).wait_recv()
    for h in range(12):
        both = duw_all[2 * (h // 3), h % 3] + duw_all[2 * (h // 3) + 1, h % 3]
        du_out[h:h + 1] = both[0:1]
        dw_out[h:h + 1] = both[1:2]

    def finish(n, _):
        for mask in range(1, 8):
            dev = jnp.bitwise_xor(me, mask)
            in_wait(n, mask).wait_send()
            for first in (0, 2):
                both = rin.at[n, dev, pl.ds(first, 2)]
                copy = remote(both, both, out_send.at[n, dev, first // 2], out_recv.at[n, mask, first // 2], dev)

                @pl.when(~made_there(first, dev, chip))
                def _():
                    copy.wait_send()

                @pl.when(~made_there(first, me, dev // 2))
                def _():
                    copy.wait_recv()

        @pl.when(chip != 3)
        def _():
            stat_copy(n).wait_send()
        return 0

    lax.fori_loop(0, NU, finish, 0)
    pair("wait_send")
    for low_end in (True, False):
        @pl.when(rows_here if low_end else cols_here)
        def _():
            for x in (16, 17):
                for copy in local_sends(x, x % 2, low_end):
                    copy.wait_send()
            whole = oq.at[pl.ds(0, 3)]
            remote(whole, whole, lr_send.at[0, 0], lr_recv, partner).wait_recv()

    for k in range(3):
        fin_copy(k, 0).wait_send()
        theirs = drk_out.at[3 * chip + k, pl.ds(4 * (1 - core), 4)]
        remote(theirs, theirs, fin_send.at[k, 0], fin_recv.at[k, 0], jnp.bitwise_xor(me, 1)).wait_recv()
        for s in (1, 2):
            fin_copy(k, s).wait_send()
        hop(k).wait_send()
        for s in (1, 2, 3):
            relay(k, s).wait_send()
            relay_arrived(k, s).wait_recv()


def exchange_attend(xq, xk, xv, xd, bias_u, bias_w, rel):
    any_spec = pl.BlockSpec(memory_space=pl.ANY)
    vmem_spec = pl.BlockSpec(memory_space=pltpu.VMEM)
    dma = pltpu.SemaphoreType.DMA
    act = pltpu.VMEM((4, 12, T, D), BF)
    bias = pltpu.VMEM((12, D), F32)
    return pl.pallas_call(
        kernel,
        out_shape=(act, act, act, act, pltpu.VMEM((12, NT, T, D), F32), bias, bias,
                   jax.ShapeDtypeStruct((4, 2, 12, T, D), BF)),
        in_specs=[any_spec] * 4 + [vmem_spec] * 2 + [any_spec],
        out_specs=(vmem_spec,) * 7 + (any_spec,),
        scratch_shapes=[
            pltpu.VMEM((NU, 8, 4, T, D), BF), pltpu.VMEM((3, NT, D, T), F32),
            pltpu.VMEM((3, 4, D, T), F32), pltpu.VMEM((3, 8, D), F32), pltpu.VMEM((8, 3, 8, D), F32),
            pltpu.VMEM((3, NT, T, D), BF), pltpu.VMEM((3, NT, T, D), BF), pltpu.VMEM((12, D), F32), pltpu.VMEM((12, D), F32),
            pltpu.VMEM((2, 2, 4, T, D), BF), pltpu.VMEM((2, 2, T, D), BF), pltpu.VMEM((2, 2, 2, T, D), BF),
            pltpu.VMEM((NU, 2, 8, T), F32), pltpu.VMEM((3, NU, 2, 8, T), F32),
            dma((NU, 8)), dma((NU, 8)), dma((NU,)), dma((NU, 8, 2)), dma((NU, 8, 2)), dma((3,)), dma((3,)),
            dma((3, 3)), dma((3, 3)), dma((3,)), dma((3,)), dma((3, 4)), dma((3, 4)), dma((8,)), dma((8,)), dma(()), dma((4,)), dma((4,)),
            dma((NU,)), dma((3, NU)), dma((2, 9)), dma((2, 2)), dma(())]
        + UNIT_SCRATCH,
        compiler_params=pltpu.CompilerParams(has_side_effects=True, vmem_limit_bytes=VMEM_LIMIT),
    )(xq, xk, xv, xd, bias_u, bias_w, rel)


def write_kernel(*refs):
    half = len(refs) // 2
    sem = refs[-1]
    copies = [pltpu.make_async_copy(refs[n], refs[half + n], sem.at[n]) for n in range(half)]
    for copy in copies:
        copy.start()
    for copy in copies:
        copy.wait()


def write_out(arrs):
    return pl.pallas_call(
        write_kernel,
        out_shape=tuple(jax.ShapeDtypeStruct(arr.shape, arr.dtype) for arr in arrs),
        in_specs=[pl.BlockSpec(memory_space=pltpu.VMEM)] * len(arrs),
        out_specs=(pl.BlockSpec(memory_space=pl.ANY),) * len(arrs),
        scratch_shapes=[pltpu.SemaphoreType.DMA((len(arrs),))],
        compiler_params=pltpu.CompilerParams(vmem_limit_bytes=1024 * 1024),
    )(*[pltpu.with_memory_space_constraint(arr, pltpu.VMEM) for arr in arrs])


def solution(mesh):
    seq_spec = P(None, 'cp', None, None)

    def local(query, key_in, value, bias_u, bias_w, rel_k, d_out):
        def by_head(arr):
            return arr.transpose(0, 2, 1, 3)

        rel = rel_k.transpose(1, 0, 2).reshape(12, NT, T, D)
        res = exchange_attend(by_head(query), by_head(key_in), by_head(value), by_head(d_out), bias_u, bias_w, rel)
        res = write_out(res[:7])
        d_rel = res[4].reshape(12, NT * T, D).transpose(1, 0, 2)
        return tuple(by_head(arr) for arr in res[:4]) + (res[5], res[6], d_rel)

    return jax.shard_map(local, mesh=mesh,
                         in_specs=(seq_spec, seq_spec, seq_spec, P(), P(), P(), seq_spec),
                         out_specs=(seq_spec, seq_spec, seq_spec, seq_spec, P(), P(), P()),
                         check_vma=False)
```

time: 343 us -> 327 us (0.953)
  Pallas kernels: 343 us -> 325 us
    pallas_call x1, Pallas kernels: 334 us -> 317 us  [exchange_attend(): pl.pallas_call(kernel, out_shape=(act, act, act, act, pltpu.VMEM((12, NT,...]
where the time goes in v5:
time: 327 us; the launch traced here: 326 us
  Pallas kernels  325 us (99%)
    pallas_call x1, Pallas kernels, exchange_attend(): pl.pallas_call(kernel, out_shape=(act, act, act, act, pltpu.VMEM((12, NT,...  317 us
    pallas_call x1, Pallas kernels, write_out(): pl.pallas_call(write_kernel, out_shape=tuple((jax.ShapeDtypeStruct(arr.sh...  8.81 us

profile of v5, /device:TPU:0, one launch (start us, length us, event | category | flops | bytes accessed | tf_op | source)
XLA Modules:
  0.0 326.0 jit_solution(7208527164934513551)
XLA Ops:
  0.6 316.5 %shard_map.126 = (bf16[4,12,256,128]{3,2,1,0:T(8,128)(2,1)S(1)}, bf16[4,12,256,128]{3,2,1,0:T(8,128)(2,1)S(1)}, bf16[4,12,256,128]{3,2,1,0:T(8,128)(2,1)S(1)}, b...) custom-call(bf16[4,12,256,128]{3,2,1,0:T(8,128)(2,1)} %bitcast.15, ...), custom_call_target="tpu_custom_call" | custom-call | tf_op jit(solution)/shard_map/pallas_call | solution.py:584
  317.2 8.8 %shard_map.127 = (bf16[4,12,256,128]{3,2,1,0:T(8,128)(2,1)}, bf16[4,12,256,128]{3,2,1,0:T(8,128)(2,1)}, bf16[4,12,256,128]{3,2,1,0:T(8,128)(2,1)}, bf16[4,12,256...) custom-call(bf16[4,12,256,128]{3,2,1,0:T(8,128)(2,1)S(1)} %get-tuple-element.21.refs_, ...), custom_call_target="tpu_custom_call" | custom-call | tf_op jit(solution)/shard_map/pallas_call | solution.py:615

commit v6 on v4

v6 whole, which is shorter than its diff:
```python
import jax
import jax.numpy as jnp
from jax import lax
from jax.experimental import pallas as pl
from jax.experimental.pallas import tpu as pltpu
from jax.sharding import PartitionSpec as P

T = 256
D = 128
H = 128
NT = 8
NU = 6
NA = 4
HC = 3
NH = 12
EARLY = 6
AHEAD = 3
VMEM_LIMIT = 39 * 1024 * 1024
F32 = jnp.float32
BF = jnp.bfloat16
SCALE = D ** -0.5
C2 = SCALE * 1.4426950408889634
MESH = pl.DeviceIdType.MESH


def dot_nt(lhs, rhs):
    return lax.dot_general(lhs, rhs, (((1,), (1,)), ((), ())), preferred_element_type=F32)


def row_max(arr):
    return jnp.max(arr, axis=1, keepdims=True)


def row_sum(arr):
    return jnp.sum(arr, axis=1, keepdims=True)


def dot_nn(lhs, rhs):
    return lax.dot_general(lhs, rhs, (((1,), (0,)), ((), ())), preferred_element_type=F32)


def unit(x, rk, rkr, u, w, drk, duw, scratch, after_softmax, after_tile):
    (s_ref, dp_ref, r_ref, mx_ref, l_ref, d_ref, u_ref, dk_ref, dv_ref, a_ref, c_ref, t_ref,
     oacc, qc_acc, qr_acc) = scratch
    nt = NT
    low = lower_mask()
    gather = gather_fn()
    dk_ref[:] = jnp.zeros_like(dk_ref)
    dv_ref[:] = jnp.zeros_like(dv_ref)

    def prep(i, sl):
        q = x[i, 0].astype(F32)
        a_ref[sl] = (q + u).astype(BF)
        c_ref[sl] = (q + w).astype(BF)
        mx_ref[:] = jnp.full((T, H), -jnp.inf, F32)
        r_ref[:] = jnp.full((2, T, H), -jnp.inf, F32)

    def logits(i, sl, n):
        j = i - n
        by = dot_nt(c_ref[sl], rkr[n])
        sc = dot_nt(a_ref[sl], x[j, 2])
        dp_ref[sl, j] = dot_nt(x[i, 1], x[j, 3])
        r0, r1 = [pltpu.roll(half, 1, 1, stride=1, stride_axis=0) for half in (by[:, :H], by[:, H:])]
        sc += shifted(low, r1, r0, r_ref[1], r_ref[0])
        r_ref[0] = r0
        r_ref[1] = r1
        s_ref[sl, j] = sc
        mx_ref[:] = jnp.maximum(mx_ref[:], jnp.maximum(sc[:, :H], sc[:, H:]))

    def softmax(i, sl):
        m = row_max(mx_ref[:])
        l_ref[:] = jnp.zeros_like(l_ref)
        d_ref[:] = jnp.zeros_like(d_ref)

        def body(j, _):
            p = jnp.exp2((s_ref[sl, j] - m) * C2)
            s_ref[sl, j] = p
            pd = p * dp_ref[sl, j]
            l_ref[:] += p[:, :H] + p[:, H:]
            d_ref[:] += pd[:, :H] + pd[:, H:]
            return 0

        lax.fori_loop(0, i + 1, body, 0)
        inv = 1.0 / row_sum(l_ref[:])
        rd = row_sum(d_ref[:]) * inv
        after_softmax(i, m, inv, rd)
        return inv, rd

    def grads(i, sl, j, inv, rd):
        pn = s_ref[sl, j] * inv
        pb = pn.astype(BF)
        ds = pn * (dp_ref[sl, j] - rd) * SCALE
        dsb = ds.astype(BF)
        oacc[:] += dot_nn(pb, x[j, 3])
        dv_ref[j] += dot_nn(t_ref[0], pb)
        qc_acc[:] += dot_nn(dsb, x[j, 2])
        dk_ref[j] += dot_nn(t_ref[1], dsb)
        g0, g1 = gather(ds)
        dist = shifted(low, g0, g1, u_ref[0], u_ref[1]).astype(BF)
        u_ref[0] = g0
        u_ref[1] = g1
        qr_acc[:] += dot_nn(dist, rk[i - j])
        drk[i - j] += dot_nn(t_ref[2], dist)

    prep(nt - 1, (nt - 1) % 2)

    def first(n, _):
        logits(nt - 1, (nt - 1) % 2, n)
        return 0

    lax.fori_loop(0, nt, first, 0)

    def tile(ii, _):
        i = nt - 1 - ii
        sl = i % 2
        inv, rd = softmax(i, sl)
        nxt = jnp.maximum(i - 1, 0)
        t_ref[0] = x[i, 1].T
        t_ref[1] = a_ref[sl].T
        t_ref[2] = c_ref[sl].T
        for acc in (oacc, qc_acc, qr_acc, u_ref):
            acc[:] = jnp.zeros_like(acc)
        prep(nxt, 1 - sl)

        def both(n, _):
            grads(i, sl, n, inv, rd)
            logits(nxt, 1 - sl, n)
            return 0

        lax.fori_loop(0, i, both, 0)
        grads(i, sl, i, inv, rd)
        qc = qc_acc[:]
        qr = qr_acc[:]
        for r, part in enumerate((qc, qr)):
            duw[r:r + 1] += jnp.sum(part, axis=0, keepdims=True)
        for r, res in enumerate((oacc[:], qc + qr, dk_ref[i].T, dv_ref[i].T)):
            x[i, r] = res.astype(BF)
        after_tile(i)
        return 0

    lax.fori_loop(0, nt, tile, 0)


def gather_fn():
    idx = (lax.broadcasted_iota(jnp.int32, (T, H), 0) - lax.broadcasted_iota(jnp.int32, (T, H), 1)) & (H - 1)

    def gather(arr):
        return [jnp.take_along_axis(half, idx, axis=1, mode="promise_in_bounds") for half in (arr[:, :H], arr[:, H:])]

    return gather


def lower_mask():
    return lax.broadcasted_iota(jnp.int32, (H, H), 1) <= lax.broadcasted_iota(jnp.int32, (H, H), 0)


def shifted(low, n0, n1, p0, p1):
    lo = jnp.concatenate([jnp.where(low, n0[:H], p1[:H]), jnp.where(low, n1[H:], n0[H:])], 0)
    hi = jnp.concatenate([jnp.where(low, p1[:H], p0[:H]), jnp.where(low, n0[H:], p1[H:])], 0)
    return jnp.concatenate([lo, hi], 1)


def row_tile(q, d_out, keys, vals, rk, u, w):
    last = len(keys) - 1
    low = lower_mask()
    gather = gather_fn()
    qf = q.astype(F32)
    a = (qf + u).astype(BF)
    c = (qf + w).astype(BF)
    by = [gather(dot_nt(c, rk[n])) for n in range(last + 1)]
    none = [jnp.full((T, H), -jnp.inf, F32)] * 2
    s = [dot_nt(a, key) + shifted(low, *by[last - j], *(by[last - j - 1] if j < last else none)) for j, key in enumerate(keys)]
    top = s[0]
    for other in s[1:]:
        top = jnp.maximum(top, other)
    m = row_max(top)
    p = [jnp.exp2((sj - m) * C2) for sj in s]
    dp = [dot_nt(d_out, val) for val in vals]
    inv = 1.0 / row_sum(sum(p))
    row_dot = row_sum(sum(pj * dj for pj, dj in zip(p, dp))) * inv
    out, d_q, prev = 0.0, 0.0, [jnp.zeros((T, H), F32)] * 2
    for j in range(last + 1):
        pn = p[j] * inv
        ds = pn * (dp[j] - row_dot) * SCALE
        out += dot_nn(pn.astype(BF), vals[j])
        mine = gather(ds)
        dist = shifted(low, *mine, *prev).astype(BF)
        prev = mine
        d_q += dot_nn(ds.astype(BF), keys[j]) + dot_nn(dist, rk[last - j])
    return out.astype(BF), d_q.astype(BF)


def col_tiles(qs, d_outs, keys, vals, rk, stats, u, w):
    low = lower_mask()
    gather = gather_fn()
    none = [jnp.full((T, H), -jnp.inf, F32)] * 2
    d_keys, d_vals = [0.0, 0.0], [0.0, 0.0]
    for i in range(len(qs)):
        qf = qs[i].astype(F32)
        a = (qf + u).astype(BF)
        c = (qf + w).astype(BF)
        by = {n: gather(dot_nt(c, rk[n])) for n in range(max(i - 2, 0), i + 1)}
        cols = jnp.concatenate([stats[i], jnp.zeros((H - 8, T), F32)], 0).T
        m, inv, row_dot = cols[:, 0:1], cols[:, 1:2], cols[:, 2:3]
        at, dot = a.T, d_outs[i].T
        for r in range(min(i + 1, 2)):
            n = i - r
            s = dot_nt(a, keys[r]) + shifted(low, *by[n], *(by[n - 1] if n else none))
            pn = jnp.exp2((s - m) * C2) * inv
            ds = pn * (dot_nt(d_outs[i], vals[r]) - row_dot) * SCALE
            d_vals[r] += dot_nn(dot, pn.astype(BF))
            d_keys[r] += dot_nn(at, ds.astype(BF))
    return [dk.T.astype(BF) for dk in d_keys], [dv.T.astype(BF) for dv in d_vals]


UNIT_SCRATCH = (
    [pltpu.VMEM((2, NT, T, T), F32)] * 2 + [pltpu.VMEM((2, T, H), F32)] + [pltpu.VMEM((T, H), F32)] * 3
    + [pltpu.VMEM((2, T, H), F32)] + [pltpu.VMEM((NT, D, T), F32)] * 2 + [pltpu.VMEM((2, T, D), BF)] * 2
    + [pltpu.VMEM((3, D, T), BF)] + [pltpu.VMEM((T, D), F32)] * 3)


def kernel(xq, xd, xk, xv, bias_u, bias_w, rel, oq, odq, odk, odv, drk_out, du_out, dw_out, lx,
           rin, rl, drk, pbuf, duw, duw_all, rk, rkr, bu, bw, lblk, lrk, lres, st_out, st_in,
           in_send, in_recv, in_loc, rl_recv, fw_send, fw_recv, out_send, out_recv, half_send, half_recv,
           fin_send, fin_recv, hop_send, hop_recv, rel_send, rel_recv, duw_send, duw_recv, rk_sem, px_send, px_recv,
           st_send, st_recv, l_sem, lr_send, lr_recv, *scratch):
    me = lax.axis_index('cp')
    chip = me // 2
    core = me % 2
    last = NA - 1
    partner = jnp.bitwise_xor(me, 1)
    outer = (chip == 0) | (chip == last)
    ins = (xq, xd, xk, xv)
    outs = (oq, odq, odk, odv)
    neighbours = (1, 2, 4)

    def remote(src, dst, ssem, rsem, dev):
        return pltpu.make_async_remote_copy(src_ref=src, dst_ref=dst, send_sem=ssem, recv_sem=rsem,
                                            device_id=(dev,), device_id_type=MESH)

    def spot(arr, dev, n):
        return arr.at[2 * (dev % 2) + n % 2, HC * (dev // 2) + n // 2]

    def send_in(n, mask):
        dev = jnp.bitwise_xor(me, mask)

        def send(first, via):
            for a in (first, first + 1):
                if via:
                    dst, rsem, to = rl.at[n, core, a % 2], rl_recv.at[n], jnp.bitwise_xor(dev, 4)
                else:
                    dst, rsem, to = rin.at[n, me, a], in_recv.at[n, mask], dev
                remote(spot(ins[a], dev, n), dst, in_send.at[n, mask], rsem, to).start()

        for first in (0, 2):
            if mask < NU:
                send(first, False)
            else:
                through = chip == (0 if first else last)
                for via in (True, False):
                    @pl.when(through == via)
                    def _():
                        send(first, via)

    def send_pair(n):
        for mask in (6, 2, 4, 7, 3, 5, 1):
            send_in(n, mask)

    def in_wait(n, mask, size=NA):
        dev = jnp.bitwise_xor(me, mask)
        piece = rin.at[n, dev, pl.ds(0, size)]
        return remote(piece, piece, in_send.at[n, mask], in_recv.at[n, mask], dev)

    def forward(n):
        dst = rin.at[n, pl.ds(2 * jnp.bitwise_xor(chip, 1), 2), pl.ds(2 * (chip % 2), 2)]
        return remote(rl.at[n], dst, fw_send.at[n], fw_recv.at[n], jnp.bitwise_xor(me, 4))

    def pass_forward(n):
        remote(rl.at[n], rl.at[n], fw_send.at[n], rl_recv.at[n], jnp.bitwise_xor(me, 2)).wait_recv()
        forward(n).start()

    def at_chip(act):
        for c, heads in enumerate(((3, 9), (9, 3), (0, 3), (0, 9))):
            @pl.when(chip == c)
            def _():
                act(c, pl.ds(*heads))

    def pair_copies(heads):
        return [remote(ins[a].at[pl.ds(2 * (1 - core), 2), heads], lx.at[a, :, heads], px_send.at[a], px_recv.at[a], partner)
                for a in range(NA)]

    rk_copy = pltpu.make_async_copy(rel.at[pl.ds(HC * chip, HC)], rk, rk_sem)
    rk_copy.start()
    for n in range(NU):
        for a in range(NA):
            pltpu.make_async_copy(spot(ins[a], me, n), rin.at[n, me, a], in_loc.at[n]).start()
        if n < AHEAD:
            send_pair(n)
        if n == 0:
            at_chip(lambda c, heads: [copy.start() for copy in pair_copies(heads)])

    bu[:] = bias_u[:].astype(F32)
    bw[:] = bias_w[:].astype(F32)
    drk[:] = jnp.zeros_like(drk)
    duw[:] = jnp.zeros_like(duw)
    rk_copy.wait()
    flip = (lax.broadcasted_iota(jnp.int32, (T, T), 0) + lax.broadcasted_iota(jnp.int32, (T, T), 1) == T - 1).astype(BF)
    for k in range(HC):
        for n in range(NT):
            rkr[k, n] = dot_nn(flip, rk[k, n]).astype(BF)

    def half_copy(k):
        return remote(drk.at[k, pl.ds(NA * (1 - core), NA)], pbuf.at[k], half_send.at[k], half_recv.at[k], partner)

    def part(src_chip, k, lo, size):
        return drk_out.at[HC * src_chip + k, pl.ds(NA * core + lo, size)]

    def fin_copy(k, s, arrived=False):
        piece = part(jnp.bitwise_xor(chip, s) if arrived else chip, k, 0, NA)
        return remote(piece, piece, fin_send.at[k, s], fin_recv.at[k, s], jnp.bitwise_xor(me, neighbours[s]))

    def hop(k, s, arrived=False):
        piece = part(jnp.bitwise_xor(chip, last if arrived else s), k, 2 * (s - 1), 2)
        return remote(piece, piece, hop_send.at[k, s], hop_recv.at[k, s], jnp.bitwise_xor(me, neighbours[-s]))

    def relay(k, s, arrived=False):
        half = 1 - core if arrived else core
        piece = drk_out.at[HC * jnp.bitwise_xor(chip, s) + k, pl.ds(NA * half, NA)]
        return remote(piece, piece, rel_send.at[k, s], rel_recv.at[k, s], partner)

    def pass_on(k):
        for s in (1, 2):
            fin_copy(k, s, True).wait_recv()
            hop(k, s).start()
            relay(k, s).start()

    def made_there(first, dev, owner):
        there = dev // 2
        if first:
            return ((there == last) & (owner != last)) | ((there == 2) & (owner == 0))
        return ((there == 0) & (owner != 0)) | ((there == 1) & (owner == last))

    def stat_copy(n, whole):
        if whole:
            return remote(st_out.at[n], st_in.at[0, n], st_send.at[n, 1], st_recv.at[0, n], 4 + core)
        piece = pl.ds(2, 2)
        return remote(st_out.at[n, piece], st_in.at[chip, n, piece], st_send.at[n, 0], st_recv.at[chip, n], 6 + core)

    def after_softmax(n, i, m, inv, rd):
        first = jnp.where(chip == 0, 4, 6)

        @pl.when((i >= first) & (chip != last))
        def _():
            lane = lax.broadcasted_iota(jnp.int32, (T, H), 1)
            table = jnp.where(lane == 0, m, jnp.where(lane == 1, inv, jnp.where(lane == 2, rd, 0.0)))
            st_out[n, i - 4] = table.T[:8]

        @pl.when((i == 6) & (chip != last))
        def _():
            stat_copy(n, False).start()

        @pl.when((i == 4) & (chip == 0))
        def _():
            stat_copy(n, True).start()

    def local_pair(x):
        owner = jnp.where(outer, x % HC + jnp.where(chip == 0, 1, 0), jnp.where(chip == 1, last, 0))
        n = jnp.where(outer, x // HC, x)
        return owner, n, 2 * core + n % 2, HC * owner + n // 2

    def local_loads(x, sl):
        _, n, bat, head = local_pair(x)
        copies = [pltpu.make_async_copy(rel.at[head, pl.ds(0, NA)], lrk.at[sl], l_sem.at[sl, 0, 2])]
        for a in range(NA):
            for r, src in enumerate((ins[a].at[bat, head], lx.at[a, n % 2, head])):
                where = core if r == 0 else 1 - core
                copies.append(pltpu.make_async_copy(src, lblk.at[sl, where, a], l_sem.at[sl, a, r]))
        return copies

    def local_sends(x, c):
        sl = x % 2
        _, _, bat, head = local_pair(x)
        dsts = outs[2 * (c // 2):]
        return [remote(lres.at[sl, 1 - core, a], dsts[a].at[bat, head], lr_send.at[sl, a], lr_recv, partner)
                for a in range(2)]

    def local_work(lo, hi, c):
        for copy in local_loads(lo, lo % 2):
            copy.start()

        def one(x, _):
            sl = x % 2

            @pl.when(x + 1 < hi)
            def _():
                for copy in local_loads(x + 1, 1 - sl):
                    copy.start()

            for copy in local_loads(x, sl):
                copy.wait()

            @pl.when(x > 1)
            def _():
                for copy in local_sends(x, c):
                    copy.wait_send()

            owner, n, bat, head = local_pair(x)
            u = bu[pl.ds(head, 1)]
            w = bw[pl.ds(head, 1)]
            q, do, key, val = [[lblk[sl, r, a] for r in range(2)] for a in range(NA)]
            table = lrk[sl]
            if c < 2:
                if c:
                    key = [rl[n, r, 0] for r in range(2)] + key
                    val = [rl[n, r, 1] for r in range(2)] + val
                for r in range(2):
                    upto = len(key) - 1 + r
                    res = row_tile(q[r], do[r], key[:upto], val[:upto], table, u, w)
                    for a in range(2):
                        lres[sl, r, a] = res[a]
            else:
                piece = st_in.at[owner, n]
                if c == last:
                    piece = st_in.at[owner, n, pl.ds(2, 2)]
                else:
                    q = q + [rl[n, r, 0] for r in range(2)]
                    do = do + [rl[n, r, 1] for r in range(2)]
                remote(piece, piece, st_send.at[n, 0], st_recv.at[owner, n], 2 * owner + core).wait_recv()
                for a, res in enumerate(col_tiles(q, do, key, val, table, piece, u, w)):
                    for r in range(2):
                        lres[sl, r, a] = res[r]
            for copy in local_sends(x, c):
                copy.start()
            for a in range(2):
                outs[2 * (c // 2) + a][bat, head] = lres[sl, core, a]
            return 0

        lax.fori_loop(lo, hi, one, 0)

    def local_count(c):
        return NU if c in (1, 2) else NU * HC

    @pl.when(chip == 0)
    def _():
        for copy in pair_copies(pl.ds(3, 9)):
            copy.wait_recv()
        local_work(0, EARLY, 0)

    def send_tile(n, i):
        mask = jnp.bitwise_xor(me, i)
        for first in (0, 2):
            @pl.when((mask != 0) & ~made_there(first, i, chip))
            def _():
                for a in (first, first + 1):
                    remote(rin.at[n, i, a], spot(outs[a], me, n), out_send.at[n, i, first // 2],
                           out_recv.at[n, mask, first // 2], i).start()

        @pl.when(mask == 0)
        def _():
            for a in range(NA):
                spot(outs[a], me, n)[:] = rin[n, i, a]

    def run_unit(n, _):
        k = n // 2

        @pl.when(n + AHEAD < NU)
        def _():
            send_pair(n + AHEAD)

        @pl.when(~outer & (n == 0))
        def _():
            pass_forward(0)

        @pl.when(~outer & (n + 1 < NU))
        def _():
            pass_forward(n + 1)

        pltpu.make_async_copy(rin.at[n, me], rin.at[n, me], in_loc.at[n]).wait()
        for mask in range(1, NT):
            if mask < NU:
                in_wait(n, mask).wait_recv()
            else:
                for split in (True, False):
                    @pl.when(outer == split)
                    def _():
                        in_wait(n, mask, 2 if split else NA).wait_recv()

        @pl.when(outer)
        def _():
            piece = rin.at[n, pl.ds(0, 2), pl.ds(0, 2)]
            remote(piece, piece, fw_send.at[n], fw_recv.at[n], jnp.bitwise_xor(me, 4)).wait_recv()

        head = pl.ds(HC * chip + k, 1)
        unit(rin.at[n], rk.at[k], rkr.at[k], bu[head], bw[head], drk.at[k], duw.at[k], scratch,
             lambda i, m, inv, rd: after_softmax(n, i, m, inv, rd), lambda i: send_tile(n, i))

        @pl.when(n % 2 == 1)
        def _():
            copy = half_copy(k)
            copy.start()
            copy.wait()
            for r in range(NA):
                part(chip, k, r, 1)[0] = (drk[k, NA * core + r] + pbuf[k, r]).T
            for s in range(3):
                fin_copy(k, s).start()

        return 0

    lax.fori_loop(0, NU, run_unit, 0)

    pass_on(0)
    pass_on(1)

    def duw_copy(mask, arrived):
        dev = jnp.bitwise_xor(me, mask)
        return remote(duw, duw_all.at[dev if arrived else me], duw_send.at[mask], duw_recv.at[mask], dev)

    for mask in range(1, NT):
        duw_copy(mask, False).start()
    duw_all[me] = duw[:]

    def late_work(c, heads):
        if c:
            for copy in pair_copies(heads):
                copy.wait_recv()
        local_work(0 if c else EARLY, local_count(c), c)

    at_chip(late_work)
    pass_on(2)
    for k in range(HC):
        for s in (1, 2):
            hop(k, s, True).wait_recv()
        relay(k, last).start()

    for mask in range(1, NT):
        duw_copy(mask, False).wait_send()
        duw_copy(mask, True).wait_recv()
    for h in range(NH):
        both = duw_all[2 * (h // HC), h % HC] + duw_all[2 * (h // HC) + 1, h % HC]
        for r, out in enumerate((du_out, dw_out)):
            out[h:h + 1] = both[r:r + 1]

    def finish(n, _):
        for mask in range(1, NT):
            dev = jnp.bitwise_xor(me, mask)
            in_wait(n, mask).wait_send()
            for first in (0, 2):
                both = rin.at[n, dev, pl.ds(first, 2)]
                copy = remote(both, both, out_send.at[n, dev, first // 2], out_recv.at[n, mask, first // 2], dev)

                @pl.when(~made_there(first, dev, chip))
                def _():
                    copy.wait_send()

                @pl.when(~made_there(first, me, dev // 2))
                def _():
                    copy.wait_recv()

        @pl.when(~outer)
        def _():
            forward(n).wait_send()

        @pl.when(chip != last)
        def _():
            stat_copy(n, False).wait_send()

        @pl.when(chip == 0)
        def _():
            stat_copy(n, True).wait_send()
        return 0

    lax.fori_loop(0, NU, finish, 0)

    def end_local(c, heads):
        for copy in pair_copies(heads):
            copy.wait_send()
        count = local_count(c)
        for x in (count - 2, count - 1):
            for copy in local_sends(x, c):
                copy.wait_send()
        whole = oq.at[pl.ds(0, count // NU)]
        remote(whole, whole, lr_send.at[0, 0], lr_recv, partner).wait_recv()

    at_chip(end_local)
    for k in range(HC):
        fin_copy(k, 0).wait_send()
        theirs = drk_out.at[HC * chip + k, pl.ds(NA * (1 - core), NA)]
        remote(theirs, theirs, fin_send.at[k, 0], fin_recv.at[k, 0], partner).wait_recv()
        for s in (1, 2):
            fin_copy(k, s).wait_send()
            hop(k, s).wait_send()
        for s in (1, 2, last):
            relay(k, s).wait_send()
            relay(k, s, True).wait_recv()


def exchange_attend(xq, xd, xk, xv, bias_u, bias_w, rel):
    any_spec = pl.BlockSpec(memory_space=pl.ANY)
    vmem_spec = pl.BlockSpec(memory_space=pltpu.VMEM)
    dma = pltpu.SemaphoreType.DMA
    act = pltpu.VMEM((NA, NH, T, D), BF)
    bias = pltpu.VMEM((NH, D), F32)
    heads = pltpu.VMEM((HC, NT, T, D), BF)
    per_head = dma((HC, NA))
    per_pair = dma((NU,))
    per_peer = dma((NU, NT))
    per_half = dma((NU, NT, 2))
    return pl.pallas_call(
        kernel,
        out_shape=(act, act, act, act, pltpu.VMEM((NH, NT, T, D), F32), bias, bias,
                   jax.ShapeDtypeStruct((NA, 2, NH, T, D), BF)),
        in_specs=[any_spec] * 4 + [vmem_spec] * 2 + [any_spec],
        out_specs=(vmem_spec,) * 7 + (any_spec,),
        scratch_shapes=[
            pltpu.VMEM((NU, NT, NA, T, D), BF), pltpu.VMEM((NU, 2, 2, T, D), BF), pltpu.VMEM((HC, NT, D, T), F32),
            pltpu.VMEM((HC, NA, D, T), F32), pltpu.VMEM((HC, 8, D), F32), pltpu.VMEM((NT, HC, 8, D), F32),
            heads, heads, bias, bias,
            pltpu.VMEM((2, 2, NA, T, D), BF), pltpu.VMEM((2, NA, T, D), BF), pltpu.VMEM((2, 2, 2, T, D), BF),
            pltpu.VMEM((NU, NA, 8, T), F32), pltpu.VMEM((HC, NU, NA, 8, T), F32),
            per_peer, per_peer, per_pair, per_pair, per_pair, per_pair, per_half, per_half, dma((HC,)), dma((HC,)),
            per_head, per_head, per_head, per_head, per_head, per_head, dma((NT,)), dma((NT,)), dma(()), dma((NA,)),
            dma((NA,)), dma((NU, 2)), dma((HC, NU)), dma((2, NA, HC)), dma((2, 2)), dma(())]
        + UNIT_SCRATCH,
        compiler_params=pltpu.CompilerParams(has_side_effects=True, vmem_limit_bytes=VMEM_LIMIT),
    )(xq, xd, xk, xv, bias_u, bias_w, rel)


def write_kernel(*refs):
    half = len(refs) // 2
    sem = refs[-1]
    copies = [pltpu.make_async_copy(refs[n], refs[half + n], sem.at[n]) for n in range(half)]
    for copy in copies:
        copy.start()
    for copy in copies:
        copy.wait()


def write_out(arrs):
    return pl.pallas_call(
        write_kernel,
        out_shape=tuple(jax.ShapeDtypeStruct(arr.shape, arr.dtype) for arr in arrs),
        in_specs=[pl.BlockSpec(memory_space=pltpu.VMEM)] * len(arrs),
        out_specs=(pl.BlockSpec(memory_space=pl.ANY),) * len(arrs),
        scratch_shapes=[pltpu.SemaphoreType.DMA((len(arrs),))],
        compiler_params=pltpu.CompilerParams(vmem_limit_bytes=1024 * 1024),
    )(*[pltpu.with_memory_space_constraint(arr, pltpu.VMEM) for arr in arrs])


def solution(mesh):
    seq_spec = P(None, 'cp', None, None)

    def local(query, key_in, value, bias_u, bias_w, rel_k, d_out):
        def by_head(arr):
            return arr.transpose(0, 2, 1, 3)

        rel = rel_k.transpose(1, 0, 2).reshape(NH, NT, T, D)
        acts = [by_head(arr) for arr in (query, d_out, key_in, value)]
        res = write_out(exchange_attend(*acts, bias_u, bias_w, rel)[:7])
        d_rel = res[4].reshape(NH, NT * T, D).transpose(1, 0, 2)
        return tuple(by_head(arr) for arr in res[:4]) + (res[5], res[6], d_rel)

    return jax.shard_map(local, mesh=mesh,
                         in_specs=(seq_spec, seq_spec, seq_spec, P(), P(), P(), seq_spec),
                         out_specs=(seq_spec, seq_spec, seq_spec, seq_spec, P(), P(), P()),
                         check_vma=False)
```

time: 343 us -> 313 us (0.913)
  Pallas kernels: 343 us -> 311 us
    pallas_call x1, Pallas kernels: 334 us -> 302 us  [exchange_attend(): pl.pallas_call(kernel, out_shape=(act, act, act, act, pltpu.VMEM((NH, NT,...]
where the time goes in v6:
time: 313 us; the launch traced here: 311 us
  Pallas kernels  311 us (99%)
    pallas_call x1, Pallas kernels, exchange_attend(): pl.pallas_call(kernel, out_shape=(act, act, act, act, pltpu.VMEM((NH, NT,...  302 us
    pallas_call x1, Pallas kernels, write_out(): pl.pallas_call(write_kernel, out_shape=tuple((jax.ShapeDtypeStruct(arr.sh...  8.81 us

profile of v6, /device:TPU:0, one launch (start us, length us, event | category | flops | bytes accessed | tf_op | source)
XLA Modules:
  0.0 311.4 jit_solution(8184215619367728073)
XLA Ops:
  0.6 301.8 %shard_map.126 = (bf16[4,12,256,128]{3,2,1,0:T(8,128)(2,1)S(1)}, bf16[4,12,256,128]{3,2,1,0:T(8,128)(2,1)S(1)}, bf16[4,12,256,128]{3,2,1,0:T(8,128)(2,1)S(1)}, b...) custom-call(bf16[4,12,256,128]{3,2,1,0:T(8,128)(2,1)} %bitcast.15, ...), custom_call_target="tpu_custom_call" | custom-call | tf_op jit(solution)/shard_map/pallas_call | solution.py:608
  302.4 8.8 %shard_map.127 = (bf16[4,12,256,128]{3,2,1,0:T(8,128)(2,1)}, bf16[4,12,256,128]{3,2,1,0:T(8,128)(2,1)}, bf16[4,12,256,128]{3,2,1,0:T(8,128)(2,1)}, bf16[4,12,256...) custom-call(bf16[4,12,256,128]{3,2,1,0:T(8,128)(2,1)S(1)} %get-tuple-element.21.refs_, ...), custom_call_target="tpu_custom_call" | custom-call | tf_op jit(solution)/shard_map/pallas_call | solution.py:639

commit v7 on v6

--- a/solution.py
+++ b/solution.py
@@ -200,8 +200,9 @@
         a = (qf + u).astype(BF)
         c = (qf + w).astype(BF)
         by = {n: gather(dot_nt(c, rk[n])) for n in range(max(i - 2, 0), i + 1)}
-        cols = jnp.concatenate([stats[i], jnp.zeros((H - 8, T), F32)], 0).T
-        m, inv, row_dot = cols[:, 0:1], cols[:, 1:2], cols[:, 2:3]
+        if i % 2 == 0:
+            cols = jnp.concatenate([stats[i // 2], jnp.zeros((H - 8, T), F32)], 0).T
+        m, inv, row_dot = [cols[:, r:r + 1] for r in range(HC * (i % 2), HC * (i % 2 + 1))]
         at, dot = a.T, d_outs[i].T
         for r in range(min(i + 1, 2)):
             n = i - r
@@ -219,7 +220,7 @@
     + [pltpu.VMEM((3, D, T), BF)] + [pltpu.VMEM((T, D), F32)] * 3)
 
 
-def kernel(xq, xd, xk, xv, bias_u, bias_w, rel, oq, odq, odk, odv, drk_out, du_out, dw_out, lx,
+def kernel(xq, xd, xk, xv, bias_u, bias_w, rel, out, drk_out, du_out, dw_out, lx,
            rin, rl, drk, pbuf, duw, duw_all, rk, rkr, bu, bw, lblk, lrk, lres, st_out, st_in,
            in_send, in_recv, in_loc, rl_recv, fw_send, fw_recv, out_send, out_recv, half_send, half_recv,
            fin_send, fin_recv, hop_send, hop_recv, rel_send, rel_recv, duw_send, duw_recv, rk_sem, px_send, px_recv,
@@ -231,15 +232,17 @@
     partner = jnp.bitwise_xor(me, 1)
     outer = (chip == 0) | (chip == last)
     ins = (xq, xd, xk, xv)
-    outs = (oq, odq, odk, odv)
     neighbours = (1, 2, 4)
 
     def remote(src, dst, ssem, rsem, dev):
         return pltpu.make_async_remote_copy(src_ref=src, dst_ref=dst, send_sem=ssem, recv_sem=rsem,
                                             device_id=(dev,), device_id_type=MESH)
 
-    def spot(arr, dev, n):
-        return arr.at[2 * (dev % 2) + n % 2, HC * (dev // 2) + n // 2]
+    def pair_of(dev, n):
+        return 2 * (dev % 2) + n % 2, HC * (dev // 2) + n // 2
+
+    def spot(a, dev, n):
+        return ins[a].at[pair_of(dev, n)]
 
     def send_in(n, mask):
         dev = jnp.bitwise_xor(me, mask)
@@ -250,7 +253,7 @@
                     dst, rsem, to = rl.at[n, core, a % 2], rl_recv.at[n], jnp.bitwise_xor(dev, 4)
                 else:
                     dst, rsem, to = rin.at[n, me, a], in_recv.at[n, mask], dev
-                remote(spot(ins[a], dev, n), dst, in_send.at[n, mask], rsem, to).start()
+                remote(spot(a, dev, n), dst, in_send.at[n, mask], rsem, to).start()
 
         for first in (0, 2):
             if mask < NU:
@@ -289,11 +292,16 @@
         return [remote(ins[a].at[pl.ds(2 * (1 - core), 2), heads], lx.at[a, :, heads], px_send.at[a], px_recv.at[a], partner)
                 for a in range(NA)]
 
+    barrier = pltpu.get_barrier_semaphore()
+    for mask in range(1, NT):
+        pl.semaphore_signal(barrier, inc=1, device_id=(jnp.bitwise_xor(me, mask),), device_id_type=MESH)
     rk_copy = pltpu.make_async_copy(rel.at[pl.ds(HC * chip, HC)], rk, rk_sem)
     rk_copy.start()
     for n in range(NU):
         for a in range(NA):
-            pltpu.make_async_copy(spot(ins[a], me, n), rin.at[n, me, a], in_loc.at[n]).start()
+            pltpu.make_async_copy(spot(a, me, n), rin.at[n, me, a], in_loc.at[n]).start()
+    pl.semaphore_wait(barrier, NT - 1)
+    for n in range(NU):
         if n < AHEAD:
             send_pair(n)
         if n == 0:
@@ -303,6 +311,7 @@
     bw[:] = bias_w[:].astype(F32)
     drk[:] = jnp.zeros_like(drk)
     duw[:] = jnp.zeros_like(duw)
+    st_out[:] = jnp.zeros_like(st_out)
     rk_copy.wait()
     flip = (lax.broadcasted_iota(jnp.int32, (T, T), 0) + lax.broadcasted_iota(jnp.int32, (T, T), 1) == T - 1).astype(BF)
     for k in range(HC):
@@ -319,9 +328,20 @@
         piece = part(jnp.bitwise_xor(chip, s) if arrived else chip, k, 0, NA)
         return remote(piece, piece, fin_send.at[k, s], fin_recv.at[k, s], jnp.bitwise_xor(me, neighbours[s]))
 
-    def hop(k, s, arrived=False):
-        piece = part(jnp.bitwise_xor(chip, last if arrived else s), k, 2 * (s - 1), 2)
+    def hop(k, s, whole, arrived=False):
+        span = (0, NA) if whole else (2 * (s - 1), 2)
+        piece = part(jnp.bitwise_xor(chip, last if arrived else s), k, *span)
         return remote(piece, piece, hop_send.at[k, s], hop_recv.at[k, s], jnp.bitwise_xor(me, neighbours[-s]))
+
+    def hops(k, s, sender, act):
+        @pl.when(sender)
+        def _():
+            act(k, s, False)
+
+        if s == 1:
+            @pl.when(~sender)
+            def _():
+                act(k, s, True)
 
     def relay(k, s, arrived=False):
         half = 1 - core if arrived else core
@@ -331,7 +351,7 @@
     def pass_on(k):
         for s in (1, 2):
             fin_copy(k, s, True).wait_recv()
-            hop(k, s).start()
+            hops(k, s, outer, lambda *args: hop(*args).start())
             relay(k, s).start()
 
     def made_there(first, dev, owner):
@@ -343,8 +363,7 @@
     def stat_copy(n, whole):
         if whole:
             return remote(st_out.at[n], st_in.at[0, n], st_send.at[n, 1], st_recv.at[0, n], 4 + core)
-        piece = pl.ds(2, 2)
-        return remote(st_out.at[n, piece], st_in.at[chip, n, piece], st_send.at[n, 0], st_recv.at[chip, n], 6 + core)
+        return remote(st_out.at[n, 1], st_in.at[chip, n, 1], st_send.at[n, 0], st_recv.at[chip, n], 6 + core)
 
     def after_softmax(n, i, m, inv, rd):
         first = jnp.where(chip == 0, 4, 6)
@@ -352,8 +371,11 @@
         @pl.when((i >= first) & (chip != last))
         def _():
             lane = lax.broadcasted_iota(jnp.int32, (T, H), 1)
-            table = jnp.where(lane == 0, m, jnp.where(lane == 1, inv, jnp.where(lane == 2, rd, 0.0)))
-            st_out[n, i - 4] = table.T[:8]
+            table = jnp.where(lane == 0, m, jnp.where(lane == 1, inv, rd)).T
+            for r in range(2):
+                @pl.when(i % 2 == r)
+                def _():
+                    st_out[n, i // 2 - 2, HC * r:HC * (r + 1)] = table[:HC]
 
         @pl.when((i == 6) & (chip != last))
         def _():
@@ -377,12 +399,11 @@
                 copies.append(pltpu.make_async_copy(src, lblk.at[sl, where, a], l_sem.at[sl, a, r]))
         return copies
 
-    def local_sends(x, c):
+    def local_send(x, c):
         sl = x % 2
         _, _, bat, head = local_pair(x)
-        dsts = outs[2 * (c // 2):]
-        return [remote(lres.at[sl, 1 - core, a], dsts[a].at[bat, head], lr_send.at[sl, a], lr_recv, partner)
-                for a in range(2)]
+        dst = out.at[pl.ds(2 * (c // 2), 2), bat, head]
+        return remote(lres.at[sl, 1 - core], dst, lr_send.at[sl], lr_recv, partner)
 
     def local_work(lo, hi, c):
         for copy in local_loads(lo, lo % 2):
@@ -401,8 +422,7 @@
 
             @pl.when(x > 1)
             def _():
-                for copy in local_sends(x, c):
-                    copy.wait_send()
+                local_send(x, c).wait_send()
 
             owner, n, bat, head = local_pair(x)
             u = bu[pl.ds(head, 1)]
@@ -419,20 +439,21 @@
                     for a in range(2):
                         lres[sl, r, a] = res[a]
             else:
-                piece = st_in.at[owner, n]
-                if c == last:
-                    piece = st_in.at[owner, n, pl.ds(2, 2)]
-                else:
+                groups = (1,)
+                piece = st_in.at[owner, n, 1]
+                if c != last:
+                    groups = (0, 1)
+                    piece = st_in.at[owner, n]
                     q = q + [rl[n, r, 0] for r in range(2)]
                     do = do + [rl[n, r, 1] for r in range(2)]
                 remote(piece, piece, st_send.at[n, 0], st_recv.at[owner, n], 2 * owner + core).wait_recv()
-                for a, res in enumerate(col_tiles(q, do, key, val, table, piece, u, w)):
+                stats = [st_in[owner, n, g] for g in groups]
+                for a, res in enumerate(col_tiles(q, do, key, val, table, stats, u, w)):
                     for r in range(2):
                         lres[sl, r, a] = res[r]
-            for copy in local_sends(x, c):
-                copy.start()
+            local_send(x, c).start()
             for a in range(2):
-                outs[2 * (c // 2) + a][bat, head] = lres[sl, core, a]
+                out[2 * (c // 2) + a, bat, head] = lres[sl, core, a]
             return 0
 
         lax.fori_loop(lo, hi, one, 0)
@@ -451,14 +472,14 @@
         for first in (0, 2):
             @pl.when((mask != 0) & ~made_there(first, i, chip))
             def _():
-                for a in (first, first + 1):
-                    remote(rin.at[n, i, a], spot(outs[a], me, n), out_send.at[n, i, first // 2],
-                           out_recv.at[n, mask, first // 2], i).start()
+                two = pl.ds(first, 2)
+                remote(rin.at[n, i, two], out.at[(two,) + pair_of(me, n)], out_send.at[n, i, first // 2],
+                       out_recv.at[n, mask, first // 2], i).start()
 
         @pl.when(mask == 0)
         def _():
             for a in range(NA):
-                spot(outs[a], me, n)[:] = rin[n, i, a]
+                out[(a,) + pair_of(me, n)] = rin[n, i, a]
 
     def run_unit(n, _):
         k = n // 2
@@ -529,7 +550,7 @@
     pass_on(2)
     for k in range(HC):
         for s in (1, 2):
-            hop(k, s, True).wait_recv()
+            hops(k, s, ~outer, lambda *args: hop(*args, True).wait_recv())
         relay(k, last).start()
 
     for mask in range(1, NT):
@@ -537,8 +558,8 @@
         duw_copy(mask, True).wait_recv()
     for h in range(NH):
         both = duw_all[2 * (h // HC), h % HC] + duw_all[2 * (h // HC) + 1, h % HC]
-        for r, out in enumerate((du_out, dw_out)):
-            out[h:h + 1] = both[r:r + 1]
+        for r, bias_out in enumerate((du_out, dw_out)):
+            bias_out[h:h + 1] = both[r:r + 1]
 
     def finish(n, _):
         for mask in range(1, NT):
@@ -576,10 +597,9 @@
             copy.wait_send()
         count = local_count(c)
         for x in (count - 2, count - 1):
-            for copy in local_sends(x, c):
-                copy.wait_send()
-        whole = oq.at[pl.ds(0, count // NU)]
-        remote(whole, whole, lr_send.at[0, 0], lr_recv, partner).wait_recv()
+            local_send(x, c).wait_send()
+        whole = out.at[0, pl.ds(0, count // NU)]
+        remote(whole, whole, lr_send.at[0], lr_recv, partner).wait_recv()
 
     at_chip(end_local)
     for k in range(HC):
@@ -588,7 +608,7 @@
         remote(theirs, theirs, fin_send.at[k, 0], fin_recv.at[k, 0], partner).wait_recv()
         for s in (1, 2):
             fin_copy(k, s).wait_send()
-            hop(k, s).wait_send()
+            hops(k, s, outer, lambda *args: hop(*args).wait_send())
         for s in (1, 2, last):
             relay(k, s).wait_send()
             relay(k, s, True).wait_recv()
@@ -598,7 +618,7 @@
     any_spec = pl.BlockSpec(memory_space=pl.ANY)
     vmem_spec = pl.BlockSpec(memory_space=pltpu.VMEM)
     dma = pltpu.SemaphoreType.DMA
-    act = pltpu.VMEM((NA, NH, T, D), BF)
+    acts = pltpu.VMEM((NA, NA, NH, T, D), BF)
     bias = pltpu.VMEM((NH, D), F32)
     heads = pltpu.VMEM((HC, NT, T, D), BF)
     per_head = dma((HC, NA))
@@ -607,28 +627,28 @@
     per_half = dma((NU, NT, 2))
     return pl.pallas_call(
         kernel,
-        out_shape=(act, act, act, act, pltpu.VMEM((NH, NT, T, D), F32), bias, bias,
+        out_shape=(acts, pltpu.VMEM((NH, NT, T, D), F32), bias, bias,
                    jax.ShapeDtypeStruct((NA, 2, NH, T, D), BF)),
         in_specs=[any_spec] * 4 + [vmem_spec] * 2 + [any_spec],
-        out_specs=(vmem_spec,) * 7 + (any_spec,),
+        out_specs=(vmem_spec,) * 4 + (any_spec,),
         scratch_shapes=[
             pltpu.VMEM((NU, NT, NA, T, D), BF), pltpu.VMEM((NU, 2, 2, T, D), BF), pltpu.VMEM((HC, NT, D, T), F32),
             pltpu.VMEM((HC, NA, D, T), F32), pltpu.VMEM((HC, 8, D), F32), pltpu.VMEM((NT, HC, 8, D), F32),
             heads, heads, bias, bias,
             pltpu.VMEM((2, 2, NA, T, D), BF), pltpu.VMEM((2, NA, T, D), BF), pltpu.VMEM((2, 2, 2, T, D), BF),
-            pltpu.VMEM((NU, NA, 8, T), F32), pltpu.VMEM((HC, NU, NA, 8, T), F32),
+            pltpu.VMEM((NU, 2, 8, T), F32), pltpu.VMEM((HC, NU, 2, 8, T), F32),
             per_peer, per_peer, per_pair, per_pair, per_pair, per_pair, per_half, per_half, dma((HC,)), dma((HC,)),
             per_head, per_head, per_head, per_head, per_head, per_head, dma((NT,)), dma((NT,)), dma(()), dma((NA,)),
-            dma((NA,)), dma((NU, 2)), dma((HC, NU)), dma((2, NA, HC)), dma((2, 2)), dma(())]
+            dma((NA,)), dma((NU, 2)), dma((HC, NU)), dma((2, NA, HC)), dma((2,)), dma(())]
         + UNIT_SCRATCH,
-        compiler_params=pltpu.CompilerParams(has_side_effects=True, vmem_limit_bytes=VMEM_LIMIT),
+        compiler_params=pltpu.CompilerParams(collective_id=0, has_side_effects=True, vmem_limit_bytes=VMEM_LIMIT),
     )(xq, xd, xk, xv, bias_u, bias_w, rel)
 
 
-def write_kernel(*refs):
-    half = len(refs) // 2
+def write_kernel(acts, table, bias_u, bias_w, *refs):
     sem = refs[-1]
-    copies = [pltpu.make_async_copy(refs[n], refs[half + n], sem.at[n]) for n in range(half)]
+    srcs = [acts.at[a] for a in range(NA)] + [table, bias_u, bias_w]
+    copies = [pltpu.make_async_copy(src, dst, sem.at[n]) for n, (src, dst) in enumerate(zip(srcs, refs[:-1]))]
     for copy in copies:
         copy.start()
     for copy in copies:
@@ -636,12 +656,14 @@
 
 
 def write_out(arrs):
+    shapes = [arrs[0].shape[1:]] * NA + [arr.shape for arr in arrs[1:]]
+    types = [arrs[0].dtype] * NA + [arr.dtype for arr in arrs[1:]]
     return pl.pallas_call(
         write_kernel,
-        out_shape=tuple(jax.ShapeDtypeStruct(arr.shape, arr.dtype) for arr in arrs),
+        out_shape=tuple(map(jax.ShapeDtypeStruct, shapes, types)),
         in_specs=[pl.BlockSpec(memory_space=pltpu.VMEM)] * len(arrs),
-        out_specs=(pl.BlockSpec(memory_space=pl.ANY),) * len(arrs),
-        scratch_shapes=[pltpu.SemaphoreType.DMA((len(arrs),))],
+        out_specs=(pl.BlockSpec(memory_space=pl.ANY),) * len(shapes),
+        scratch_shapes=[pltpu.SemaphoreType.DMA((len(shapes),))],
         compiler_params=pltpu.CompilerParams(vmem_limit_bytes=1024 * 1024),
     )(*[pltpu.with_memory_space_constraint(arr, pltpu.VMEM) for arr in arrs])
 
@@ -655,7 +677,7 @@
 
         rel = rel_k.transpose(1, 0, 2).reshape(NH, NT, T, D)
         acts = [by_head(arr) for arr in (query, d_out, key_in, value)]
-        res = write_out(exchange_attend(*acts, bias_u, bias_w, rel)[:7])
+        res = write_out(exchange_attend(*acts, bias_u, bias_w, rel)[:4])
         d_rel = res[4].reshape(NH, NT * T, D).transpose(1, 0, 2)
         return tuple(by_head(arr) for arr in res[:4]) + (res[5], res[6], d_rel)
 

time: 313 us -> 310 us (level)
  no operation moved by 1% of the time
where the time goes in v7:
time: 310 us
  Pallas kernels  309 us (100%)
    pallas_call x1, Pallas kernels, exchange_attend(): pl.pallas_call(kernel, out_shape=(acts, pltpu.VMEM((NH, NT, T, D), F32),...  301 us
    pallas_call x1, Pallas kernels, write_out(): pl.pallas_call(write_kernel, out_shape=tuple(map(jax.ShapeDtypeStruct, sh...  8.81 us

profile of v7, /device:TPU:0, one launch (start us, length us, event | category | flops | bytes accessed | tf_op | source)
XLA Modules:
  0.0 310.2 jit_solution(10987203755697311585)
XLA Ops:
  0.6 300.6 %shard_map.126 = (bf16[4,4,12,256,128]{4,3,2,1,0:T(8,128)(2,1)S(1)}, f32[12,8,256,128]{3,2,1,0:T(8,128)S(1)}, f32[12,128]{1,0:T(8,128)S(1)}, f32[12,128]{1,0:T(8,128)S(1)}, bf16[4,2,12,256,128]{4,3,2,1,0:T(8,128)(2,1)}) custom-call(bf16[4,12,256,128]{3,2,1,0:T(8,128)(2,1)} %bitcast.15, bf16[4,12,256,128]{3,2,1,0:T(8,128)(2,1)} %bitcast.16, ...), custom_call_target="tpu_custom_call" | custom-call | tf_op jit(solution)/shard_map/pallas_call | solution.py:628
  301.3 8.8 %shard_map.127 = (bf16[4,12,256,128]{3,2,1,0:T(8,128)(2,1)}, bf16[4,12,256,128]{3,2,1,0:T(8,128)(2,1)}, bf16[4,12,256,128]{3,2,1,0:T(8,128)(2,1)}, bf16[4,12,256...) custom-call(bf16[4,4,12,256,128]{4,3,2,1,0:T(8,128)(2,1)S(1)} %get-tuple-element.18.a, ...), custom_call_target="tpu_custom_call" | custom-call | tf_op jit(solution)/shard_map/pallas_call | solution.py:661

commit v8 on v7

--- a/solution.py
+++ b/solution.py
@@ -14,7 +14,10 @@
 HC = 3
 NH = 12
 EARLY = 6
+GROUPS = ((0, 1), (1, 1), (2, 2), (4, 2))
 AHEAD = 3
+SEND_AT = 1
+FORWARD_AT = (0, 0, 1, 3)
 VMEM_LIMIT = 39 * 1024 * 1024
 F32 = jnp.float32
 BF = jnp.bfloat16
@@ -221,10 +224,10 @@
 
 
 def kernel(xq, xd, xk, xv, bias_u, bias_w, rel, out, drk_out, du_out, dw_out, lx,
-           rin, rl, drk, pbuf, duw, duw_all, rk, rkr, bu, bw, lblk, lrk, lres, st_out, st_in,
-           in_send, in_recv, in_loc, rl_recv, fw_send, fw_recv, out_send, out_recv, half_send, half_recv,
-           fin_send, fin_recv, hop_send, hop_recv, rel_send, rel_recv, duw_send, duw_recv, rk_sem, px_send, px_recv,
-           st_send, st_recv, l_sem, lr_send, lr_recv, *scratch):
+           rin, rl, drk, pbuf, duw, duw_all, rk, rkr, bias, bu, bw, lblk, lrk, lres, st_out, st_in,
+           in_recv, rl_recv, st_recv, half_send, half_recv, fin_recv, hop_recv, l_sem, lr_send,
+           in_send, in_loc, fw_send, out_send, out_recv, table_send, table_recv, duw_send, duw_recv, rk_sem, px_send,
+           px_recv, st_send, st_send_all, lr_recv, *scratch):
     me = lax.axis_index('cp')
     chip = me // 2
     core = me % 2
@@ -244,16 +247,20 @@
     def spot(a, dev, n):
         return ins[a].at[pair_of(dev, n)]
 
-    def send_in(n, mask):
+    def pairs(n, count):
+        return pl.ds(n, count) if count > 1 else n
+
+    def send_in(n, count, mask):
         dev = jnp.bitwise_xor(me, mask)
+        bat, head = pair_of(dev, n)
 
         def send(first, via):
             for a in (first, first + 1):
                 if via:
-                    dst, rsem, to = rl.at[n, core, a % 2], rl_recv.at[n], jnp.bitwise_xor(dev, 4)
+                    dst, rsem, to = rl.at[pairs(n, count), core, a % 2], rl_recv.at[n], jnp.bitwise_xor(dev, 4)
                 else:
-                    dst, rsem, to = rin.at[n, me, a], in_recv.at[n, mask], dev
-                remote(spot(a, dev, n), dst, in_send.at[n, mask], rsem, to).start()
+                    dst, rsem, to = rin.at[pairs(n, count), me, a], in_recv.at[n], dev
+                remote(ins[a].at[pairs(bat, count), head], dst, in_send, rsem, to).start()
 
         for first in (0, 2):
             if mask < NU:
@@ -265,22 +272,22 @@
                     def _():
                         send(first, via)
 
-    def send_pair(n):
+    def send_group(n, count):
         for mask in (6, 2, 4, 7, 3, 5, 1):
-            send_in(n, mask)
-
-    def in_wait(n, mask, size=NA):
-        dev = jnp.bitwise_xor(me, mask)
-        piece = rin.at[n, dev, pl.ds(0, size)]
-        return remote(piece, piece, in_send.at[n, mask], in_recv.at[n, mask], dev)
-
-    def forward(n):
-        dst = rin.at[n, pl.ds(2 * jnp.bitwise_xor(chip, 1), 2), pl.ds(2 * (chip % 2), 2)]
-        return remote(rl.at[n], dst, fw_send.at[n], fw_recv.at[n], jnp.bitwise_xor(me, 4))
-
-    def pass_forward(n):
-        remote(rl.at[n], rl.at[n], fw_send.at[n], rl_recv.at[n], jnp.bitwise_xor(me, 2)).wait_recv()
-        forward(n).start()
+            send_in(n, count, mask)
+
+    def forward(n, count):
+        dst = rin.at[pairs(n, count), pl.ds(2 * jnp.bitwise_xor(chip, 1), 2), pl.ds(2 * (chip % 2), 2)]
+        return remote(rl.at[pairs(n, count)], dst, fw_send, in_recv.at[n], jnp.bitwise_xor(me, 4))
+
+    def pass_forward(n, count):
+        piece = rl.at[pairs(n, count)]
+        remote(piece, piece, fw_send, rl_recv.at[n], jnp.bitwise_xor(me, 2)).wait_recv()
+        forward(n, count).start()
+
+    def arrive(n, count):
+        piece = rin.at[pairs(n, count), pl.ds(0, NT - 1)]
+        remote(piece, piece, in_send, in_recv.at[n], partner).wait_recv()
 
     def at_chip(act):
         for c, heads in enumerate(((3, 9), (9, 3), (0, 3), (0, 9))):
@@ -288,31 +295,38 @@
             def _():
                 act(c, pl.ds(*heads))
 
+    def pair_wait(heads, wait):
+        piece = lx.at[:, :, heads]
+        getattr(remote(piece, piece, px_send, px_recv, partner), wait)()
+
     def pair_copies(heads):
-        return [remote(ins[a].at[pl.ds(2 * (1 - core), 2), heads], lx.at[a, :, heads], px_send.at[a], px_recv.at[a], partner)
+        return [remote(ins[a].at[pl.ds(2 * (1 - core), 2), heads], lx.at[a, :, heads], px_send, px_recv, partner)
                 for a in range(NA)]
 
     barrier = pltpu.get_barrier_semaphore()
     for mask in range(1, NT):
         pl.semaphore_signal(barrier, inc=1, device_id=(jnp.bitwise_xor(me, mask),), device_id_type=MESH)
-    rk_copy = pltpu.make_async_copy(rel.at[pl.ds(HC * chip, HC)], rk, rk_sem)
-    rk_copy.start()
+    copies = [pltpu.make_async_copy(bias_u, bias.at[0], rk_sem.at[0]), pltpu.make_async_copy(bias_w, bias.at[1], rk_sem.at[1]),
+              pltpu.make_async_copy(rel.at[pl.ds(HC * chip, HC)], rk, rk_sem.at[2])]
+    for copy in copies:
+        copy.start()
     for n in range(NU):
         for a in range(NA):
-            pltpu.make_async_copy(spot(a, me, n), rin.at[n, me, a], in_loc.at[n]).start()
+            pltpu.make_async_copy(spot(a, me, n), rin.at[n, me, a], in_loc).start()
     pl.semaphore_wait(barrier, NT - 1)
-    for n in range(NU):
-        if n < AHEAD:
-            send_pair(n)
-        if n == 0:
+    for g, (n, count) in enumerate(GROUPS):
+        if g < AHEAD:
+            send_group(n, count)
+        if g == 0:
             at_chip(lambda c, heads: [copy.start() for copy in pair_copies(heads)])
 
-    bu[:] = bias_u[:].astype(F32)
-    bw[:] = bias_w[:].astype(F32)
+    for copy in copies:
+        copy.wait()
+    bu[:] = bias[0].astype(F32)
+    bw[:] = bias[1].astype(F32)
     drk[:] = jnp.zeros_like(drk)
     duw[:] = jnp.zeros_like(duw)
     st_out[:] = jnp.zeros_like(st_out)
-    rk_copy.wait()
     flip = (lax.broadcasted_iota(jnp.int32, (T, T), 0) + lax.broadcasted_iota(jnp.int32, (T, T), 1) == T - 1).astype(BF)
     for k in range(HC):
         for n in range(NT):
@@ -326,44 +340,43 @@
 
     def fin_copy(k, s, arrived=False):
         piece = part(jnp.bitwise_xor(chip, s) if arrived else chip, k, 0, NA)
-        return remote(piece, piece, fin_send.at[k, s], fin_recv.at[k, s], jnp.bitwise_xor(me, neighbours[s]))
-
-    def hop(k, s, whole, arrived=False):
-        span = (0, NA) if whole else (2 * (s - 1), 2)
-        piece = part(jnp.bitwise_xor(chip, last if arrived else s), k, *span)
-        return remote(piece, piece, hop_send.at[k, s], hop_recv.at[k, s], jnp.bitwise_xor(me, neighbours[-s]))
-
-    def hops(k, s, sender, act):
-        @pl.when(sender)
-        def _():
-            act(k, s, False)
+        rsem = fin_recv.at[k, s - 1] if s else table_recv
+        return remote(piece, piece, table_send, rsem, jnp.bitwise_xor(me, neighbours[s]))
+
+    def hop(k, s, whole):
+        piece = part(jnp.bitwise_xor(chip, s), k, *((0, NA) if whole else (2 * (s - 1), 2)))
+        return remote(piece, piece, table_send, hop_recv.at[k], jnp.bitwise_xor(me, neighbours[-s]))
+
+    def hops(k, s):
+        @pl.when(outer)
+        def _():
+            hop(k, s, False).start()
 
         if s == 1:
-            @pl.when(~sender)
+            @pl.when(~outer)
             def _():
-                act(k, s, True)
-
-    def relay(k, s, arrived=False):
-        half = 1 - core if arrived else core
-        piece = drk_out.at[HC * jnp.bitwise_xor(chip, s) + k, pl.ds(NA * half, NA)]
-        return remote(piece, piece, rel_send.at[k, s], rel_recv.at[k, s], partner)
+                hop(k, s, True).start()
+
+    def relay(k, s):
+        piece = part(jnp.bitwise_xor(chip, s), k, 0, NA)
+        return remote(piece, piece, table_send, table_recv, partner)
 
     def pass_on(k):
         for s in (1, 2):
             fin_copy(k, s, True).wait_recv()
-            hops(k, s, outer, lambda *args: hop(*args).start())
+            hops(k, s)
             relay(k, s).start()
 
-    def made_there(first, dev, owner):
+    def sent_parts(dev, owner):
         there = dev // 2
-        if first:
-            return ((there == last) & (owner != last)) | ((there == 2) & (owner == 0))
-        return ((there == 0) & (owner != 0)) | ((there == 1) & (owner == last))
+        rows = ((there == 0) & (owner != 0)) | ((there == 1) & (owner == last))
+        cols = ((there == last) & (owner != last)) | ((there == 2) & (owner == 0))
+        return ((0, NA), ~rows & ~cols), ((2, 2), rows), ((0, 2), cols)
 
     def stat_copy(n, whole):
         if whole:
-            return remote(st_out.at[n], st_in.at[0, n], st_send.at[n, 1], st_recv.at[0, n], 4 + core)
-        return remote(st_out.at[n, 1], st_in.at[chip, n, 1], st_send.at[n, 0], st_recv.at[chip, n], 6 + core)
+            return remote(st_out.at[n], st_in.at[0, n], st_send_all, st_recv.at[n], 4 + core)
+        return remote(st_out.at[n, 1], st_in.at[chip, n, 1], st_send, st_recv.at[n], 6 + core)
 
     def after_softmax(n, i, m, inv, rd):
         first = jnp.where(chip == 0, 4, 6)
@@ -392,11 +405,11 @@
 
     def local_loads(x, sl):
         _, n, bat, head = local_pair(x)
-        copies = [pltpu.make_async_copy(rel.at[head, pl.ds(0, NA)], lrk.at[sl], l_sem.at[sl, 0, 2])]
+        copies = [pltpu.make_async_copy(rel.at[head, pl.ds(0, NA)], lrk.at[sl], l_sem.at[sl])]
         for a in range(NA):
             for r, src in enumerate((ins[a].at[bat, head], lx.at[a, n % 2, head])):
                 where = core if r == 0 else 1 - core
-                copies.append(pltpu.make_async_copy(src, lblk.at[sl, where, a], l_sem.at[sl, a, r]))
+                copies.append(pltpu.make_async_copy(src, lblk.at[sl, where, a], l_sem.at[sl]))
         return copies
 
     def local_send(x, c):
@@ -417,8 +430,7 @@
                 for copy in local_loads(x + 1, 1 - sl):
                     copy.start()
 
-            for copy in local_loads(x, sl):
-                copy.wait()
+            pltpu.make_async_copy(rin.at[0, pl.ds(0, HC)], rin.at[0, pl.ds(0, HC)], l_sem.at[sl]).wait()
 
             @pl.when(x > 1)
             def _():
@@ -440,13 +452,17 @@
                         lres[sl, r, a] = res[a]
             else:
                 groups = (1,)
-                piece = st_in.at[owner, n, 1]
+                piece = st_in.at[:, n, 1]
                 if c != last:
                     groups = (0, 1)
-                    piece = st_in.at[owner, n]
+                    piece = st_in.at[0, n]
                     q = q + [rl[n, r, 0] for r in range(2)]
                     do = do + [rl[n, r, 1] for r in range(2)]
-                remote(piece, piece, st_send.at[n, 0], st_recv.at[owner, n], 2 * owner + core).wait_recv()
+
+                @pl.when((owner == 0) | (c != last))
+                def _():
+                    remote(piece, piece, st_send, st_recv.at[n], partner).wait_recv()
+
                 stats = [st_in[owner, n, g] for g in groups]
                 for a, res in enumerate(col_tiles(q, do, key, val, table, stats, u, w)):
                     for r in range(2):
@@ -463,18 +479,16 @@
 
     @pl.when(chip == 0)
     def _():
-        for copy in pair_copies(pl.ds(3, 9)):
-            copy.wait_recv()
+        pair_wait(pl.ds(3, 9), "wait_recv")
         local_work(0, EARLY, 0)
 
     def send_tile(n, i):
         mask = jnp.bitwise_xor(me, i)
-        for first in (0, 2):
-            @pl.when((mask != 0) & ~made_there(first, i, chip))
+        for span, sent in sent_parts(i, chip):
+            @pl.when((mask != 0) & sent)
             def _():
-                two = pl.ds(first, 2)
-                remote(rin.at[n, i, two], out.at[(two,) + pair_of(me, n)], out_send.at[n, i, first // 2],
-                       out_recv.at[n, mask, first // 2], i).start()
+                some = pl.ds(*span)
+                remote(rin.at[n, i, some], out.at[(some,) + pair_of(me, n)], out_send, out_recv, i).start()
 
         @pl.when(mask == 0)
         def _():
@@ -484,32 +498,24 @@
     def run_unit(n, _):
         k = n // 2
 
-        @pl.when(n + AHEAD < NU)
-        def _():
-            send_pair(n + AHEAD)
-
-        @pl.when(~outer & (n == 0))
-        def _():
-            pass_forward(0)
-
-        @pl.when(~outer & (n + 1 < NU))
-        def _():
-            pass_forward(n + 1)
-
-        pltpu.make_async_copy(rin.at[n, me], rin.at[n, me], in_loc.at[n]).wait()
-        for mask in range(1, NT):
-            if mask < NU:
-                in_wait(n, mask).wait_recv()
-            else:
-                for split in (True, False):
-                    @pl.when(outer == split)
-                    def _():
-                        in_wait(n, mask, 2 if split else NA).wait_recv()
-
-        @pl.when(outer)
-        def _():
-            piece = rin.at[n, pl.ds(0, 2), pl.ds(0, 2)]
-            remote(piece, piece, fw_send.at[n], fw_recv.at[n], jnp.bitwise_xor(me, 4)).wait_recv()
+        for g, group in enumerate(GROUPS):
+            if g >= AHEAD:
+                @pl.when(n == SEND_AT)
+                def _():
+                    send_group(*group)
+
+            @pl.when(~outer & (n == FORWARD_AT[g]))
+            def _():
+                pass_forward(*group)
+
+        @pl.when(n == 0)
+        def _():
+            pltpu.make_async_copy(rin.at[:, me], rin.at[:, me], in_loc).wait()
+
+        for group in GROUPS:
+            @pl.when(n == group[0])
+            def _():
+                arrive(*group)
 
         head = pl.ds(HC * chip + k, 1)
         unit(rin.at[n], rk.at[k], rkr.at[k], bu[head], bw[head], drk.at[k], duw.at[k], scratch,
@@ -532,69 +538,54 @@
     pass_on(0)
     pass_on(1)
 
-    def duw_copy(mask, arrived):
-        dev = jnp.bitwise_xor(me, mask)
-        return remote(duw, duw_all.at[dev if arrived else me], duw_send.at[mask], duw_recv.at[mask], dev)
-
     for mask in range(1, NT):
-        duw_copy(mask, False).start()
+        remote(duw, duw_all.at[me], duw_send, duw_recv, jnp.bitwise_xor(me, mask)).start()
     duw_all[me] = duw[:]
 
     def late_work(c, heads):
         if c:
-            for copy in pair_copies(heads):
-                copy.wait_recv()
+            pair_wait(heads, "wait_recv")
         local_work(0 if c else EARLY, local_count(c), c)
 
     at_chip(late_work)
     pass_on(2)
     for k in range(HC):
-        for s in (1, 2):
-            hops(k, s, ~outer, lambda *args: hop(*args, True).wait_recv())
+        far = part(jnp.bitwise_xor(chip, last), k, 0, NA)
+        remote(far, far, table_send, hop_recv.at[k], partner).wait_recv()
         relay(k, last).start()
 
-    for mask in range(1, NT):
-        duw_copy(mask, False).wait_send()
-        duw_copy(mask, True).wait_recv()
+    others = duw_all.at[pl.ds(0, NT - 1)]
+    remote(others, others, duw_send, duw_recv, partner).wait()
     for h in range(NH):
         both = duw_all[2 * (h // HC), h % HC] + duw_all[2 * (h // HC) + 1, h % HC]
         for r, bias_out in enumerate((du_out, dw_out)):
             bias_out[h:h + 1] = both[r:r + 1]
 
-    def finish(n, _):
-        for mask in range(1, NT):
-            dev = jnp.bitwise_xor(me, mask)
-            in_wait(n, mask).wait_send()
-            for first in (0, 2):
-                both = rin.at[n, dev, pl.ds(first, 2)]
-                copy = remote(both, both, out_send.at[n, dev, first // 2], out_recv.at[n, mask, first // 2], dev)
-
-                @pl.when(~made_there(first, dev, chip))
-                def _():
-                    copy.wait_send()
-
-                @pl.when(~made_there(first, me, dev // 2))
-                def _():
-                    copy.wait_recv()
-
-        @pl.when(~outer)
-        def _():
-            forward(n).wait_send()
-
-        @pl.when(chip != last)
-        def _():
-            stat_copy(n, False).wait_send()
-
-        @pl.when(chip == 0)
-        def _():
-            stat_copy(n, True).wait_send()
-        return 0
-
-    lax.fori_loop(0, NU, finish, 0)
+    sent = rin.at[:, pl.ds(0, NT - 1)]
+    remote(sent, sent, in_send, in_recv.at[0], partner).wait_send()
+    sent = rin.at[:, pl.ds(0, 5)]
+    remote(sent, sent, out_send, out_recv, partner).wait_send()
+    for inner, count in ((True, 6), (False, 4)):
+        @pl.when(outer != inner)
+        def _():
+            got = rin.at[:, pl.ds(0, count)]
+            remote(got, got, out_send, out_recv, partner).wait_recv()
+
+    @pl.when(~outer)
+    def _():
+        remote(rl, rl, fw_send, in_recv.at[0], partner).wait_send()
+
+    @pl.when(chip != last)
+    def _():
+        some = st_out.at[:, 1]
+        remote(some, some, st_send, st_recv.at[0], partner).wait_send()
+
+    @pl.when(chip == 0)
+    def _():
+        remote(st_out, st_out, st_send_all, st_recv.at[0], partner).wait_send()
 
     def end_local(c, heads):
-        for copy in pair_copies(heads):
-            copy.wait_send()
+        pair_wait(heads, "wait_send")
         count = local_count(c)
         for x in (count - 2, count - 1):
             local_send(x, c).wait_send()
@@ -602,16 +593,9 @@
         remote(whole, whole, lr_send.at[0], lr_recv, partner).wait_recv()
 
     at_chip(end_local)
-    for k in range(HC):
-        fin_copy(k, 0).wait_send()
-        theirs = drk_out.at[HC * chip + k, pl.ds(NA * (1 - core), NA)]
-        remote(theirs, theirs, fin_send.at[k, 0], fin_recv.at[k, 0], partner).wait_recv()
-        for s in (1, 2):
-            fin_copy(k, s).wait_send()
-            hops(k, s, outer, lambda *args: hop(*args).wait_send())
-        for s in (1, 2, last):
-            relay(k, s).wait_send()
-            relay(k, s, True).wait_recv()
+    sent, got = drk_out.at[:, pl.ds(0, NT - 1)], drk_out.at[:, pl.ds(0, NA)]
+    remote(sent, sent, table_send, table_recv, partner).wait_send()
+    remote(got, got, table_send, table_recv, partner).wait_recv()
 
 
 def exchange_attend(xq, xd, xk, xv, bias_u, bias_w, rel):
@@ -621,25 +605,24 @@
     acts = pltpu.VMEM((NA, NA, NH, T, D), BF)
     bias = pltpu.VMEM((NH, D), F32)
     heads = pltpu.VMEM((HC, NT, T, D), BF)
-    per_head = dma((HC, NA))
     per_pair = dma((NU,))
-    per_peer = dma((NU, NT))
-    per_half = dma((NU, NT, 2))
+    per_head = dma((HC,))
+    two = dma((2,))
+    one = dma(())
     return pl.pallas_call(
         kernel,
         out_shape=(acts, pltpu.VMEM((NH, NT, T, D), F32), bias, bias,
                    jax.ShapeDtypeStruct((NA, 2, NH, T, D), BF)),
-        in_specs=[any_spec] * 4 + [vmem_spec] * 2 + [any_spec],
+        in_specs=[any_spec] * 7,
         out_specs=(vmem_spec,) * 4 + (any_spec,),
         scratch_shapes=[
             pltpu.VMEM((NU, NT, NA, T, D), BF), pltpu.VMEM((NU, 2, 2, T, D), BF), pltpu.VMEM((HC, NT, D, T), F32),
             pltpu.VMEM((HC, NA, D, T), F32), pltpu.VMEM((HC, 8, D), F32), pltpu.VMEM((NT, HC, 8, D), F32),
-            heads, heads, bias, bias,
+            heads, heads, pltpu.VMEM((2, NH, D), BF), bias, bias,
             pltpu.VMEM((2, 2, NA, T, D), BF), pltpu.VMEM((2, NA, T, D), BF), pltpu.VMEM((2, 2, 2, T, D), BF),
             pltpu.VMEM((NU, 2, 8, T), F32), pltpu.VMEM((HC, NU, 2, 8, T), F32),
-            per_peer, per_peer, per_pair, per_pair, per_pair, per_pair, per_half, per_half, dma((HC,)), dma((HC,)),
-            per_head, per_head, per_head, per_head, per_head, per_head, dma((NT,)), dma((NT,)), dma(()), dma((NA,)),
-            dma((NA,)), dma((NU, 2)), dma((HC, NU)), dma((2, NA, HC)), dma((2,)), dma(())]
+            per_pair, per_pair, per_pair, per_head, per_head, dma((HC, 2)), per_head, two, two]
+        + [one] * 9 + [per_head] + [one] * 5
         + UNIT_SCRATCH,
         compiler_params=pltpu.CompilerParams(collective_id=0, has_side_effects=True, vmem_limit_bytes=VMEM_LIMIT),
     )(xq, xd, xk, xv, bias_u, bias_w, rel)

time: 310 us -> 306 us (0.987)
  Pallas kernels: 309 us -> 304 us
    pallas_call x1, Pallas kernels: 301 us -> 295 us  [exchange_attend(): pl.pallas_call(kernel, out_shape=(acts, pltpu.VMEM((NH, NT, T, D), F32),...]
where the time goes in v8:
time: 306 us; the launch traced here: 304 us
  Pallas kernels  304 us (99%)
    pallas_call x1, Pallas kernels, exchange_attend(): pl.pallas_call(kernel, out_shape=(acts, pltpu.VMEM((NH, NT, T, D), F32),...  295 us
    pallas_call x1, Pallas kernels, write_out(): pl.pallas_call(write_kernel, out_shape=tuple(map(jax.ShapeDtypeStruct, sh...  8.81 us

profile of v8, /device:TPU:0, one launch (start us, length us, event | category | flops | bytes accessed | tf_op | source)
XLA Modules:
  0.0 304.3 jit_solution(18109685150957790683)
XLA Ops:
  0.6 294.7 %shard_map.126 = (bf16[4,4,12,256,128]{4,3,2,1,0:T(8,128)(2,1)S(1)}, f32[12,8,256,128]{3,2,1,0:T(8,128)S(1)}, f32[12,128]{1,0:T(8,128)S(1)}, f32[12,128]{1,0:T(8,128)S(1)}, bf16[4,2,12,256,128]{4,3,2,1,0:T(8,128)(2,1)}) custom-call(bf16[4,12,256,128]{3,2,1,0:T(8,128)(2,1)} %bitcast.15, bf16[4,12,256,128]{3,2,1,0:T(8,128)(2,1)} %bitcast.16, ...), custom_call_target="tpu_custom_call" | custom-call | tf_op jit(solution)/shard_map/pallas_call | solution.py:612
  295.4 8.8 %shard_map.127 = (bf16[4,12,256,128]{3,2,1,0:T(8,128)(2,1)}, bf16[4,12,256,128]{3,2,1,0:T(8,128)(2,1)}, bf16[4,12,256,128]{3,2,1,0:T(8,128)(2,1)}, bf16[4,12,256...) custom-call(bf16[4,4,12,256,128]{4,3,2,1,0:T(8,128)(2,1)S(1)} %get-tuple-element.18.a, ...), custom_call_target="tpu_custom_call" | custom-call | tf_op jit(solution)/shard_map/pallas_call | solution.py:644

commit v9 on v8

--- a/solution.py
+++ b/solution.py
@@ -390,14 +390,6 @@
                 def _():
                     st_out[n, i // 2 - 2, HC * r:HC * (r + 1)] = table[:HC]
 
-        @pl.when((i == 6) & (chip != last))
-        def _():
-            stat_copy(n, False).start()
-
-        @pl.when((i == 4) & (chip == 0))
-        def _():
-            stat_copy(n, True).start()
-
     def local_pair(x):
         owner = jnp.where(outer, x % HC + jnp.where(chip == 0, 1, 0), jnp.where(chip == 1, last, 0))
         n = jnp.where(outer, x // HC, x)
@@ -467,9 +459,9 @@
                 for a, res in enumerate(col_tiles(q, do, key, val, table, stats, u, w)):
                     for r in range(2):
                         lres[sl, r, a] = res[r]
-            local_send(x, c).start()
             for a in range(2):
                 out[2 * (c // 2) + a, bat, head] = lres[sl, core, a]
+            local_send(x, c).start()
             return 0
 
         lax.fori_loop(lo, hi, one, 0)
@@ -484,6 +476,11 @@
 
     def send_tile(n, i):
         mask = jnp.bitwise_xor(me, i)
+        for tile, whole, chips in ((6, False, chip != last), (4, True, chip == 0)):
+            @pl.when((i == tile) & chips)
+            def _():
+                stat_copy(n, whole).start()
+
         for span, sent in sent_parts(i, chip):
             @pl.when((mask != 0) & sent)
             def _():

time: 306 us -> 306 us (level)
  no operation moved by 1% of the time
where the time goes in v9:
time: 306 us; the launch traced here: 304 us
  Pallas kernels  304 us (99%)
    pallas_call x1, Pallas kernels, exchange_attend(): pl.pallas_call(kernel, out_shape=(acts, pltpu.VMEM((NH, NT, T, D), F32),...  295 us
    pallas_call x1, Pallas kernels, write_out(): pl.pallas_call(write_kernel, out_shape=tuple(map(jax.ShapeDtypeStruct, sh...  8.81 us

profile of v9, /device:TPU:0, one launch (start us, length us, event | category | flops | bytes accessed | tf_op | source)
XLA Modules:
  0.0 304.3 jit_solution(6668700831600033122)
XLA Ops:
  0.6 294.7 %shard_map.126 = (bf16[4,4,12,256,128]{4,3,2,1,0:T(8,128)(2,1)S(1)}, f32[12,8,256,128]{3,2,1,0:T(8,128)S(1)}, f32[12,128]{1,0:T(8,128)S(1)}, f32[12,128]{1,0:T(8,128)S(1)}, bf16[4,2,12,256,128]{4,3,2,1,0:T(8,128)(2,1)}) custom-call(bf16[4,12,256,128]{3,2,1,0:T(8,128)(2,1)} %bitcast.15, bf16[4,12,256,128]{3,2,1,0:T(8,128)(2,1)} %bitcast.16, ...), custom_call_target="tpu_custom_call" | custom-call | tf_op jit(solution)/shard_map/pallas_call | solution.py:609
  295.4 8.8 %shard_map.127 = (bf16[4,12,256,128]{3,2,1,0:T(8,128)(2,1)}, bf16[4,12,256,128]{3,2,1,0:T(8,128)(2,1)}, bf16[4,12,256,128]{3,2,1,0:T(8,128)(2,1)}, bf16[4,12,256...) custom-call(bf16[4,4,12,256,128]{4,3,2,1,0:T(8,128)(2,1)S(1)} %get-tuple-element.18.a, ...), custom_call_target="tpu_custom_call" | custom-call | tf_op jit(solution)/shard_map/pallas_call | solution.py:641

commit v10 on v9

--- a/solution.py
+++ b/solution.py
@@ -12,6 +12,8 @@
 NU = 6
 NA = 4
 HC = 3
+HALF = 1024
+CUT = 480
 NH = 12
 EARLY = 6
 GROUPS = ((0, 1), (1, 1), (2, 2), (4, 2))
@@ -335,36 +337,46 @@
     def half_copy(k):
         return remote(drk.at[k, pl.ds(NA * (1 - core), NA)], pbuf.at[k], half_send.at[k], half_recv.at[k], partner)
 
-    def part(src_chip, k, lo, size):
-        return drk_out.at[HC * src_chip + k, pl.ds(NA * core + lo, size)]
+    def part(src_chip, k, lo=0, rows=HALF):
+        return drk_out.at[HC * src_chip + k, pl.ds(HALF * core + lo, rows)]
 
     def fin_copy(k, s, arrived=False):
-        piece = part(jnp.bitwise_xor(chip, s) if arrived else chip, k, 0, NA)
+        piece = part(jnp.bitwise_xor(chip, s) if arrived else chip, k)
         rsem = fin_recv.at[k, s - 1] if s else table_recv
         return remote(piece, piece, table_send, rsem, jnp.bitwise_xor(me, neighbours[s]))
 
-    def hop(k, s, whole):
-        piece = part(jnp.bitwise_xor(chip, s), k, *((0, NA) if whole else (2 * (s - 1), 2)))
-        return remote(piece, piece, table_send, hop_recv.at[k], jnp.bitwise_xor(me, neighbours[-s]))
-
-    def hops(k, s):
-        @pl.when(outer)
-        def _():
-            hop(k, s, False).start()
-
-        if s == 1:
-            @pl.when(~outer)
-            def _():
-                hop(k, s, True).start()
-
-    def relay(k, s):
-        piece = part(jnp.bitwise_xor(chip, s), k, 0, NA)
+    even = ((0, HALF // 2), (HALF // 2, HALF // 2))
+    uneven = ((0, CUT), (CUT, HALF - CUT))
+    going = ((uneven[0], even[1]), ((0, HALF),), ((0, HALF),), (even[0], uneven[1]))
+    coming = (((0, HALF),), even, uneven, ((0, HALF),))
+
+    def each_span(spans, act):
+        for c, here in enumerate(spans):
+            @pl.when(chip == c)
+            def _():
+                act(here)
+
+    def hop(k, s, span):
+        piece = part(jnp.bitwise_xor(chip, s), k, *span)
+        return remote(piece, piece, table_send, hop_recv.at[k, s - 1], jnp.bitwise_xor(me, neighbours[-s]))
+
+    def relay(k, s, *span):
+        piece = part(jnp.bitwise_xor(chip, s), k, *span)
         return remote(piece, piece, table_send, table_recv, partner)
+
+    def far_relay(k):
+        def act(spans):
+            for r, span in enumerate(spans):
+                piece = part(jnp.bitwise_xor(chip, last), k, *span)
+                remote(piece, piece, table_send, hop_recv.at[k, r], partner).wait_recv()
+                relay(k, last, *span).start()
+
+        each_span(coming, act)
 
     def pass_on(k):
         for s in (1, 2):
             fin_copy(k, s, True).wait_recv()
-            hops(k, s)
+            each_span(going, lambda spans: [hop(k, s, span).start() for span in spans[s - 1:s]])
             relay(k, s).start()
 
     def sent_parts(dev, owner):
@@ -524,7 +536,7 @@
             copy.start()
             copy.wait()
             for r in range(NA):
-                part(chip, k, r, 1)[0] = (drk[k, NA * core + r] + pbuf[k, r]).T
+                part(chip, k, r * T, T)[:] = (drk[k, NA * core + r] + pbuf[k, r]).T
             for s in range(3):
                 fin_copy(k, s).start()
 
@@ -547,9 +559,7 @@
     at_chip(late_work)
     pass_on(2)
     for k in range(HC):
-        far = part(jnp.bitwise_xor(chip, last), k, 0, NA)
-        remote(far, far, table_send, hop_recv.at[k], partner).wait_recv()
-        relay(k, last).start()
+        far_relay(k)
 
     others = duw_all.at[pl.ds(0, NT - 1)]
     remote(others, others, duw_send, duw_recv, partner).wait()
@@ -590,8 +600,14 @@
         remote(whole, whole, lr_send.at[0], lr_recv, partner).wait_recv()
 
     at_chip(end_local)
-    sent, got = drk_out.at[:, pl.ds(0, NT - 1)], drk_out.at[:, pl.ds(0, NA)]
-    remote(sent, sent, table_send, table_recv, partner).wait_send()
+    more = (HALF // 2 - CUT) // NA
+    for c, rows in enumerate((-more, 0, 0, more)):
+        @pl.when(chip == c)
+        def _():
+            sent = drk_out.at[:, pl.ds(0, (NT - 1) * T + rows)]
+            remote(sent, sent, table_send, table_recv, partner).wait_send()
+
+    got = drk_out.at[:, pl.ds(0, HALF)]
     remote(got, got, table_send, table_recv, partner).wait_recv()
 
 
@@ -608,7 +624,7 @@
     one = dma(())
     return pl.pallas_call(
         kernel,
-        out_shape=(acts, pltpu.VMEM((NH, NT, T, D), F32), bias, bias,
+        out_shape=(acts, pltpu.VMEM((NH, NT * T, D), F32), bias, bias,
                    jax.ShapeDtypeStruct((NA, 2, NH, T, D), BF)),
         in_specs=[any_spec] * 7,
         out_specs=(vmem_spec,) * 4 + (any_spec,),
@@ -618,7 +634,7 @@
             heads, heads, pltpu.VMEM((2, NH, D), BF), bias, bias,
             pltpu.VMEM((2, 2, NA, T, D), BF), pltpu.VMEM((2, NA, T, D), BF), pltpu.VMEM((2, 2, 2, T, D), BF),
             pltpu.VMEM((NU, 2, 8, T), F32), pltpu.VMEM((HC, NU, 2, 8, T), F32),
-            per_pair, per_pair, per_pair, per_head, per_head, dma((HC, 2)), per_head, two, two]
+            per_pair, per_pair, per_pair, per_head, per_head, dma((HC, 2)), dma((HC, 2)), two, two]
         + [one] * 9 + [per_head] + [one] * 5
         + UNIT_SCRATCH,
         compiler_params=pltpu.CompilerParams(collective_id=0, has_side_effects=True, vmem_limit_bytes=VMEM_LIMIT),

time: 306 us -> 305 us (level)
  no operation moved by 1% of the time
where the time goes in v10:
time: 305 us; the launch traced here: 304 us
  Pallas kernels  303 us (99%)
    pallas_call x1, Pallas kernels, exchange_attend(): pl.pallas_call(kernel, out_shape=(acts, pltpu.VMEM((NH, NT * T, D), F32),...  294 us
    pallas_call x1, Pallas kernels, write_out(): pl.pallas_call(write_kernel, out_shape=tuple(map(jax.ShapeDtypeStruct, sh...  8.81 us

profile of v10, /device:TPU:0, one launch (start us, length us, event | category | flops | bytes accessed | tf_op | source)
XLA Modules:
  0.0 303.7 jit_solution(6545357475989332652)
XLA Ops:
  0.6 294.1 %shard_map.126 = (bf16[4,4,12,256,128]{4,3,2,1,0:T(8,128)(2,1)S(1)}, f32[12,2048,128]{2,1,0:T(8,128)S(1)}, f32[12,128]{1,0:T(8,128)S(1)}, f32[12,128]{1,0:T(8,128)S(1)}, bf16[4,2,12,256,128]{4,3,2,1,0:T(8,128)(2,1)}) custom-call(bf16[4,12,256,128]{3,2,1,0:T(8,128)(2,1)} %bitcast.13, bf16[4,12,256,128]{3,2,1,0:T(8,128)(2,1)} %bitcast.14, ...), custom_call_target="tpu_custom_call" | custom-call | tf_op jit(solution)/shard_map/pallas_call | solution.py:625
  294.8 8.8 %shard_map.127 = (bf16[4,12,256,128]{3,2,1,0:T(8,128)(2,1)}, bf16[4,12,256,128]{3,2,1,0:T(8,128)(2,1)}, bf16[4,12,256,128]{3,2,1,0:T(8,128)(2,1)}, bf16[4,12,256...) custom-call(bf16[4,4,12,256,128]{4,3,2,1,0:T(8,128)(2,1)S(1)} %get-tuple-element.18.acts, ...), custom_call_target="tpu_custom_call" | custom-call | tf_op jit(solution)/shard_map/pallas_call | solution.py:657

commit v11 on v10

--- a/solution.py
+++ b/solution.py
@@ -645,8 +645,8 @@
     sem = refs[-1]
     srcs = [acts.at[a] for a in range(NA)] + [table, bias_u, bias_w]
     copies = [pltpu.make_async_copy(src, dst, sem.at[n]) for n, (src, dst) in enumerate(zip(srcs, refs[:-1]))]
-    for copy in copies:
-        copy.start()
+    for r, copy in enumerate(copies):
+        copy.start(priority=r % 2)
     for copy in copies:
         copy.wait()
 

time: 305 us -> 304 us (level)
  no operation moved by 1% of the time
where the time goes in v11:
time: 304 us; the launch traced here: 303 us
  Pallas kernels  303 us (100%)
    pallas_call x1, Pallas kernels, exchange_attend(): pl.pallas_call(kernel, out_shape=(acts, pltpu.VMEM((NH, NT * T, D), F32),...  294 us
    pallas_call x1, Pallas kernels, write_out(): pl.pallas_call(write_kernel, out_shape=tuple(map(jax.ShapeDtypeStruct, sh...  8.54 us

profile of v11, /device:TPU:0, one launch (start us, length us, event | category | flops | bytes accessed | tf_op | source)
XLA Modules:
  0.0 303.5 jit_solution(7846511113464198609)
XLA Ops:
  0.6 294.1 %shard_map.126 = (bf16[4,4,12,256,128]{4,3,2,1,0:T(8,128)(2,1)S(1)}, f32[12,2048,128]{2,1,0:T(8,128)S(1)}, f32[12,128]{1,0:T(8,128)S(1)}, f32[12,128]{1,0:T(8,128)S(1)}, bf16[4,2,12,256,128]{4,3,2,1,0:T(8,128)(2,1)}) custom-call(bf16[4,12,256,128]{3,2,1,0:T(8,128)(2,1)} %bitcast.13, bf16[4,12,256,128]{3,2,1,0:T(8,128)(2,1)} %bitcast.14, ...), custom_call_target="tpu_custom_call" | custom-call | tf_op jit(solution)/shard_map/pallas_call | solution.py:625
  294.8 8.5 %shard_map.127 = (bf16[4,12,256,128]{3,2,1,0:T(8,128)(2,1)}, bf16[4,12,256,128]{3,2,1,0:T(8,128)(2,1)}, bf16[4,12,256,128]{3,2,1,0:T(8,128)(2,1)}, bf16[4,12,256...) custom-call(bf16[4,4,12,256,128]{4,3,2,1,0:T(8,128)(2,1)S(1)} %get-tuple-element.18.acts, ...), custom_call_target="tpu_custom_call" | custom-call | tf_op jit(solution)/shard_map/pallas_call | solution.py:657

commit v12 on v11

--- a/solution.py
+++ b/solution.py
@@ -13,7 +13,8 @@
 NA = 4
 HC = 3
 HALF = 1024
-CUT = 480
+CUT = 472
+CUT_BACK = 520
 NH = 12
 EARLY = 6
 GROUPS = ((0, 1), (1, 1), (2, 2), (4, 2))
@@ -229,7 +230,7 @@
            rin, rl, drk, pbuf, duw, duw_all, rk, rkr, bias, bu, bw, lblk, lrk, lres, st_out, st_in,
            in_recv, rl_recv, st_recv, half_send, half_recv, fin_recv, hop_recv, l_sem, lr_send,
            in_send, in_loc, fw_send, out_send, out_recv, table_send, table_recv, duw_send, duw_recv, rk_sem, px_send,
-           px_recv, st_send, st_send_all, lr_recv, *scratch):
+           px_recv, st_send, st_send_all, lr_recv, hop_send, *scratch):
     me = lax.axis_index('cp')
     chip = me // 2
     core = me % 2
@@ -345,7 +346,7 @@
         rsem = fin_recv.at[k, s - 1] if s else table_recv
         return remote(piece, piece, table_send, rsem, jnp.bitwise_xor(me, neighbours[s]))
 
-    even = ((0, HALF // 2), (HALF // 2, HALF // 2))
+    even = ((0, CUT_BACK), (CUT_BACK, HALF - CUT_BACK))
     uneven = ((0, CUT), (CUT, HALF - CUT))
     going = ((uneven[0], even[1]), ((0, HALF),), ((0, HALF),), (even[0], uneven[1]))
     coming = (((0, HALF),), even, uneven, ((0, HALF),))
@@ -358,7 +359,7 @@
 
     def hop(k, s, span):
         piece = part(jnp.bitwise_xor(chip, s), k, *span)
-        return remote(piece, piece, table_send, hop_recv.at[k, s - 1], jnp.bitwise_xor(me, neighbours[-s]))
+        return remote(piece, piece, hop_send, hop_recv.at[k, s - 1], jnp.bitwise_xor(me, neighbours[-s]))
 
     def relay(k, s, *span):
         piece = part(jnp.bitwise_xor(chip, s), k, *span)
@@ -600,13 +601,13 @@
         remote(whole, whole, lr_send.at[0], lr_recv, partner).wait_recv()
 
     at_chip(end_local)
-    more = (HALF // 2 - CUT) // NA
-    for c, rows in enumerate((-more, 0, 0, more)):
-        @pl.when(chip == c)
-        def _():
-            sent = drk_out.at[:, pl.ds(0, (NT - 1) * T + rows)]
-            remote(sent, sent, table_send, table_recv, partner).wait_send()
-
+    def hops_sent(spans):
+        sent = drk_out.at[pl.ds(0, HC), pl.ds(0, sum(rows for _, rows in spans))]
+        remote(sent, sent, hop_send, table_recv, partner).wait_send()
+
+    each_span(going, hops_sent)
+    sent = drk_out.at[:, pl.ds(0, 6 * T)]
+    remote(sent, sent, table_send, table_recv, partner).wait_send()
     got = drk_out.at[:, pl.ds(0, HALF)]
     remote(got, got, table_send, table_recv, partner).wait_recv()
 
@@ -635,7 +636,7 @@
             pltpu.VMEM((2, 2, NA, T, D), BF), pltpu.VMEM((2, NA, T, D), BF), pltpu.VMEM((2, 2, 2, T, D), BF),
             pltpu.VMEM((NU, 2, 8, T), F32), pltpu.VMEM((HC, NU, 2, 8, T), F32),
             per_pair, per_pair, per_pair, per_head, per_head, dma((HC, 2)), dma((HC, 2)), two, two]
-        + [one] * 9 + [per_head] + [one] * 5
+        + [one] * 9 + [per_head] + [one] * 6
         + UNIT_SCRATCH,
         compiler_params=pltpu.CompilerParams(collective_id=0, has_side_effects=True, vmem_limit_bytes=VMEM_LIMIT),
     )(xq, xd, xk, xv, bias_u, bias_w, rel)

time: 304 us -> 304 us (level)
  no operation moved by 1% of the time
where the time goes in v12:
time: 304 us; the launch traced here: 303 us
  Pallas kernels  302 us (99%)
    pallas_call x1, Pallas kernels, exchange_attend(): pl.pallas_call(kernel, out_shape=(acts, pltpu.VMEM((NH, NT * T, D), F32),...  294 us
    pallas_call x1, Pallas kernels, write_out(): pl.pallas_call(write_kernel, out_shape=tuple(map(jax.ShapeDtypeStruct, sh...  8.54 us

profile of v12, /device:TPU:0, one launch (start us, length us, event | category | flops | bytes accessed | tf_op | source)
XLA Modules:
  0.0 303.2 jit_solution(17572261692744561101)
XLA Ops:
  0.6 293.9 %shard_map.126 = (bf16[4,4,12,256,128]{4,3,2,1,0:T(8,128)(2,1)S(1)}, f32[12,2048,128]{2,1,0:T(8,128)S(1)}, f32[12,128]{1,0:T(8,128)S(1)}, f32[12,128]{1,0:T(8,128)S(1)}, bf16[4,2,12,256,128]{4,3,2,1,0:T(8,128)(2,1)}) custom-call(bf16[4,12,256,128]{3,2,1,0:T(8,128)(2,1)} %bitcast.13, bf16[4,12,256,128]{3,2,1,0:T(8,128)(2,1)} %bitcast.14, ...), custom_call_target="tpu_custom_call" | custom-call | tf_op jit(solution)/shard_map/pallas_call | solution.py:626
  294.5 8.5 %shard_map.127 = (bf16[4,12,256,128]{3,2,1,0:T(8,128)(2,1)}, bf16[4,12,256,128]{3,2,1,0:T(8,128)(2,1)}, bf16[4,12,256,128]{3,2,1,0:T(8,128)(2,1)}, bf16[4,12,256...) custom-call(bf16[4,4,12,256,128]{4,3,2,1,0:T(8,128)(2,1)S(1)} %get-tuple-element.18.acts, ...), custom_call_target="tpu_custom_call" | custom-call | tf_op jit(solution)/shard_map/pallas_call | solution.py:658
